TPU v7x, 32 devices: a whole 2x2x4 slice. The times are simulated.
32 devices in a mesh: dp: 4 (over y, x), fsdp: 8 (over z, core).
Axes of the slice: x: 2, y: 2, z: 4, core: 2. Of those that a mesh axis runs over, the one named last changes fastest.
Arguments:
- hidden_in: bfloat16 [32768, 1024], P(('dp', 'fsdp')), may hold values from -6 to 6
- w_query: float32 [1048576], P(('dp', 'fsdp')), may hold values from -0.1875 to 0.1875
- w_latent: float32 [524288], P(('dp', 'fsdp')), may hold values from -0.1875 to 0.1875
- w_key_up: float32 [262144], P(('dp', 'fsdp')), may hold values from -0.375 to 0.375
- w_value_up: float32 [262144], P(('dp', 'fsdp')), may hold values from -0.375 to 0.375
- w_decay: float32 [1048576], P(('dp', 'fsdp')), may hold values from -0.1875 to 0.1875
- w_outgate: float32 [1048576], P(('dp', 'fsdp')), may hold values from -0.1875 to 0.1875
- w_out: float32 [1048576], P(('dp', 'fsdp')), may hold values from -0.1875 to 0.1875
- w_gate: float32 [2883584], P(('dp', 'fsdp')), may hold values from -0.1875 to 0.1875
- w_up: float32 [2883584], P(('dp', 'fsdp')), may hold values from -0.1875 to 0.1875
- w_down: float32 [2883584], P(('dp', 'fsdp')), may hold values from -0.109375 to 0.109375
- vectors: float32 [4096], P(('dp', 'fsdp')), may hold values from -3 to 5, as said below
- seg_ids: int32 [32768], P(('dp', 'fsdp')), may hold values from 0 to 127, never falling along the last dimension, each value on 1 to 1024 neighbouring positions
- pad_mask: int32 [32768], P(('dp', 'fsdp')), may hold values 0 or 1
- cotangent: bfloat16 [32768, 1024], P(('dp', 'fsdp')), may hold values from -6 to 6
Outputs:
- block_out: bfloat16 [32768, 1024], P(('dp', 'fsdp'))
- grad_input: float32 [32768, 1024], P(('dp', 'fsdp'))
- grad_query: float32 [1048576], P(('dp', 'fsdp'))
- grad_latent: float32 [524288], P(('dp', 'fsdp'))
- grad_key_up: float32 [262144], P(('dp', 'fsdp'))
- grad_value_up: float32 [262144], P(('dp', 'fsdp'))
- grad_decay: float32 [1048576], P(('dp', 'fsdp'))
- grad_outgate: float32 [1048576], P(('dp', 'fsdp'))
- grad_out: float32 [1048576], P(('dp', 'fsdp'))
- grad_gate: float32 [2883584], P(('dp', 'fsdp'))
- grad_up: float32 [2883584], P(('dp', 'fsdp'))
- grad_down: float32 [2883584], P(('dp', 'fsdp'))
- grad_vectors: float32 [4096], P(('dp', 'fsdp'))
Inputs may be any that keep to these rules, and one draw needn't show every extreme that they name: `vectors`: the first 2048 entries and the last 1024 entries are norm gains between 0.5 and 1.5.
All inputs are finite; a program needn't handle non-finite values. No bound on the sum of `pad_mask` on one device may be relied on, other than what follows from the above.
Results may differ from a plain program's by a relative error of at most 0.0095.
The roundings to bfloat16 on the way count: a program that leaves them out, or rounds other values in their place, can miss the bound.
Values may be sent and summed in bfloat16 or wider, within the bound.
A program may use at most 384 MiB of HBM per device.

v0:
```python
from functools import partial

import jax
import jax.numpy as jnp
from jax import lax
from jax.sharding import PartitionSpec as P

D = 1024
HEADS = 16
HEAD_DIM = 64
GROUPS = 2
LATENT = 256
FF = 2816
SPAN = 64
LEN = 1024


highest = lax.Precision.HIGHEST


def flat_dot(left, right):
    return jnp.dot(left, right, preferred_element_type=jnp.float32)


def left_grad(grad, weight):
    return lax.dot_general(
        grad, weight, (((1,), (1,)), ((), ())), preferred_element_type=jnp.float32
    )


def weight_grad(inputs, grad):
    return lax.dot_general(
        inputs, grad, (((0,), (0,)), ((), ())), preferred_element_type=jnp.float32
    )


def rms_scale(values, gain_vec):
    return values * lax.rsqrt(jnp.mean(values * values, axis=-1, keepdims=True) + 1e-05) * gain_vec


def up_project(latent, weight):
    grouped = latent.reshape(latent.shape[0], GROUPS, LATENT)
    result = jnp.einsum("tgl,glm->tgm", grouped, weight, preferred_element_type=jnp.float32)
    return result.reshape(latent.shape[0], -1)


def gather_all(pieces):
    return (
        lax.all_gather(pieces[0], ("dp", "fsdp"), axis=0, tiled=True),
        lax.all_gather(pieces[1], ("dp", "fsdp"), axis=0, tiled=True),
        lax.all_gather(pieces[2], ("dp", "fsdp"), axis=0, tiled=True),
        lax.all_gather(pieces[3], ("dp", "fsdp"), axis=0, tiled=True),
        lax.all_gather(pieces[4], ("dp", "fsdp"), axis=0, tiled=True),
        lax.all_gather(pieces[5], ("dp", "fsdp"), axis=0, tiled=True),
        lax.all_gather(pieces[6], ("dp", "fsdp"), axis=0, tiled=True),
        lax.all_gather(pieces[7], ("dp", "fsdp"), axis=0, tiled=True),
        lax.all_gather(pieces[8], ("dp", "fsdp"), axis=0, tiled=True),
        lax.all_gather(pieces[9], ("dp", "fsdp"), axis=0, tiled=True),
        lax.all_gather(pieces[10], ("dp", "fsdp"), axis=0, tiled=True),
    )


def unpack(flats):
    width = HEADS * HEAD_DIM
    per_group = HEADS // GROUPS * HEAD_DIM
    return (
        flats[0].reshape(D, width),
        flats[1].reshape(D, GROUPS * LATENT),
        flats[2].reshape(GROUPS, LATENT, per_group),
        flats[3].reshape(GROUPS, LATENT, per_group),
        flats[4].reshape(D, width),
        flats[5].reshape(D, width),
        flats[6].reshape(width, D),
        flats[7].reshape(D, FF),
        flats[8].reshape(D, FF),
        flats[9].reshape(FF, D),
        flats[10].astype(jnp.float32),
    )


def mixer(query, keys, values, decay_in, gate_in, out_gain, keep_flag, pad_flag):
    tok_count = query.shape[0]
    row_count = tok_count // LEN
    span_count = LEN // SPAN
    blocks = (row_count, span_count, SPAN, HEADS, HEAD_DIM)
    log_decay = (jax.nn.log_sigmoid(decay_in) / 16.0 * pad_flag[:, None]).reshape(blocks)
    scaled = (query * HEAD_DIM ** (-0.5)).reshape(blocks)
    masked = (keys * pad_flag[:, None]).reshape(blocks)
    value_blocks = values.reshape(blocks)
    resets = jnp.cumsum((1.0 - keep_flag).reshape(row_count, span_count, SPAN), axis=2)
    cumulative = jnp.cumsum(log_decay, axis=2)
    ending = cumulative[:, :, -1:]
    query_up = scaled * jnp.exp(cumulative)
    key_down = masked * jnp.exp(-cumulative)
    scores = jnp.einsum("rnihd,rnjhd->rnhij", query_up, key_down, precision=highest)
    position = jnp.arange(SPAN)
    causal = position[:, None] >= position[None, :]
    allowed = (resets[:, :, :, None] == resets[:, :, None, :]) & causal
    scores = jnp.where(allowed[:, :, None], scores, 0.0)
    within = jnp.einsum("rnhij,rnjhe->rnihe", scores, value_blocks, precision=highest)
    to_end = (resets == resets[:, :, -1:]).astype(jnp.float32)
    key_tail = masked * jnp.exp(ending - cumulative) * to_end[..., None, None]
    added_state = jnp.einsum("rnjhd,rnjhe->rnhde", key_tail, value_blocks, precision=highest)
    carried = (
        jnp.exp(ending[:, :, 0]) * (resets[:, :, -1] == 0).astype(jnp.float32)[..., None, None]
    )

    def advance(carry_state, inputs):
        factor, extra = inputs
        return (carry_state * factor[..., None] + extra, carry_state)

    zero_state = jnp.zeros((row_count, HEADS, HEAD_DIM, HEAD_DIM), jnp.float32)
    _, before = lax.scan(
        advance, zero_state, (jnp.moveaxis(carried, 1, 0), jnp.moveaxis(added_state, 1, 0))
    )
    before = jnp.moveaxis(before, 0, 1)
    fresh_mask = (resets == 0).astype(jnp.float32)[..., None, None]
    across = jnp.einsum("rnihd,rnhde->rnihe", query_up * fresh_mask, before, precision=highest)
    heads_out = (within + across).reshape(tok_count, HEADS, HEAD_DIM)
    normed = heads_out * lax.rsqrt(jnp.mean(heads_out * heads_out, axis=-1, keepdims=True) + 0.01)
    return normed.reshape(tok_count, HEADS * HEAD_DIM) * out_gain * jax.nn.silu(gate_in)


def split_vector(vector_all):
    width = HEADS * HEAD_DIM
    return (
        vector_all[:D],
        vector_all[D : 2 * D],
        vector_all[2 * D : 2 * D + width],
        vector_all[2 * D + width :],
    )


def forward_pass(weights, hidden_in, keep_flag, pad_flag):
    (
        w_query,
        w_latent,
        w_keyup,
        w_valup,
        w_decay,
        w_outgate,
        w_output,
        w_gate,
        w_upward,
        w_down,
        vector_all,
    ) = weights
    gain_in, gain_mid, decay_bias, out_gain = split_vector(vector_all)
    inputs = hidden_in.astype(jnp.float32)
    normed = rms_scale(inputs, gain_in).astype(jnp.bfloat16)
    query = flat_dot(normed, w_query)
    latent = flat_dot(normed, w_latent).astype(jnp.bfloat16)
    keys = up_project(latent, w_keyup)
    values = up_project(latent, w_valup)
    decay_in = flat_dot(normed, w_decay) + decay_bias
    gate_in = flat_dot(normed, w_outgate)
    mixed = mixer(query, keys, values, decay_in, gate_in, out_gain, keep_flag, pad_flag).astype(
        jnp.bfloat16
    )
    middle = inputs + flat_dot(mixed, w_output)
    normed_mid = rms_scale(middle, gain_mid).astype(jnp.bfloat16)
    gate_val = flat_dot(normed_mid, w_gate)
    upward = flat_dot(normed_mid, w_upward)
    hidden = (jax.nn.silu(gate_val) * upward).astype(jnp.bfloat16)
    output = middle + flat_dot(hidden, w_down)
    saved = (
        inputs,
        normed,
        query,
        latent,
        keys,
        values,
        decay_in,
        gate_in,
        mixed,
        middle,
        normed_mid,
        gate_val,
        upward,
        hidden,
    )
    return (output, saved)


def swiglu(gate_val, upward):
    return jax.nn.silu(gate_val) * upward


def backward(weights, saved, cotangent, keep_flag, pad_flag):
    (
        w_query,
        w_latent,
        w_keyup,
        w_valup,
        w_decay,
        w_outgate,
        w_output,
        w_gate,
        w_upward,
        w_down,
        vector_all,
    ) = weights
    (
        inputs,
        normed,
        query,
        latent,
        keys,
        values,
        decay_in,
        gate_in,
        mixed,
        middle,
        normed_mid,
        gate_val,
        upward,
        hidden,
    ) = saved
    gain_in, gain_mid, decay_bias, out_gain = split_vector(vector_all)
    tok_count = inputs.shape[0]
    d_outf = cotangent.astype(jnp.float32) * pad_flag[:, None]
    d_ffn = d_outf.astype(jnp.bfloat16)
    grad_down = weight_grad(hidden, d_ffn)
    owned_down = lax.psum_scatter(
        grad_down.reshape(-1), ("dp", "fsdp"), scatter_dimension=0, tiled=True
    )
    d_hidden = left_grad(d_ffn, w_down)
    _, swiglu_back = jax.vjp(swiglu, gate_val, upward)
    d_gate, d_upward = swiglu_back(d_hidden)
    d_gate = d_gate.astype(jnp.bfloat16)
    d_upward = d_upward.astype(jnp.bfloat16)
    grad_gate = weight_grad(normed_mid, d_gate)
    owned_gate = lax.psum_scatter(
        grad_gate.reshape(-1), ("dp", "fsdp"), scatter_dimension=0, tiled=True
    )
    grad_upward = weight_grad(normed_mid, d_upward)
    owned_up = lax.psum_scatter(
        grad_upward.reshape(-1), ("dp", "fsdp"), scatter_dimension=0, tiled=True
    )
    d_normed_mid = left_grad(d_gate, w_gate) + left_grad(d_upward, w_upward)
    _, middle_back = jax.vjp(rms_scale, middle, gain_mid)
    d_middle, d_gain_mid = middle_back(d_normed_mid)
    d_middle = d_middle + d_outf
    d_branch = d_middle.astype(jnp.bfloat16)
    grad_output = weight_grad(mixed, d_branch)
    owned_out = lax.psum_scatter(
        grad_output.reshape(-1), ("dp", "fsdp"), scatter_dimension=0, tiled=True
    )
    d_mixed = left_grad(d_branch, w_output)
    local_mixer = partial(mixer, keep_flag=keep_flag, pad_flag=pad_flag)
    _, mixer_back = jax.vjp(local_mixer, query, keys, values, decay_in, gate_in, out_gain)
    d_query, d_keys, d_values, d_decay, d_gatein, d_out_gain = mixer_back(d_mixed)
    d_bias = jnp.sum(d_decay, axis=0)
    d_query = d_query.astype(jnp.bfloat16)
    d_keys = d_keys.astype(jnp.bfloat16).reshape(tok_count, GROUPS, -1)
    d_values = d_values.astype(jnp.bfloat16).reshape(tok_count, GROUPS, -1)
    d_decay = d_decay.astype(jnp.bfloat16)
    d_gatein = d_gatein.astype(jnp.bfloat16)
    grad_query = weight_grad(normed, d_query)
    grad_decay = weight_grad(normed, d_decay)
    grad_outgate = weight_grad(normed, d_gatein)
    grouped = latent.reshape(tok_count, GROUPS, LATENT)
    grad_keyup = jnp.einsum("tgl,tgm->glm", grouped, d_keys, preferred_element_type=jnp.float32)
    grad_valup = jnp.einsum("tgl,tgm->glm", grouped, d_values, preferred_element_type=jnp.float32)
    d_latent = jnp.einsum("tgm,glm->tgl", d_keys, w_keyup, preferred_element_type=jnp.float32)
    d_latent = d_latent + jnp.einsum(
        "tgm,glm->tgl", d_values, w_valup, preferred_element_type=jnp.float32
    )
    d_latent = d_latent.reshape(tok_count, GROUPS * LATENT).astype(jnp.bfloat16)
    grad_latent = weight_grad(normed, d_latent)
    d_normed = left_grad(d_query, w_query) + left_grad(d_latent, w_latent)
    d_normed = d_normed + left_grad(d_decay, w_decay) + left_grad(d_gatein, w_outgate)
    _, first_back = jax.vjp(rms_scale, inputs, gain_in)
    d_inputs, d_gain_in = first_back(d_normed)
    grad_input = d_middle + d_inputs
    grad_vector = jnp.concatenate([d_gain_in, d_gain_mid, d_bias, d_out_gain])
    rest = (
        lax.psum_scatter(grad_query.reshape(-1), ("dp", "fsdp"), scatter_dimension=0, tiled=True),
        lax.psum_scatter(grad_latent.reshape(-1), ("dp", "fsdp"), scatter_dimension=0, tiled=True),
        lax.psum_scatter(grad_keyup.reshape(-1), ("dp", "fsdp"), scatter_dimension=0, tiled=True),
        lax.psum_scatter(grad_valup.reshape(-1), ("dp", "fsdp"), scatter_dimension=0, tiled=True),
        lax.psum_scatter(grad_decay.reshape(-1), ("dp", "fsdp"), scatter_dimension=0, tiled=True),
        lax.psum_scatter(grad_outgate.reshape(-1), ("dp", "fsdp"), scatter_dimension=0, tiled=True),
        lax.psum_scatter(grad_vector, ("dp", "fsdp"), scatter_dimension=0, tiled=True),
    )
    owned = (
        rest[0],
        rest[1],
        rest[2],
        rest[3],
        rest[4],
        rest[5],
        owned_out,
        owned_gate,
        owned_up,
        owned_down,
        rest[6],
    )
    return (grad_input, owned)


def per_device(
    hidden_in,
    w_query,
    w_latent,
    w_key_up,
    w_value_up,
    w_decay,
    w_outgate,
    w_out,
    w_gate,
    w_up,
    w_down,
    vectors,
    seg_ids,
    pad_mask,
    cotangent,
):
    shards = (
        w_query,
        w_latent,
        w_key_up,
        w_value_up,
        w_decay,
        w_outgate,
        w_out,
        w_gate,
        w_up,
        w_down,
        vectors,
    )
    low_shards = tuple((piece.astype(jnp.bfloat16) for piece in shards))
    seg_rows = seg_ids.reshape(-1, LEN)
    same_doc = (seg_rows[:, 1:] == seg_rows[:, :-1]).astype(jnp.float32)
    keep_flag = jnp.concatenate(
        [jnp.zeros((seg_rows.shape[0], 1), jnp.float32), same_doc], axis=1
    ).reshape(-1)
    pad_flag = pad_mask.astype(jnp.float32)
    weights = unpack(gather_all(low_shards))
    output, saved = forward_pass(weights, hidden_in, keep_flag, pad_flag)
    weights_back = unpack(gather_all(low_shards))
    _, saved = forward_pass(weights_back, hidden_in, keep_flag, pad_flag)
    grad_input, owned = backward(weights_back, saved, cotangent, keep_flag, pad_flag)
    return (
        output.astype(jnp.bfloat16),
        grad_input,
        owned[0],
        owned[1],
        owned[2],
        owned[3],
        owned[4],
        owned[5],
        owned[6],
        owned[7],
        owned[8],
        owned[9],
        owned[10],
    )


def solution(mesh):
    in_specs = (
        P(("dp", "fsdp"), None),
        P(("dp", "fsdp")),
        P(("dp", "fsdp")),
        P(("dp", "fsdp")),
        P(("dp", "fsdp")),
        P(("dp", "fsdp")),
        P(("dp", "fsdp")),
        P(("dp", "fsdp")),
        P(("dp", "fsdp")),
        P(("dp", "fsdp")),
        P(("dp", "fsdp")),
        P(("dp", "fsdp")),
        P(("dp", "fsdp")),
        P(("dp", "fsdp")),
        P(("dp", "fsdp"), None),
    )
    out_specs = (
        P(("dp", "fsdp"), None),
        P(("dp", "fsdp"), None),
        P(("dp", "fsdp")),
        P(("dp", "fsdp")),
        P(("dp", "fsdp")),
        P(("dp", "fsdp")),
        P(("dp", "fsdp")),
        P(("dp", "fsdp")),
        P(("dp", "fsdp")),
        P(("dp", "fsdp")),
        P(("dp", "fsdp")),
        P(("dp", "fsdp")),
        P(("dp", "fsdp")),
    )
    return jax.shard_map(
        per_device, mesh=mesh, in_specs=in_specs, out_specs=out_specs, check_vma=False
    )
```

profile of v0, /device:TPU:0, one launch (start us, length us, event | category | flops | bytes accessed | tf_op | source)
XLA Modules:
  0.0 1979.2 jit_solution(14795139988891333581)
XLA Ops:
  24.3 43.3 %all-gather = bf16[32,1,128]{2,1,0:T(2,128)(2,1)S(1)} all-gather(bf16[1,1,128]{2,1,0:T(2,128)(2,1)S(1)} %convert_bitcast_fusion), channel_id=1, replica_groups=mesh['dp'=4,'fsdp'=8] {'dp','fsdp'}, dimensions={0}, use_global_device_ids=true | all-gather | bytes 8448 | tf_op jit(solution)/shard_map/all_gather | solution.py:59
  68.7 42.2 %all_gather.49 = bf16[262144]{0:T(1024)(128)(2,1)} all-gather(bf16[8192]{0:T(1024)(128)(2,1)S(1)} %convert_element_type.167), channel_id=1, replica_groups=mesh['dp'=4,'fsdp'=8] {'dp','fsdp'}, dimensions={0}, use_global_device_ids=true | all-gather | bytes 540672 | tf_op jit(solution)/shard_map/all_gather | solution.py:51
  112.4 43.0 %all_gather.46 = bf16[262144]{0:T(1024)(128)(2,1)} all-gather(bf16[8192]{0:T(1024)(128)(2,1)S(1)} %convert_element_type.163), channel_id=1, replica_groups=mesh['dp'=4,'fsdp'=8] {'dp','fsdp'}, dimensions={0}, use_global_device_ids=true | all-gather | bytes 540672 | tf_op jit(solution)/shard_map/all_gather | solution.py:52
  177.3 8.6 reshape.639
  195.3 7.3 reshape.597
  202.7 8.7 copy.121
  211.4 7.3 reshape.617
  218.7 8.7 copy.156
  238.0 7.2 reshape.600
  245.2 7.2 reshape.618
  256.6 8.7 negate_multiply_fusion
  265.3 7.3 reshape.602
  272.6 7.4 fusion.133
  280.0 9.3 copy.119
  290.9 18.2 fusion.31
  309.1 20.1 %fusion.87 = f32[16,1,16,64,64]{4,3,2,1,0:T(8,128)} fusion(f32[16,64,16,64]{3,1,2,0:T(8,128)S(1)} %bitcast.295, f32[16,64,16,64]{3,2,1,0:T(8,128)} %get-tuple-element.410), kind=kOutput, calls=%fused_computation.146 | convolution fusion | flops 805306368 | bytes 12582912 | tf_op jit(solution)/shard_map/rnjhd,rnjhe->rnhde/dot_general | solution.py:103
  333.6 35.2 %while.52 = (s32[]{:T(128)}, f32[1,16,64,64]{3,2,1,0:T(8,128)S(1)}, f32[16,1,16,64,64]{4,3,2,1,0:T(8,128)}, f32[16,1,16,64]{3,2,1,0:T(8,128)S(1)}, f32[16,1,16,64,64]{4,3,2,1,0:T(8,128)}, /*index=5*/s32[]{:T(128)}, s32[]{:T(128)}) while((s32[]{:T(128)}, f32[1,16,64,64]{3,2,1,0:T(8,128)S(1)}, f32[16,1,16,64,64]{4,3,2,1,0:T(8,128)}, ...), condition=%wide.region_4.5_spmd.clone, body=%wide.region_3.4_spmd.clone.sunk | while | flops 262147 | bytes 1585760 | solution.py:113
  368.8 26.1 %fusion.39 = f32[16,16,64,64]{3,2,1,0:T(8,128)} fusion(f32[16,64,16,64]{3,2,1,0:T(8,128)} %get-tuple-element.411, f32[16,64,16,64]{3,2,1,0:T(8,128)} %get-tuple-element.416), kind=kOutput, calls=%fused_computation.85 | convolution fusion | flops 805306368 | bytes 12582912 | tf_op jit(solution)/shard_map/rnihd,rnjhd->rnhij/dot_general | solution.py:95
  395.0 19.8 fusion.48
  414.7 21.0 %multiply_reduce_fusion.2 = (f32[16,64,16]{1,2,0:T(8,128)S(1)}, f32[1,16,64,16,64]{2,4,3,1,0:T(8,128)}) fusion(f32[16,16,64,64]{3,2,1,0:T(8,128)} %fusion.48, f32[16,64,16,64]{3,2,1,0:T(8,128)S(1)} %bitcast.297, f32[16,1,16,64,64]{4,3,2,1,0:T(8,128)} %get-tuple-element.225), kind=kOutput, calls=%fused_computation.73 | convolution fusion | flops 808435712 | bytes 16842752 | tf_op jit(solution)/shard_map/rnihd,rnhde->rnihe/dot_general | solution.py:118
  435.8 9.8 copy.126
  445.5 7.6 reshape.606
  465.5 8.0 multiply_convert_fusion.4
  487.3 44.6 %while.53 = (s32[]{:T(128)}, f32[1,16,64,64]{3,2,1,0:T(8,128)S(1)}, f32[16,1,16,64,64]{4,3,2,1,0:T(8,128)}, f32[16,1,16,64,1]{3,2,4,1,0:T(8,128)}, f32[16,1,16,6...) while((s32[]{:T(128)}, f32[1,16,64,64]{3,2,1,0:T(8,128)S(1)}, ...), condition=%wide.region_9.10_spmd.clone, body=%wide.region_8.9_spmd.clone.sunk | while | flops 262147 | bytes 1598568 | solution.py:113
  531.9 11.5 reshape.609
  543.4 11.5 reshape.610
  555.0 11.5 fusion.134
  566.5 8.8 fusion.135
  575.3 9.7 reshape.611
  585.0 21.8 %multiply_convert_fusion = (bf16[1024,2816]{1,0:T(8,128)(2,1)}, bf16[1024,2816]{1,0:T(8,128)(2,1)}, bf16[1024,2816]{1,0:T(8,128)(2,1)}) fusion(f32[1024,2816]{1,0:T(8,128)} %fusion.134, f32[1024,2816]{1,0:T(8,128)} %fusion.135, bf16[2816,1024]{1,0:T(8,128)(2,1)} %reshape.611, bf16[1024,1024]{1,0:T(8,128)(2,1)} %param.35, f32[1024]{0:T(1024)S(1)} %copy-done.46), kind=kOutput, calls=%fused_computation.22 | convolution fusion | flops 5954863104 | bytes 48238592 | tf_op jit(solution)/shard_map/dot_general | solution.py:26
  606.8 10.0 fusion.136
  616.9 9.8 multiply_reduce_fusion.4
  630.6 6.0 broadcast_multiply_fusion.1
  636.6 7.7 reshape.612
  644.3 9.6 copy.134
  653.9 25.9 %multiply_reduce_fusion = (f32[16,64,16]{1,2,0:T(8,128)S(1)}, f32[16,64,16]{1,2,0:T(8,128)S(1)}, f32[1,16,64,16,64]{2,4,3,1,0:T(8,128)}) fusion(f32[1,16,64,16,64]{2,4,3,1,0:T(8,128)} %copy.134, f32[16,16,64,64]{3,2,1,0:T(8,128)} %fusion.48, f32[16,64,16,64]{3,2,1,0:T(8,128)} %get-tuple-element.415, f32[16,1,16,64,64]{4,3,2,1,0:T(8,128)} %get-tuple-element.608), kind=kOutput, calls=%fused_computation.70 | convolution fusion | flops 810516480 | bytes 21102592 | tf_op jit(solution)/shard_map/jvp(rnihd,rnhde->rnihe)/dot_general | solution.py:118
  679.9 12.3 fusion.5
  692.1 17.6 fusion.80
  709.8 17.8 fusion.137
  727.6 16.3 fusion.20
  744.0 9.8 copy.159
  753.8 12.0 fusion.141
  765.7 11.7 fusion.142
  786.1 70.2 %while.54 = (s32[]{:T(128)}, f32[1,16,64,64]{3,2,1,0:T(8,128)S(1)}, f32[16,1,16,64]{3,2,1,0:T(8,128)S(1)}, f32[16,1,16,64,64]{4,3,2,1,0:T(8,128)}, f32[16,1,16,6...) while((s32[]{:T(128)}, f32[1,16,64,64]{3,2,1,0:T(8,128)S(1)}, ...), condition=%wide.region_14.15_spmd.clone, body=%wide.region_12.14_spmd.clone.sunk | while | flops 392196 | bytes 2916496 | solution.py:113
  856.4 22.5 %fusion.13 = f32[16,16,64,64]{3,2,1,0:T(8,128)} fusion(f32[16,1,16,64,64]{4,3,2,1,0:T(8,128)} %get-tuple-element.228, f32[16,64,16,64]{3,2,1,0:T(8,128)} %get-tuple-element.410), kind=kOutput, calls=%fused_computation.39 | convolution fusion | flops 805306368 | bytes 12582912 | tf_op jit(solution)/shard_map/transpose(jvp(rnjhd,rnjhe->rnhde))/dot_general | solution.py:103
  878.9 24.7 %fusion.54 = (f32[16,16,64]{2,1,0:T(8,128)S(1)}, f32[16,16,64,64]{2,3,1,0:T(8,128)}) fusion(f32[1,16,64,16,64]{4,2,3,1,0:T(8,128)} %copy.156, f32[16,64]{1,0:T(8,128)S(1)} %copy-done.51, f32[16,16,64]{2,1,0:T(8,128)S(1)} %bitcast.319, f32[16,64]{1,0:T(8,128)S(1)} %copy-done.49, f32[1,16,64,16,64]{4,3,2,1,0:T(8,128)} %fusion.133, ...), kind=kOutput, calls=%fused_computation.103 | convolution fusion | flops 811581440 | bytes 21110784 | tf_op jit(solution)/shard_map/transpose(jvp(rnjhd,rnjhe->rnhde))/dot_general | solution.py:103
  903.6 19.8 bitcast_add_fusion.3
  924.9 36.4 %fusion.6 = (f32[1,16,64,16,64]{4,2,3,1,0:T(8,128)}, f32[1,16,64,16,64]{4,2,3,1,0:T(8,128)}, bf16[1,16,64,16,64]{4,2,3,1,0:T(8,128)(2,1)}) fusion(f32[16,16,64,64]{2,3,1,0:T(8,128)S(1)} %copy-done.6, f32[16,16,64]{2,1,0:T(8,128)S(1)} %bitcast.320, f32[16,64]{1,0:T(8,128)S(1)} %copy-done.49, f32[1,16,64,16,64]{4,3,2,1,0:T(8,128)} %fusion.133, ...), kind=kOutput, calls=%fused_computation.29 | convolution fusion | flops 828375040 | bytes 40050688 | tf_op jit(solution)/shard_map/transpose(jvp(rnihd,rnjhd->rnhij))/dot_general | solution.py:95
  961.4 9.8 copy.149
  971.1 7.7 reshape.616
  985.0 14.8 fusion.66
  1013.7 19.4 fusion.32
  1033.0 7.6 reshape.620
  1040.7 7.6 copy.141
  1048.3 6.5 convert_element_type.186
  1062.7 7.8 reshape.621
  1075.2 12.6 reshape.629
  1087.8 12.8 reshape.630
  1100.6 6.4 fusion.128
  1135.0 9.4 convolution_bitcast_fusion
  1144.4 11.3 copy.187
  1170.2 40.9 %all-reduce.11 = f32[4096]{0:T(1024)S(1)} all-reduce(f32[4096]{0:T(1024)S(1)} %pad_maximum_fusion), channel_id=12, replica_groups=mesh['dp'=4,'fsdp'=8] {'dp','fsdp'}, use_global_device_ids=true, to_apply=%region_32.33.clone | all-reduce | flops 4096 | bytes 32768
  1218.0 11.0 add_convert_fusion.1
  1229.0 727.7 %all-reduce.15.cloned.1.call-done = (f32[1048576]{0:T(1024)}, f32[524288]{0:T(1024)}, f32[262144]{0:T(1024)}, f32[262144]{0:T(1024)}, f32[1048576]{0:T(1024)}, /...) async-done(((f32[1048576]{0:T(1024)}, f32[524288]{0:T(1024)}, f32[262144]{0:T(1024)}, f32[262144]{0:T(1024)}, ...) | async-done | bytes 55574544
  (502 shorter events, 357.8 us)
Async XLA Ops:
  7.2 61.0 %copy-start.7 = (bf16[1024,1024]{1,0:T(8,128)(2,1)S(1)}, bf16[1024,1024]{1,0:T(8,128)(2,1)}, u32[]{:S(2)}) copy-start(bf16[1024,1024]{1,0:T(8,128)(2,1)} %param.21) | copy-start | bytes 6291460
  7.2 61.5 %copy-start.61 = (f32[8192]{0:T(1024)S(1)}, f32[8192]{0:T(1024)}, u32[]{:S(2)}) copy-start(f32[8192]{0:T(1024)} %param.24) | copy-start | bytes 98308
  7.2 105.2 %copy-start.62 = (f32[8192]{0:T(1024)S(1)}, f32[8192]{0:T(1024)}, u32[]{:S(2)}) copy-start(f32[8192]{0:T(1024)} %param.25) | copy-start | bytes 98308
  7.2 150.6 %all-gather.10.cloned.1.call-start = ((), (), s32[]{:S(2)}) async-start(), calls=%async_computation | async-start | bytes 1081344 | tf_op jit(solution)/shard_map/all_gather | solution.py:50
  8.9 218.5 %all-gather.12.cloned.1.call-start = ((), (), s32[]{:S(2)}) async-start(), calls=%async_computation.1 | async-start | bytes 2162688 | tf_op jit(solution)/shard_map/all_gather | solution.py:49
  10.5 242.0 %all-gather.14.cloned.1.call-start = ((), (), s32[]{:S(2)}) async-start(), calls=%async_computation.2 | async-start | bytes 2162688 | tf_op jit(solution)/shard_map/all_gather | solution.py:53
  12.1 449.2 %all-gather.16.cloned.1.call-start = ((), (), s32[]{:S(2)}) async-start(), calls=%async_computation.3 | async-start | bytes 2162688 | tf_op jit(solution)/shard_map/all_gather | solution.py:54
  13.7 459.7 %all-gather.18.cloned.1.call-start = ((), (), s32[]{:S(2)}) async-start(), calls=%async_computation.4 | async-start | bytes 2162688 | tf_op jit(solution)/shard_map/all_gather | solution.py:55
  15.3 516.5 %all-gather.20.cloned.1.call-start = ((), (), s32[]{:S(2)}) async-start(), calls=%async_computation.5 | async-start | bytes 5947392 | tf_op jit(solution)/shard_map/all_gather | solution.py:56
  17.1 526.3 %all-gather.22.cloned.1.call-start = ((), (), s32[]{:S(2)}) async-start(), calls=%async_computation.6 | async-start | bytes 5947392 | tf_op jit(solution)/shard_map/all_gather | solution.py:57
  18.8 556.5 %all-gather.24.cloned.1.call-start = ((), (), s32[]{:S(2)}) async-start(), calls=%async_computation.7 | async-start | bytes 5947392 | tf_op jit(solution)/shard_map/all_gather | solution.py:58
  20.6 1936.1 %all-reduce.15.cloned.1.call-start = ((), (), s32[]{:S(2)}) async-start(), calls=%async_computation.8 | async-start | bytes 111149056
  22.0 135.5 %copy-start.45 = (f32[1024]{0:T(1024)}, f32[1024]{0:T(1024)S(1)}, u32[]{:S(2)}) copy-start(f32[1024]{0:T(1024)S(1)} %convert_element_type.166) | copy-start | bytes 12292
  23.5 267.3 %copy-start.48 = (f32[16,64]{1,0:T(8,128)}, f32[16,64]{1,0:T(8,128)S(1)}, u32[]{:S(2)}) copy-start(f32[16,64]{1,0:T(8,128)S(1)} %get-tuple-element.425) | copy-start | bytes 12292
  23.5 267.3 %copy-start.52 = (f32[16,64]{1,0:T(8,128)}, f32[16,64]{1,0:T(8,128)S(1)}, u32[]{:S(2)}) copy-start(f32[16,64]{1,0:T(8,128)S(1)} %get-tuple-element.426) | copy-start | bytes 12292
  23.6 305.6 %copy-start.68 = (f32[16]{0:T(128)}, f32[16]{0:T(128)S(1)}, u32[]{:S(2)}) copy-start(f32[16]{0:T(128)S(1)} %compare_convert_fusion.2) | copy-start | bytes 196
  68.2 188.5 %copy-start.63 = (f32[8,1,128]{2,1,0:T(1,128)}, f32[8,1,128]{2,1,0:T(1,128)S(1)}, u32[]{:S(2)}) copy-start(f32[8,1,128]{2,1,0:T(1,128)S(1)} %get-tuple-element.423) | copy-start | bytes 12292
  68.2 397.3 %copy-start.59 = (f32[8,1,128]{2,1,0:T(1,128)}, f32[8,1,128]{2,1,0:T(1,128)S(1)}, u32[]{:S(2)}) copy-start(f32[8,1,128]{2,1,0:T(1,128)S(1)} %get-tuple-element.424) | copy-start | bytes 12292
  68.2 560.0 %copy-start.65 = (f32[8,1,128]{2,1,0:T(1,128)}, f32[8,1,128]{2,1,0:T(1,128)S(1)}, u32[]{:S(2)}) copy-start(f32[8,1,128]{2,1,0:T(1,128)S(1)} %get-tuple-element.422) | copy-start | bytes 12292
  68.6 42.3 %copy-start.55 = (f32[1024]{0:T(1024)}, f32[1024]{0:T(1024)S(1)}, u32[]{:S(2)}) copy-start(f32[1024]{0:T(1024)S(1)} %fusion.64) | copy-start | bytes 12292
  68.7 396.8 %copy-start.57 = (f32[1024]{0:T(1024)}, f32[1024]{0:T(1024)S(1)}, u32[]{:S(2)}) copy-start(f32[1024]{0:T(1024)S(1)} %fusion.112) | copy-start | bytes 12292
  112.3 50.7 %copy-start.20 = (bf16[2,256,512]{2,1,0:T(8,128)(2,1)}, bf16[2,256,512]{2,1,0:T(8,128)(2,1)S(1)}, u32[]{:S(2)}) copy-start(bf16[2,256,512]{2,1,0:T(8,128)(2,1)S(1)} %reshape.603) | copy-start | bytes 1572868
  112.4 178.4 %copy-start.50 = (f32[16,64]{1,0:T(8,128)}, f32[16,64]{1,0:T(8,128)S(1)}, u32[]{:S(2)}) copy-start(f32[16,64]{1,0:T(8,128)S(1)} %mul.633) | copy-start | bytes 12292
  157.8 237.2 %copy-start.33 = (pred[16,64,64]{2,1,0:T(8,128)(4,1)}, pred[16,64,64]{2,1,0:T(8,128)(4,1)S(1)}, u32[]{:S(2)}) copy-start(pred[16,64,64]{2,1,0:T(8,128)(4,1)S(1)} %compare_and_fusion) | copy-start | bytes 196612
  177.3 8.6 copy-start.22
  280.0 10.8 copy-start.1
  280.0 29.0 %slice-start = ((s8[8388608]{0:T(1024)(128)(4,1)}), s8[4194304]{0:T(1024)(128)(4,1)S(1)}, s32[]{:S(2)}) async-start(s8[8388608]{0:T(1024)(128)(4,1)} %bitcast.294), calls=%async_computation.9 | async-start | bytes 8388608
  290.8 18.2 copy-start.35
  290.9 18.2 slice-start.1
  368.8 45.9 %slice-start.2 = ((s8[8388608]{0:T(1024)(128)(4,1)}), s8[4194304]{0:T(1024)(128)(4,1)S(1)}, s32[]{:S(2)}) async-start(s8[8388608]{0:T(1024)(128)(4,1)} %bitcast.296), calls=%async_computation.11 | async-start | bytes 8388608
  395.0 19.8 slice-start.3
  482.5 4.8 copy-start.10
  555.0 11.5 copy-start.19
  575.3 9.7 copy-start.46
  606.8 10.0 copy-start.11
  606.8 10.0 copy-start.70
  616.8 9.8 copy-start.43
  628.1 8.4 copy-start.14
  692.1 17.6 copy-start
  692.1 35.5 %slice-start.4 = ((s8[8388608]{0:T(1024)(128)(4,1)}), s8[4194304]{0:T(1024)(128)(4,1)S(1)}, s32[]{:S(2)}) async-start(s8[8388608]{0:T(1024)(128)(4,1)} %bitcast.298), calls=%async_computation.13 | async-start | bytes 8388608
  709.8 17.9 slice-start.5
  765.7 11.7 copy-start.15
  765.7 11.7 copy-start.71
  856.4 22.5 %copy-start.36 = (f32[1,16,1,16,64]{4,2,3,1,0:T(1,128)S(1)}, f32[1,16,1,16,64]{4,2,3,1,0:T(1,128)}, u32[]{:S(2)}) copy-start(f32[1,16,1,16,64]{4,2,3,1,0:T(1,128)} %copy-done.35) | copy-start | bytes 196612
  856.4 22.5 %copy-start.49 = (f32[16,64]{1,0:T(8,128)S(1)}, f32[16,64]{1,0:T(8,128)}, u32[]{:S(2)}) copy-start(f32[16,64]{1,0:T(8,128)} %copy-done.48) | copy-start | bytes 12292
  856.4 22.5 %copy-start.51 = (f32[16,64]{1,0:T(8,128)S(1)}, f32[16,64]{1,0:T(8,128)}, u32[]{:S(2)}) copy-start(f32[16,64]{1,0:T(8,128)} %copy-done.50) | copy-start | bytes 12292
  878.9 24.7 %copy-start.34 = (pred[16,64,64]{2,1,0:T(8,128)(4,1)S(1)}, pred[16,64,64]{2,1,0:T(8,128)(4,1)}, u32[]{:S(2)}) copy-start(pred[16,64,64]{2,1,0:T(8,128)(4,1)} %copy-done.33) | copy-start | bytes 196612
  878.9 24.7 %copy-start.53 = (f32[16,64]{1,0:T(8,128)S(1)}, f32[16,64]{1,0:T(8,128)}, u32[]{:S(2)}) copy-start(f32[16,64]{1,0:T(8,128)} %copy-done.52) | copy-start | bytes 12292
  903.6 19.8 copy-start.69
  903.6 21.3 %copy-start.6 = (f32[16,16,64,64]{2,3,1,0:T(8,128)S(1)}, f32[16,16,64,64]{2,3,1,0:T(8,128)}, u32[]{:S(2)}) copy-start(f32[16,16,64,64]{2,3,1,0:T(8,128)} %get-tuple-element.440) | copy-start | bytes 12582916
  971.1 7.7 copy-start.21
  971.1 7.7 copy-start.47
  1062.7 7.8 copy-start.8
  1062.7 7.8 copy-start.58
  1062.7 7.8 copy-start.60
  1087.8 12.8 copy-start.64
  1118.9 5.7 copy-start.31
  1118.9 5.7 copy-start.32
  1118.9 5.7 copy-start.66
  1121.4 5.1 copy-start.13
  1126.6 8.4 slice-start.6
  1129.4 5.6 slice-start.7
  1165.9 45.7 %copy-start.56 = (f32[1024]{0:T(1024)S(1)}, f32[1024]{0:T(1024)}, u32[]{:S(2)}) copy-start(f32[1024]{0:T(1024)} %copy-done.55) | copy-start | bytes 12292
  1211.7 6.4 copy-start.12
  (25 other events, 79.3 us)
Sparse Core Ops, SparseCore 0:
  11.6 56.5 all-gather.9
  71.7 56.1 all-gather.11
  131.5 55.2 all-gather.13
  190.3 55.2 all-gather.15
  248.3 55.2 all-gather.17
  306.9 66.1 all-gather.19
  376.6 65.9 all-gather.21
  446.0 65.9 all-gather.23
  1155.9 800.7 all-reduce.14
where the time goes:
time: 1990 us; the launch traced here: 1980 us
  waiting for transfers between devices  728 us (37%)
  matrix products  466 us (23%)
  local copies, waits for them, and re-layouts  400 us (20%)
  other arithmetic  200 us (10%)
  blocking collectives  169 us (8%)
    unnamed x10, waiting for transfers between devices  728 us
    dot_general x3, matrix products, mixer(): jnp.einsum('rnihd,rnjhd->rnhij', query_up, key_down, precision=highest)  82.3 us
    dot_general x4, matrix products, mixer(): jnp.einsum('rnihd,rnhde->rnihe', query_up * fresh_mask, before, precision...  80.9 us
    dot_general x3, matrix products, mixer(): jnp.einsum('rnjhd,rnjhe->rnhde', key_tail, value_blocks, precision=highest)  67.2 us
    dot_general x8, matrix products, left_grad(): lax.dot_general(grad, weight, (((1,), (1,)), ((), ())), preferred_element...  61.4 us
    dot_general x8, matrix products, flat_dot(): return jnp.dot(left, right, preferred_element_type=jnp.float32)  61.3 us
    unnamed x179, local copies, waits for them, and re-layouts  54.8 us
    dot_general x3, matrix products, mixer(): jnp.einsum('rnhij,rnjhe->rnihe', scores, value_blocks, precision=highest)  52.4 us
  transfers between devices with their start and end apart: 9, of which 1 were waited for; matrix products, arithmetic and copies ran while one was open for 23% of the time, Pallas kernels for 0%

commit v1 on v0

v1 whole, which is shorter than its diff:
```python
from functools import partial

import jax
import jax.numpy as jnp
from jax import lax
from jax.experimental import pallas as pl
from jax.experimental.pallas import tpu as pltpu
from jax.sharding import PartitionSpec as P

D = 1024
HEADS = 16
HEAD_DIM = 64
GROUPS = 2
LATENT = 256
FF = 2816
LEN = 1024
WIDTH = HEADS * HEAD_DIM
SPAN = 128
LANES = 256
PACK = LANES // HEAD_DIM
BANDS = WIDTH // LANES
CHUNKS = LEN // SPAN
LIMIT = 85.0
AXES = ("dp", "fsdp")
BF = jnp.bfloat16
F32 = jnp.float32


def mm(left, right):
    return lax.dot_general(left, right, (((1,), (0,)), ((), ())), preferred_element_type=F32)


def mm_nt(left, right):
    return lax.dot_general(left, right, (((1,), (1,)), ((), ())), preferred_element_type=F32)


def mm_tn(left, right):
    return lax.dot_general(left, right, (((0,), (0,)), ((), ())), preferred_element_type=F32)


def halves(value):
    high = value.astype(BF)
    return high, (value - high.astype(F32)).astype(BF)


def exact_left(ones, value):
    high, rest = halves(value)
    return mm(ones, high) + mm(ones, rest)


def exact_right(value, ones):
    high, rest = halves(value)
    return mm(high, ones) + mm(rest, ones)


def head_masks():
    lane = lax.broadcasted_iota(jnp.int32, (1, LANES), 1) // HEAD_DIM
    return [lane == head for head in range(PACK)]


def stacked(value, masks):
    zero = jnp.zeros_like(value)
    return jnp.concatenate([jnp.where(mask, value, zero) for mask in masks], axis=0)


def side_by_side(value):
    return jnp.concatenate([value[h * SPAN : (h + 1) * SPAN] for h in range(PACK)], axis=1)


def same_head():
    row = lax.broadcasted_iota(jnp.int32, (LANES, LANES), 0) // HEAD_DIM
    col = lax.broadcasted_iota(jnp.int32, (LANES, LANES), 1) // HEAD_DIM
    return row == col


def triangle(lower):
    row = lax.broadcasted_iota(jnp.int32, (SPAN, SPAN), 0)
    col = lax.broadcasted_iota(jnp.int32, (SPAN, SPAN), 1)
    return (row >= col) if lower else (row <= col)


def decays(decay, pad, lower_ones):
    small = jnp.exp(-jnp.abs(decay))
    log_sig = jnp.minimum(decay, 0.0) - jnp.log(1.0 + small)
    total = exact_left(lower_ones, log_sig * (pad * (1.0 / 16.0)))
    ending = total[SPAN - 1 : SPAN]
    middle = 0.5 * ending
    centred = total - middle
    up = jnp.exp(jnp.minimum(centred, LIMIT))
    down = jnp.exp(jnp.minimum(-centred, LIMIT))
    half = jnp.exp(middle)
    return up, down, half, small


def flags(cols_ref, seg_ref, rows, index):
    cols = cols_ref[rows, :]
    seg_col, fresh, to_end, pad = cols[:, 0:1], cols[:, 1:2], cols[:, 2:3], cols[:, 3:4]
    allowed = (seg_col == seg_ref[index]) & triangle(True)
    return fresh, to_end, pad, allowed, fresh[SPAN - 1 : SPAN]


def mixer_fwd_kernel(
    q_ref, k_ref, v_ref, decay_ref, gate_ref, gain_ref, cols_ref, seg_ref, mixed_ref, heads_ref, states_ref, state
):
    masks = head_masks()
    diag = same_head()
    diag_ones = diag.astype(F32).astype(BF)
    lower_ones = triangle(True).astype(F32).astype(BF)
    state[...] = jnp.zeros_like(state)
    gain = gain_ref[...]

    def chunk(index, carry):
        rows = pl.ds(pl.multiple_of(index * SPAN, SPAN), SPAN)
        fresh, to_end, pad, allowed, keep = flags(cols_ref, seg_ref, rows, index)
        up, down, half, _ = decays(decay_ref[rows, :], pad, lower_ones)
        query = q_ref[rows, :] * (HEAD_DIM**-0.5) * up
        key = k_ref[rows, :] * pad * down
        value = v_ref[rows, :].astype(BF)
        query_low, key_low = query.astype(BF), key.astype(BF)
        scores = mm_nt(stacked(query_low, masks), key_low)
        scores = scores.reshape(PACK, SPAN, SPAN)
        scores = jnp.where(allowed[None], scores, 0.0).astype(BF).reshape(PACK * SPAN, SPAN)
        old = state[...]
        old_low = old.astype(BF)
        states_ref[0, index] = old_low
        heads = mm(side_by_side(scores), stacked(value, masks))
        heads += mm_nt((query * (half * fresh)).astype(BF), old_low)
        tail = (key * (half * to_end)).astype(BF)
        state[...] = old * (half * half * keep) + jnp.where(diag, mm_tn(value, tail), 0.0)
        heads_ref[rows, :] = heads
        scale = lax.rsqrt(exact_right(heads * heads, diag_ones) * (1.0 / HEAD_DIM) + 1e-2)
        gate = gate_ref[rows, :]
        silu = gate / (1.0 + jnp.exp(-gate))
        mixed_ref[rows, :] = (heads * scale * gain * silu).astype(BF)
        return carry

    lax.fori_loop(0, CHUNKS, chunk, 0)


def mixer_bwd_kernel(
    q_ref,
    k_ref,
    v_ref,
    decay_ref,
    gate_ref,
    gain_ref,
    cols_ref,
    seg_ref,
    heads_ref,
    states_ref,
    dmix_ref,
    dq_ref,
    dk_ref,
    dv_ref,
    ddecay_ref,
    dgate_ref,
    dbias_ref,
    dgain_ref,
    state,
):
    masks = head_masks()
    diag = same_head()
    diag_ones = diag.astype(F32).astype(BF)
    lower_ones = triangle(True).astype(F32).astype(BF)
    upper_ones = triangle(False).astype(F32).astype(BF)
    state[...] = jnp.zeros_like(state)
    dbias_ref[...] = jnp.zeros_like(dbias_ref)
    dgain_ref[...] = jnp.zeros_like(dgain_ref)
    gain = gain_ref[...]

    def chunk(step, carry):
        index = CHUNKS - 1 - step
        rows = pl.ds(pl.multiple_of(index * SPAN, SPAN), SPAN)
        fresh, to_end, pad, allowed, keep = flags(cols_ref, seg_ref, rows, index)
        heads = heads_ref[rows, :]
        scale = lax.rsqrt(exact_right(heads * heads, diag_ones) * (1.0 / HEAD_DIM) + 1e-2)
        normed = heads * scale
        gate = gate_ref[rows, :]
        sig = 1.0 / (1.0 + jnp.exp(-gate))
        silu = gate * sig
        dmix = dmix_ref[rows, :]
        both = dmix * normed
        dgain_ref[...] += jnp.sum(both * silu, axis=0, keepdims=True)
        dgate_ref[rows, :] = (both * gain * (sig * (1.0 + gate * (1.0 - sig)))).astype(BF)
        dnormed = dmix * gain * silu
        mean = exact_right(dnormed * normed, diag_ones) * (1.0 / HEAD_DIM)
        dheads = (scale * (dnormed - normed * mean)).astype(BF)
        decay = decay_ref[rows, :]
        up, down, half, small = decays(decay, pad, lower_ones)
        unit = HEAD_DIM**-0.5
        query = q_ref[rows, :] * unit * up
        key = k_ref[rows, :] * pad * down
        value = v_ref[rows, :].astype(BF)
        query_low, key_low = query.astype(BF), key.astype(BF)
        enter = half * fresh
        leave = half * to_end
        query_in = (query * enter).astype(BF)
        tail = (key * leave).astype(BF)
        query_stack = stacked(query_low, masks)
        dheads_stack = stacked(dheads, masks)
        scores = mm_nt(query_stack, key_low).reshape(PACK, SPAN, SPAN)
        scores = jnp.where(allowed[None], scores, 0.0).astype(BF).reshape(PACK * SPAN, SPAN)
        dscores = mm_nt(dheads_stack, value).reshape(PACK, SPAN, SPAN)
        dscores = jnp.where(allowed[None], dscores, 0.0).astype(BF).reshape(PACK * SPAN, SPAN)
        dstate = state[...]
        dstate_low = dstate.astype(BF)
        old = states_ref[0, index]
        dvalue = mm_tn(scores, dheads_stack) + mm_nt(tail, dstate_low)
        dv_ref[rows, :] = dvalue.astype(BF)
        dquery = mm(side_by_side(dscores), stacked(key_low, masks))
        dkey = mm_tn(dscores, query_stack)
        dquery_in = mm(dheads, old)
        dtail = mm(value, dstate_low)
        whole = half * half * keep
        state[...] = dstate * whole + jnp.where(diag, mm_tn(dheads, query_in), 0.0)
        dq_ref[rows, :] = ((dquery + dquery_in * enter) * (up * unit)).astype(BF)
        dk_ref[rows, :] = ((dkey + dtail * leave) * (down * pad)).astype(BF)
        from_tail = dtail * tail.astype(F32)
        dtotal = (
            dquery * query_low.astype(F32)
            - dkey * key_low.astype(F32)
            + dquery_in * query_in.astype(F32)
            - from_tail
        )
        ends = jnp.sum(from_tail, axis=0, keepdims=True)
        ends += whole * jnp.sum(dstate * old.astype(F32), axis=0, keepdims=True)
        dlog = exact_left(upper_ones, dtotal) + ends
        other = jnp.where(decay >= 0, small, 1.0) / (1.0 + small)
        ddecay = dlog * (pad * (1.0 / 16.0)) * other
        dbias_ref[...] += jnp.sum(ddecay, axis=0, keepdims=True)
        ddecay_ref[rows, :] = ddecay.astype(BF)
        return carry

    lax.fori_loop(0, CHUNKS, chunk, 0)


def band_specs():
    tokens = pl.BlockSpec((LEN, LANES), lambda band: (0, band))
    vector = pl.BlockSpec((1, LANES), lambda band: (0, band))
    cols = pl.BlockSpec((LEN, 128), lambda band: (0, 0))
    segs = pl.BlockSpec((CHUNKS, 1, SPAN), lambda band: (0, 0, 0))
    states = pl.BlockSpec((1, CHUNKS, LANES, LANES), lambda band: (band, 0, 0, 0))
    return tokens, vector, cols, segs, states


def mixer_fwd(query, keys, values, decay_in, gate_in, out_gain, cols, segs):
    tokens, vector, cols_spec, segs_spec, states = band_specs()
    return pl.pallas_call(
        mixer_fwd_kernel,
        grid=(BANDS,),
        in_specs=[tokens] * 5 + [vector, cols_spec, segs_spec],
        out_specs=[tokens, tokens, states],
        out_shape=[
            jax.ShapeDtypeStruct((LEN, WIDTH), BF),
            jax.ShapeDtypeStruct((LEN, WIDTH), F32),
            jax.ShapeDtypeStruct((BANDS, CHUNKS, LANES, LANES), BF),
        ],
        scratch_shapes=[pltpu.VMEM((LANES, LANES), F32)],
        compiler_params=pltpu.CompilerParams(vmem_limit_bytes=48 << 20),
        name="mixer_fwd",
    )(query, keys, values, decay_in, gate_in, out_gain, cols, segs)


def mixer_bwd(query, keys, values, decay_in, gate_in, out_gain, cols, segs, heads, states_in, dmix):
    tokens, vector, cols_spec, segs_spec, states = band_specs()
    low = jax.ShapeDtypeStruct((LEN, WIDTH), BF)
    sums = jax.ShapeDtypeStruct((1, WIDTH), F32)
    return pl.pallas_call(
        mixer_bwd_kernel,
        grid=(BANDS,),
        in_specs=[tokens] * 5 + [vector, cols_spec, segs_spec, tokens, states, tokens],
        out_specs=[tokens] * 5 + [vector, vector],
        out_shape=[low] * 5 + [sums, sums],
        scratch_shapes=[pltpu.VMEM((LANES, LANES), F32)],
        compiler_params=pltpu.CompilerParams(vmem_limit_bytes=56 << 20),
        name="mixer_bwd",
    )(query, keys, values, decay_in, gate_in, out_gain, cols, segs, heads, states_in, dmix)


def rms_factor(values, eps):
    return lax.rsqrt(jnp.mean(values * values, axis=-1, keepdims=True) + eps)


def rms_back(grad, values, factor, gain):
    scaled = values * factor
    dscaled = grad * gain
    dvalues = factor * (dscaled - scaled * jnp.mean(dscaled * scaled, axis=-1, keepdims=True))
    return dvalues, jnp.sum(grad * scaled, axis=0)


def gather(shards):
    return [lax.all_gather(piece, AXES, axis=0) for piece in shards]


def scatter(grads):
    return [lax.psum_scatter(piece, AXES, scatter_dimension=0) for piece in grads]


def per_device(
    hidden_in,
    w_query,
    w_latent,
    w_key_up,
    w_value_up,
    w_decay,
    w_outgate,
    w_out,
    w_gate,
    w_up,
    w_down,
    vectors,
    seg_ids,
    pad_mask,
    cotangent,
    *,
    count,
):
    per_group = WIDTH // GROUPS
    latents = GROUPS * LATENT
    rows_d, rows_kv, rows_ff = D // count, latents // count, FF // count

    def rows_of(piece, rows):
        return piece.astype(BF).reshape(rows, -1)

    in_shard = jnp.concatenate(
        [rows_of(piece, rows_d) for piece in (w_query, w_decay, w_outgate, w_latent)], axis=1
    )
    kv_shard = jnp.concatenate([rows_of(w_key_up, rows_kv), rows_of(w_value_up, rows_kv)], axis=1)
    out_shard = rows_of(w_out, rows_d)
    ff_shard = jnp.concatenate([rows_of(w_gate, rows_d), rows_of(w_up, rows_d)], axis=1)
    down_shard = rows_of(w_down, rows_ff)
    vec_shard = rows_of(vectors, 1)
    w_in, w_kv, w_output, w_ff, w_dn, vecs = gather(
        (in_shard, kv_shard, out_shard, ff_shard, down_shard, vec_shard)
    )
    w_in = w_in.reshape(D, 3 * WIDTH + latents)
    w_kv = w_kv.reshape(GROUPS, LATENT, 2 * per_group)
    w_output = w_output.reshape(WIDTH, D)
    w_ff = w_ff.reshape(D, 2 * FF)
    w_dn = w_dn.reshape(FF, D)
    vecs = vecs.reshape(-1).astype(F32)
    gain_in, gain_mid = vecs[:D], vecs[D : 2 * D]
    decay_bias, out_gain = vecs[2 * D : 2 * D + WIDTH], vecs[2 * D + WIDTH :]

    seg = seg_ids.reshape(CHUNKS, SPAN)
    before = jnp.concatenate([jnp.full((1,), -1, seg.dtype), seg[:-1, -1]])
    fresh = (seg == before[:, None]).astype(F32).reshape(LEN, 1)
    to_end = (seg == seg[:, -1:]).astype(F32).reshape(LEN, 1)
    pad = pad_mask.astype(F32).reshape(LEN, 1)
    seg_col = seg_ids.astype(F32).reshape(LEN, 1)
    cols = jnp.concatenate(
        [seg_col, fresh, to_end, pad, jnp.zeros((LEN, 124), F32)], axis=1
    )
    segs = seg_ids.astype(F32).reshape(CHUNKS, 1, SPAN)

    inputs = hidden_in.astype(F32)
    factor_in = rms_factor(inputs, 1e-5)
    normed = (inputs * factor_in * gain_in).astype(BF)
    query = mm(normed, w_in[:, :WIDTH])
    decay_in = mm(normed, w_in[:, WIDTH : 2 * WIDTH]) + decay_bias
    gate_in = mm(normed, w_in[:, 2 * WIDTH : 3 * WIDTH])
    latent = mm(normed, w_in[:, 3 * WIDTH :]).astype(BF)
    keys = jnp.concatenate(
        [mm(latent[:, g * LATENT : (g + 1) * LATENT], w_kv[g, :, :per_group]) for g in range(GROUPS)], axis=1
    )
    values = jnp.concatenate(
        [mm(latent[:, g * LATENT : (g + 1) * LATENT], w_kv[g, :, per_group:]) for g in range(GROUPS)], axis=1
    )
    gain_row = out_gain.reshape(1, WIDTH)
    mixed, heads, states = mixer_fwd(query, keys, values, decay_in, gate_in, gain_row, cols, segs)
    middle = inputs + mm(mixed, w_output)
    factor_mid = rms_factor(middle, 1e-5)
    normed_mid = (middle * factor_mid * gain_mid).astype(BF)
    gate_val = mm(normed_mid, w_ff[:, :FF])
    up_val = mm(normed_mid, w_ff[:, FF:])
    sig = jax.nn.sigmoid(gate_val)
    silu = gate_val * sig
    hidden = (silu * up_val).astype(BF)
    block_out = (middle + mm(hidden, w_dn)).astype(BF)

    d_outf = cotangent.astype(F32) * pad
    d_ffn = d_outf.astype(BF)
    grad_down = mm_tn(hidden, d_ffn)
    d_hidden = mm_nt(d_ffn, w_dn)
    d_gate = (d_hidden * up_val * (sig * (1.0 + gate_val * (1.0 - sig)))).astype(BF)
    d_up = (d_hidden * silu).astype(BF)
    d_both = jnp.concatenate([d_gate, d_up], axis=1)
    grad_ff = mm_tn(normed_mid, d_both)
    d_normed_mid = mm_nt(d_both, w_ff)
    d_middle, d_gain_mid = rms_back(d_normed_mid, middle, factor_mid, gain_mid)
    d_middle = d_middle + d_outf
    d_branch = d_middle.astype(BF)
    grad_out = mm_tn(mixed, d_branch)
    d_mixed = mm_nt(d_branch, w_output)

    d_query, d_keys, d_values, d_decay, d_gatein, d_bias, d_out_gain = mixer_bwd(
        query, keys, values, decay_in, gate_in, gain_row, cols, segs, heads, states, d_mixed
    )
    grad_kv, d_latent = [], []
    for g in range(GROUPS):
        d_kv = jnp.concatenate(
            [part[:, g * per_group : (g + 1) * per_group] for part in (d_keys, d_values)], axis=1
        )
        grad_kv.append(mm_tn(latent[:, g * LATENT : (g + 1) * LATENT], d_kv))
        d_latent.append(mm_nt(d_kv, w_kv[g]))
    grad_kv = jnp.concatenate(grad_kv, axis=0)
    d_latent = jnp.concatenate(d_latent, axis=1).astype(BF)
    d_in = jnp.concatenate([d_query, d_decay, d_gatein, d_latent], axis=1)
    grad_in = mm_tn(normed, d_in)
    d_normed = mm_nt(d_in, w_in)
    d_inputs, d_gain_in = rms_back(d_normed, inputs, factor_in, gain_in)
    grad_input = d_middle + d_inputs
    grad_vec = jnp.concatenate([d_gain_in, d_gain_mid, d_bias.reshape(-1), d_out_gain.reshape(-1)])

    own_in, own_kv, own_out, own_ff, own_down, own_vec = scatter(
        (
            grad_in.reshape(count, rows_d, -1),
            grad_kv.reshape(count, rows_kv, -1),
            grad_out.reshape(count, rows_d, -1),
            grad_ff.reshape(count, rows_d, -1),
            grad_down.reshape(count, rows_ff, -1),
            grad_vec.reshape(count, 1, -1),
        )
    )
    return (
        block_out,
        grad_input,
        own_in[:, :WIDTH].reshape(-1),
        own_in[:, 3 * WIDTH :].reshape(-1),
        own_kv[:, :per_group].reshape(-1),
        own_kv[:, per_group:].reshape(-1),
        own_in[:, WIDTH : 2 * WIDTH].reshape(-1),
        own_in[:, 2 * WIDTH : 3 * WIDTH].reshape(-1),
        own_out.reshape(-1),
        own_ff[:, :FF].reshape(-1),
        own_ff[:, FF:].reshape(-1),
        own_down.reshape(-1),
        own_vec.reshape(-1),
    )


def solution(mesh):
    count = mesh.shape["dp"] * mesh.shape["fsdp"]
    rows, flat = P(AXES, None), P(AXES)
    in_specs = (rows,) + (flat,) * 13 + (rows,)
    out_specs = (rows, rows) + (flat,) * 11
    return jax.shard_map(
        partial(per_device, count=count), mesh=mesh, in_specs=in_specs, out_specs=out_specs, check_vma=False
    )
```

time: 1990 us -> 1360 us (0.68)
  local copies, waits for them, and re-layouts: 400 us -> 47.4 us
  matrix products: 466 us -> 181 us
  waiting for transfers between devices: 728 us -> 926 us
  other arithmetic: 200 us -> 26.5 us
  blocking collectives: 169 us -> 83 us
  Pallas kernels: 0 us -> 77.3 us
    unnamed x10, waiting for transfers between devices: 728 us -> 0.16 us
    reduce_scatter x0 -> x5, waiting for transfers between devices: none -> 723 us  [scatter(): lax.psum_scatter(piece, AXES, scatter_dimension=0)]
    dot_general x43 -> x24, matrix products: 466 us -> 181 us  [the longest x12 76.6 us: mm(): lax.dot_general(left, right, (((1,), (0,)), ((), ())), preferred_element_...]
    all_gather x8 -> x5, waiting for transfers between devices: 0.03 us -> 202 us  [gather(): return [lax.all_gather(piece, AXES, axis=0) for piece in shards]]
    reshape x25 -> x13, local copies, waits for them, and re-layouts: 181 us -> 4.2 us  [the longest x1 1.03 us: per_device(): pad = pad_mask.astype(F32).reshape(LEN, 1)]
    all_gather x3 -> x1, blocking collectives: 128 us -> 43.6 us  [gather(): return [lax.all_gather(piece, AXES, axis=0) for piece in shards]]
    pallas_call x0 -> x2, Pallas kernels: none -> 77.3 us  [the longest x1 44.2 us: mixer_bwd(): pl.pallas_call(mixer_bwd_kernel, grid=(BANDS,), in_specs=[tokens] * 5 + [...]
    add x34 -> x2, other arithmetic: 49.8 us -> 7.83 us  [the longest x1 4.8 us: per_device(): d_middle = d_middle + d_outf]
  transfers between devices with their start and end apart: 9 -> 10, of which waited for: 1 -> 9; matrix products, arithmetic and copies ran while one was open for 23% -> 13% of each run, Pallas kernels for 0% -> 2%
where the time goes in v1:
time: 1360 us
  waiting for transfers between devices  926 us (68%)
  matrix products  181 us (13%)
  blocking collectives  83 us (6%)
  Pallas kernels  77.3 us (6%)
  local copies, waits for them, and re-layouts  47.4 us (3%)
  other arithmetic  26.5 us (2%)
  between operations  15.1 us (1%)
    reduce_scatter x5, waiting for transfers between devices, scatter(): lax.psum_scatter(piece, AXES, scatter_dimension=0)  723 us
    all_gather x5, waiting for transfers between devices, gather(): return [lax.all_gather(piece, AXES, axis=0) for piece in shards]  202 us
    dot_general x12, matrix products, mm(): lax.dot_general(left, right, (((1,), (0,)), ((), ())), preferred_element_...  76.6 us
    dot_general x6, matrix products, mm_tn(): lax.dot_general(left, right, (((0,), (0,)), ((), ())), preferred_element_...  52.1 us
    dot_general x6, matrix products, mm_nt(): lax.dot_general(left, right, (((1,), (1,)), ((), ())), preferred_element_...  52.1 us
    pallas_call x1, Pallas kernels, mixer_bwd(): pl.pallas_call(mixer_bwd_kernel, grid=(BANDS,), in_specs=[tokens] * 5 + [...  44.2 us
    all_gather x1, blocking collectives, gather(): return [lax.all_gather(piece, AXES, axis=0) for piece in shards]  43.6 us
    unnamed x1, blocking collectives  39.4 us
  transfers between devices with their start and end apart: 10, of which 9 were waited for; matrix products, arithmetic and copies ran while one was open for 13% of the time, Pallas kernels for 2%

profile of v1, /device:TPU:0, one launch (start us, length us, event | category | flops | bytes accessed | tf_op | source)
XLA Modules:
  0.0 1356.3 jit_solution(10263420658861036922)
XLA Ops:
  7.2 1.0 convert_element_type.114
  9.1 0.9 convert_element_type.96
  10.1 0.9 convert_element_type.97
  11.0 0.9 convert_element_type.98
  12.0 0.8 convert_element_type.99
  13.6 0.8 convert_element_type.101
  15.9 0.9 convert_element_type.109
  17.6 1.0 convert_element_type.111
  19.9 2.9 copy.87
  23.6 1.0 copy.94
  24.6 1.0 copy.95
  25.7 1.0 copy.92
  26.7 43.6 %all-gather.4 = bf16[32,1,128]{2,1,0:T(2,128)(2,1)S(1)} all-gather(bf16[1,1,128]{2,1,0:T(2,128)(2,1)S(1)} %convert_bitcast_fusion), channel_id=2, replica_groups=mesh['dp'=4,'fsdp'=8] {'dp','fsdp'}, dimensions={0}, use_global_device_ids=true | all-gather | bytes 8448 | tf_op jit(solution)/shard_map/all_gather | solution.py:292
  70.3 3.9 copy.97
  74.3 0.8 broadcast_in_dim.2
  75.1 2.0 concatenate.56.cols_ref
  77.6 3.9 all-gather.13.cloned.1.call-done
  81.6 12.1 fusion.29
  93.6 63.3 %all-gather.15.cloned.1.call-done = bf16[1024,3584]{1,0:T(8,128)(2,1)} async-done(((bf16[32,3584]{1,0:T(8,128)(2,1)}), bf16[1024,3584]{1,0:T(8,128)(2,1)}) %all-gather.15.cloned.1.call-update) | async-done | bytes 7340048 | tf_op jit(solution)/shard_map/all_gather | solution.py:292
  156.9 3.6 convolution_convert_fusion
  160.5 52.4 %all-gather.17.cloned.1.call-done = bf16[512,1024]{1,0:T(8,128)(2,1)} async-done(((bf16[16,1024]{1,0:T(8,128)(2,1)}), bf16[512,1024]{1,0:T(8,128)(2,1)}) %all-gather.17.cloned.1.call-update) | async-done | bytes 1048592 | tf_op jit(solution)/shard_map/all_gather | solution.py:292
  212.9 1.7 fusion.47
  214.6 1.5 fusion.49
  217.0 4.5 pad_maximum_fusion.3
  221.6 6.2 fusion.19.gate_ref
  227.7 6.2 fusion.23.q_ref
  233.9 6.2 broadcast_add_fusion.decay_ref
  240.1 33.1 %mixer_fwd.1 = (bf16[1024,1024]{1,0:T(8,128)(2,1)S(1)}, f32[1024,1024]{1,0:T(8,128)}, bf16[4,8,256,256]{3,2,1,0:T(8,128)(2,1)}) custom-call(f32[1024,1024]{1,0:T(8,128)} %fusion.23.q_ref, f32[1024,1024]{1,0:T(8,128)} %get-tuple-element.112.k_ref, f32[1024,1024]{1,0:T(8,128)} %get-tuple-element.113.v_ref, f32[1024,1024]{1,0:T(8,128)} %broadcast_add_fusion.decay_ref, ...), custom_call_target="tpu_custom_call" | custom-call | tf_op jit(solution)/shard_map/mixer_fwd/pallas_call | solution.py:248
  273.2 4.9 multiply_reduce_fusion.2
  278.1 1.9 copy-done.5
  280.1 1.7 multiply_convert_fusion.3
  281.8 82.7 %all-gather.19.cloned.1.call-done = bf16[1024,5632]{1,0:T(8,128)(2,1)} async-done(((bf16[32,5632]{1,0:T(8,128)(2,1)}), bf16[1024,5632]{1,0:T(8,128)(2,1)}) %all-gather.19.cloned.1.call-update) | async-done | bytes 11534352 | tf_op jit(solution)/shard_map/all_gather | solution.py:292
  364.5 11.8 fusion.7
  376.3 23.1 %multiply_convert_fusion.1 = (bf16[1024,2816]{1,0:T(8,128)(2,1)}, bf16[1024,2816]{1,0:T(8,128)(2,1)}, bf16[1024,2816]{1,0:T(8,128)(2,1)}) fusion(f32[1024,2816]{1,0:T(8,128)} %fusion.29, f32[1024,2816]{1,0:T(8,128)} %fusion.7, bf16[1024,1024]{0,1:T(8,128)(2,1)} %multiply_convert_fusion.3, bf16[1024,5632]{1,0:T(8,128)(2,1)} %all-gather.19.cloned.1.call-done), kind=kOutput, calls=%fused_computation.2 | convolution fusion | flops 5948833792 | bytes 48234496 | tf_op jit(solution)/shard_map/dot_general | solution.py:30
  399.4 21.5 %multiply_reduce_fusion = (f32[1024]{0:T(1024)}, f32[1024]{0:T(1024)S(1)}, f32[1024,1024]{0,1:T(8,128)}) fusion(f32[1024,1024]{0,1:T(8,128)} %copy-done.5, f32[1024]{0:T(1024)S(1)} %add_rsqrt_fusion, f32[1024]{0:T(1024)S(1)} %bitcast.119, bf16[1024,5632]{1,0:T(8,128)(2,1)} %all-gather.19.cloned.1.call-done, bf16[1024,2816]{1,0:T(8,128)(2,1)} %get-tuple-element.90, ...), kind=kOutput, calls=%fused_computation.28 | convolution fusion | flops 11840518144 | bytes 31473664 | tf_op jit(solution)/shard_map/dot_general | solution.py:34
  420.9 4.8 multiply_add_fusion
  425.7 4.3 fusion.42.dmix_ref
  430.1 44.2 %mixer_bwd.1 = (bf16[1024,1024]{1,0:T(8,128)(2,1)}, bf16[1024,1024]{1,0:T(8,128)(2,1)}, bf16[1024,1024]{1,0:T(8,128)(2,1)}, bf16[1024,1024]{1,0:T(8,128)(2,1)}, ...) custom-call(f32[1024,1024]{1,0:T(8,128)} %fusion.23.q_ref, ...), custom_call_target="tpu_custom_call" | custom-call | tf_op jit(solution)/shard_map/mixer_bwd/pallas_call | solution.py:268
  474.2 1.8 fusion.70
  478.2 1.5 pad_maximum_fusion.7
  479.8 6.7 fusion.40
  486.5 1.5 copy-done.9
  488.0 11.5 fusion.27
  499.7 1.9 constant_dynamic-update-slice_fusion.2
  505.4 0.8 copy-done.4
  506.2 11.0 fusion.64
  517.3 21.5 %fusion.1 = f32[1024,5632]{1,0:T(8,128)} fusion(bf16[1024,1024]{0,1:T(8,128)(2,1)} %multiply_convert_fusion.3, bf16[1024,2816]{1,0:T(8,128)(2,1)} %get-tuple-element.90, bf16[1024,2816]{1,0:T(8,128)(2,1)} %get-tuple-element.89), kind=kOutput, calls=%fused_computation.6 | convolution fusion | flops 11834228736 | bytes 36700160 | tf_op jit(solution)/shard_map/dot_general | solution.py:38
  538.8 12.7 fusion.16
  551.5 3.0 fusion.15
  554.6 5.4 copy.107
  559.9 10.6 add_convert_fusion
  570.5 2.6 copy.106
  573.1 39.4 %all-reduce = f32[32,1,128]{2,1,0:T(1,128)S(1)} all-reduce(f32[32,1,128]{2,1,0:T(1,128)S(1)} %pad_maximum_fusion.23), channel_id=11, replica_groups=mesh['dp'=4,'fsdp'=8] {'dp','fsdp'}, use_global_device_ids=true, to_apply=%region_11.0.clone | all-reduce | flops 4096 | bytes 32768
  613.0 4.4 reduce-scatter.8.cloned.1.call-done
  617.4 0.8 slice_bitcast_fusion.12
  619.4 140.4 %reduce-scatter.10.cloned.1.call-done = f32[1,32,1024]{2,1,0:T(8,128)} async-done(((f32[32,32,1024]{2,1,0:T(8,128)}), f32[1,32,1024]{2,1,0:T(8,128)}) %reduce-scatter.10.cloned.1.call-update) | async-done | bytes 131088 | tf_op jit(solution)/shard_map/reduce_scatter | solution.py:296
  759.8 1.6 copy.123
  761.4 160.6 %reduce-scatter.14.cloned.1.call-done = f32[1,88,1024]{2,1,0:T(8,128)} async-done(((f32[32,88,1024]{2,1,0:T(8,128)}), f32[1,88,1024]{2,1,0:T(8,128)}) %reduce-scatter.14.cloned.1.call-update) | async-done | bytes 360464 | tf_op jit(solution)/shard_map/reduce_scatter | solution.py:296
  922.0 1.8 copy.124
  923.7 170.1 %reduce-scatter.6.cloned.1.call-done = f32[1,32,3584]{2,1,0:T(8,128)} async-done(((f32[32,32,3584]{2,1,0:T(8,128)}), f32[1,32,3584]{2,1,0:T(8,128)}) %reduce-scatter.6.cloned.1.call-update) | async-done | bytes 458768 | tf_op jit(solution)/shard_map/reduce_scatter | solution.py:296
  1093.9 1.1 slice_bitcast_fusion.8
  1097.0 0.8 slice_bitcast_fusion.11
  1098.5 247.9 %reduce-scatter.12.cloned.1.call-done = f32[1,32,5632]{2,1,0:T(8,128)} async-done(((f32[32,32,5632]{2,1,0:T(8,128)}), f32[1,32,5632]{2,1,0:T(8,128)}) %reduce-scatter.12.cloned.1.call-update) | async-done | bytes 720912 | tf_op jit(solution)/shard_map/reduce_scatter | solution.py:296
  1346.4 1.1 fusion.72
  (132 shorter events, 19.5 us)
Async XLA Ops:
  7.2 11.6 copy-start.24
  7.2 74.4 %all-gather.13.cloned.1.call-start = ((), (), s32[]{:S(2)}) async-start(), calls=%async_computation.6 | async-start | bytes 5947392 | tf_op jit(solution)/shard_map/all_gather | solution.py:292
  9.1 147.9 %all-gather.15.cloned.1.call-start = ((), (), s32[]{:S(2)}) async-start(), calls=%async_computation.12 | async-start | bytes 7569408 | tf_op jit(solution)/shard_map/all_gather | solution.py:292
  12.8 10.0 copy-start.25
  13.6 199.3 %all-gather.17.cloned.1.call-start = ((), (), s32[]{:S(2)}) async-start(), calls=%async_computation.13 | async-start | bytes 1081344 | tf_op jit(solution)/shard_map/all_gather | solution.py:292
  15.9 257.4 %all-gather.11.cloned.1.call-start = ((), (), s32[]{:S(2)}) async-start(), calls=%async_computation.5 | async-start | bytes 2162688 | tf_op jit(solution)/shard_map/all_gather | solution.py:292
  16.8 7.8 copy-start.26
  17.5 347.0 %all-gather.19.cloned.1.call-start = ((), (), s32[]{:S(2)}) async-start(), calls=%async_computation.14 | async-start | bytes 11894784 | tf_op jit(solution)/shard_map/all_gather | solution.py:292
  18.8 7.9 copy-start.31
  19.9 597.5 %reduce-scatter.8.cloned.1.call-start = ((), (), s32[]{:S(2)}) async-start(), calls=%async_computation.8 | async-start | bytes 2162688 | tf_op jit(solution)/shard_map/reduce_scatter | solution.py:296
  22.8 211.1 %copy-start.3 = (bf16[1024,1024]{0,1:T(8,128)(2,1)}, bf16[1024,1024]{0,1:T(8,128)(2,1)S(1)}, u32[]{:S(2)}) copy-start(bf16[1024,1024]{0,1:T(8,128)(2,1)S(1)} %copy.87) | copy-start | bytes 6291460
  22.8 217.2 %copy-start.1 = (f32[1024]{0:T(1024)}, f32[1024]{0:T(1024)S(1)}, u32[]{:S(2)}) copy-start(f32[1024]{0:T(1024)S(1)} %convert_element_type.103) | copy-start | bytes 12292
  77.1 163.0 %copy-start = (f32[1024,128]{1,0:T(8,128)}, f32[1024,128]{1,0:T(8,128)S(1)}, u32[]{:S(2)}) copy-start(f32[1024,128]{1,0:T(8,128)S(1)} %concatenate.56.cols_ref) | copy-start | bytes 1572868
  77.6 162.5 %copy-start.2 = (f32[1,1024]{1,0:T(1,128)}, f32[1,1024]{1,0:T(1,128)S(1)}, u32[]{:S(2)}) copy-start(f32[1,1024]{1,0:T(1,128)S(1)} %slice_bitcast_fusion.14.gain_ref) | copy-start | bytes 12292
  212.9 3.2 copy-start.10
  212.9 3.2 copy-start.21
  278.1 2.0 copy-start.5
  399.4 21.5 %copy-start.8 = (bf16[1024,1024]{0,1:T(8,128)(2,1)S(1)}, bf16[1024,1024]{0,1:T(8,128)(2,1)}, u32[]{:S(2)}) copy-start(bf16[1024,1024]{0,1:T(8,128)(2,1)} %copy.97) | copy-start | bytes 6291460
  420.9 4.8 copy-start.30
  425.7 4.3 copy-start.6
  474.2 2.2 copy-start.14
  474.2 2.5 copy-start.11
  476.1 1.4 copy-start.17
  476.6 1.6 copy-start.15
  476.6 1.6 copy-start.19
  479.7 280.1 %reduce-scatter.10.cloned.1.call-start = ((), (), s32[]{:S(2)}) async-start(), calls=%async_computation.9 | async-start | bytes 4325376 | tf_op jit(solution)/shard_map/reduce_scatter | solution.py:296
  486.4 1.6 copy-start.9
  486.5 435.5 %reduce-scatter.14.cloned.1.call-start = ((), (), s32[]{:S(2)}) async-start(), calls=%async_computation.11 | async-start | bytes 11894784 | tf_op jit(solution)/shard_map/reduce_scatter | solution.py:296
  499.6 2.2 copy-start.13
  499.6 594.3 %reduce-scatter.6.cloned.1.call-start = ((), (), s32[]{:S(2)}) async-start(), calls=%async_computation.7 | async-start | bytes 15138816 | tf_op jit(solution)/shard_map/reduce_scatter | solution.py:296
  499.7 2.8 copy-start.12
  501.8 1.4 copy-start.18
  501.8 1.7 copy-start.20
  501.8 2.0 copy-start.22
  502.5 2.1 copy-start.16
  504.6 1.6 copy-start.4
  506.2 11.0 copy-start.23
  517.2 829.1 %reduce-scatter.12.cloned.1.call-start = ((), (), s32[]{:S(2)}) async-start(), calls=%async_computation.10 | async-start | bytes 23789568 | tf_op jit(solution)/shard_map/reduce_scatter | solution.py:296
  538.8 12.8 copy-start.7
  570.5 2.6 copy-start.27
  570.5 2.6 copy-start.28
  570.5 2.6 copy-start.29
Sparse Core Ops, SparseCore 0:
  11.4 70.0 all-gather.12
  85.0 71.8 all-gather.14
  160.5 52.3 all-gather.16
  216.3 55.3 all-gather.10
  275.0 89.4 all-gather.18
  479.8 137.5 reduce-scatter.7
  619.7 140.0 reduce-scatter.9
  762.1 159.7 reduce-scatter.13
  924.3 169.5 reduce-scatter.5
  1096.0 250.2 reduce-scatter.11

commit v2 on v1

--- a/solution.py
+++ b/solution.py
@@ -24,6 +24,7 @@
 AXES = ("dp", "fsdp")
 BF = jnp.bfloat16
 F32 = jnp.float32
+MESH = pl.DeviceIdType.MESH
 
 
 def mm(left, right):
@@ -277,6 +278,352 @@
     )(query, keys, values, decay_in, gate_in, out_gain, cols, segs, heads, states_in, dmix)
 
 
+class Place:
+    def __init__(self, ring_size, line_size):
+        self.ring_size, self.line_size = ring_size, line_size
+        self.d, f = lax.axis_index("dp"), lax.axis_index("fsdp")
+        self.z, self.core = f // 2, f % 2
+        self.pos = self.at_ring(self.d)
+
+    def at_ring(self, index):
+        if self.ring_size != 4:
+            return index
+        return index + (index // 2) * (1 - 2 * (index % 2))
+
+    def ring(self, offset):
+        return self.at_ring((self.pos + offset + self.ring_size) % self.ring_size)
+
+    def far(self, i):
+        n = self.line_size
+        low = self.z < n // 2
+        near = jnp.where(low, self.z, n - 1 - self.z)
+        if i == n - 1:
+            return self.z
+        line = n - 1 - i - jnp.where(n - 1 - i <= near, 1, 0)
+        return jnp.where(low, line, n - 1 - line)
+
+    def device(self, d, z, core):
+        return (d, 2 * z + core)
+
+    def slot(self, d, z, core):
+        return d * (2 * self.line_size) + 2 * z + core
+
+
+def greet(place, peers):
+    barrier = pltpu.get_barrier_semaphore()
+    for peer in peers:
+        pl.semaphore_signal(barrier, inc=1, device_id=peer, device_id_type=MESH)
+    pl.semaphore_wait(barrier, len(peers))
+
+
+def peers_of(place):
+    me = place
+    peers = [me.device(me.d, me.z, 1 - me.core)]
+    peers += [me.device(me.ring(step), me.z, me.core) for step in (1, -1)]
+    peers += [me.device(me.d, me.far(i), me.core) for i in range(me.line_size - 1)]
+    return peers
+
+
+def send(src, dst, send_sem, recv_sem, device):
+    return pltpu.make_async_remote_copy(
+        src_ref=src, dst_ref=dst, send_sem=send_sem, recv_sem=recv_sem, device_id=device, device_id_type=MESH
+    )
+
+
+def scatter_kernel(ring_size, line_size, ways, *refs):
+    kinds = len(ways)
+    grads, outs = refs[:kinds], refs[kinds : 2 * kinds]
+    accs, parts, hops, tails = (refs[(2 + k) * kinds : (3 + k) * kinds] for k in range(4))
+    load_sem, psend, precv, hsend, hrecv, tsend, trecv = refs[6 * kinds :]
+    me = Place(ring_size, line_size)
+    last = line_size - 1
+    order = [me.far(i) for i in range(line_size)]
+    waves = [
+        (step, wave - step)
+        for wave in range(1, ring_size + line_size)
+        for step in range(1, ring_size + 1)
+        if 0 <= wave - step < line_size
+    ]
+
+    def dest(a, step):
+        return me.ring(-step * ways[a])
+
+    def load(a, step, i):
+        src = grads[a].at[me.slot(dest(a, step), order[i], me.core)]
+        return pltpu.make_async_copy(src, accs[a].at[step - 1, i], load_sem.at[a, step - 1, i])
+
+    def to_pair(a, step, i):
+        src = grads[a].at[me.slot(dest(a, step), order[i], 1 - me.core)]
+        return send(
+            src,
+            parts[a].at[step - 1, i],
+            psend.at[a, step - 1, i],
+            precv.at[a, step - 1, i],
+            me.device(me.d, me.z, 1 - me.core),
+        )
+
+    def to_ring(a, step, i):
+        return send(
+            accs[a].at[step - 1, i],
+            hops[a].at[step - 1, i],
+            hsend.at[a, step - 1, i],
+            hrecv.at[a, step - 1, i],
+            me.device(me.ring(ways[a]), me.z, me.core),
+        )
+
+    def to_line(a, i):
+        return send(
+            accs[a].at[ring_size - 1, i],
+            tails[a].at[me.z],
+            tsend.at[a, i],
+            trecv.at[a, me.z],
+            me.device(me.d, order[i], me.core),
+        )
+
+    def from_line(a, i):
+        here = tails[a].at[order[i]]
+        return send(here, here, tsend.at[a, i], trecv.at[a, order[i]], me.device(me.d, order[i], me.core))
+
+    for step, i in waves:
+        for a in range(kinds):
+            load(a, step, i).start()
+    greet(me, peers_of(me))
+    for step, i in waves:
+        for a in range(kinds):
+            to_pair(a, step, i).start()
+
+    def blocks(a):
+        width = grads[a].shape[-1]
+        block = 512 if width % 512 == 0 else width
+        return width // block, block
+
+    def add_up(a, step, i):
+        number, block = blocks(a)
+
+        def body(j, carry):
+            cols = pl.ds(pl.multiple_of(j * block, block), block)
+            total = accs[a][step - 1, i, :, cols].astype(F32) + parts[a][step - 1, i, :, cols].astype(F32)
+            if step > 1:
+                total += hops[a][step - 2, i, :, cols].astype(F32)
+            if step == ring_size and i == last:
+                outs[a][:, cols] = total
+            else:
+                accs[a][step - 1, i, :, cols] = total.astype(accs[a].dtype)
+            return carry
+
+        lax.fori_loop(0, number, body, 0)
+
+    for step, i in waves:
+        for a in range(kinds):
+            load(a, step, i).wait()
+            to_pair(a, step, i).wait_recv()
+            if step > 1:
+                to_ring(a, step - 1, i).wait_recv()
+            add_up(a, step, i)
+            if step < ring_size:
+                to_ring(a, step, i).start()
+            elif i < last:
+                to_line(a, i).start()
+
+    def finish(a):
+        number, block = blocks(a)
+
+        def body(j, carry):
+            cols = pl.ds(pl.multiple_of(j * block, block), block)
+            total = outs[a][:, cols]
+            for i in range(last):
+                total += tails[a][order[i], :, cols].astype(F32)
+            outs[a][:, cols] = total
+            return carry
+
+        lax.fori_loop(0, number, body, 0)
+
+    for a in range(kinds):
+        for i in range(last):
+            from_line(a, i).wait_recv()
+        finish(a)
+    for step, i in waves:
+        for a in range(kinds):
+            to_pair(a, step, i).wait_send()
+            if step < ring_size:
+                to_ring(a, step, i).wait_send()
+            elif i < last:
+                to_line(a, i).wait_send()
+
+
+def scatter(grads, ways, ring_size, line_size, ident):
+    kinds = len(grads)
+    shapes = [grad.shape[1:] for grad in grads]
+    types = [grad.dtype for grad in grads]
+
+    def room(*lead):
+        return [pltpu.VMEM(lead + shape, dtype) for shape, dtype in zip(shapes, types)]
+
+    sems = pltpu.SemaphoreType.DMA
+    return pl.pallas_call(
+        partial(scatter_kernel, ring_size, line_size, ways),
+        in_specs=[pl.BlockSpec(memory_space=pl.ANY)] * kinds,
+        out_specs=[pl.BlockSpec(memory_space=pltpu.VMEM)] * kinds,
+        out_shape=[jax.ShapeDtypeStruct(shape, F32) for shape in shapes],
+        scratch_shapes=room(ring_size, line_size)
+        + room(ring_size, line_size)
+        + room(ring_size - 1, line_size)
+        + room(line_size)
+        + [sems((kinds, ring_size, line_size))] * 5
+        + [sems((kinds, line_size))] * 2,
+        compiler_params=pltpu.CompilerParams(
+            collective_id=ident, has_side_effects=True, vmem_limit_bytes=60 << 20
+        ),
+        name="scatter_sums",
+    )(*grads)
+
+
+def gather_kernel(ring_size, line_size, *refs):
+    sem_refs = refs[-11:]
+    kinds = (len(refs) - 11) // 2
+    shards, outs = refs[:kinds], refs[kinds : 2 * kinds]
+    own_sem, zsend, zrecv, hsend, hrecv, osend, orecv, psend, precv, qsend, qrecv = sem_refs
+    me = Place(ring_size, line_size)
+    order = [me.far(line_size - 1 - i) for i in range(line_size)]
+    pair = me.device(me.d, me.z, 1 - me.core)
+    ways = (1, -1)
+    mine = me.slot(me.d, me.z, me.core)
+
+    def half(a, way):
+        width = shards[a].shape[-1]
+        if width % 256:
+            return pl.ds(0, width)
+        return pl.ds(0 if way == 0 else width // 2, width // 2)
+
+    def halved(a, way):
+        return shards[a].shape[-1] % 256 == 0 or way == 0
+
+    def own(a):
+        return pltpu.make_async_copy(shards[a], outs[a].at[mine], own_sem.at[a])
+
+    def to_line(a, i):
+        return send(
+            shards[a], outs[a].at[mine], zsend.at[a, i], zrecv.at[a, me.z], me.device(me.d, order[i], me.core)
+        )
+
+    def from_line(a, i):
+        here = outs[a].at[me.slot(me.d, order[i], me.core)]
+        return send(here, here, zsend.at[a, i], zrecv.at[a, order[i]], me.device(me.d, order[i], me.core))
+
+    def to_ring(a, i, way):
+        here = outs[a].at[me.slot(me.d, order[i], me.core)]
+        src = shards[a] if i == 0 else here
+        return send(
+            src, here, hsend.at[a, way, i], hrecv.at[a, way, i], me.device(me.ring(ways[way]), me.z, me.core)
+        )
+
+    def came(a, i, way):
+        return outs[a].at[me.slot(me.ring(-ways[way]), order[i], me.core)]
+
+    def from_ring(a, i, way):
+        here = came(a, i, way)
+        return send(
+            here, here, hsend.at[a, way, i], hrecv.at[a, way, i], me.device(me.ring(-ways[way]), me.z, me.core)
+        )
+
+    def onward(a, i, way):
+        here = came(a, i, way).at[:, half(a, way)]
+        return send(
+            here, here, osend.at[a, way, i], orecv.at[a, way, i], me.device(me.ring(ways[way]), me.z, me.core)
+        )
+
+    def from_onward(a, i, way):
+        here = outs[a].at[me.slot(me.ring(2), order[i], me.core), :, half(a, way)]
+        return send(
+            here, here, osend.at[a, way, i], orecv.at[a, way, i], me.device(me.ring(-ways[way]), me.z, me.core)
+        )
+
+    def to_pair(a, i, lane, core):
+        offset = (0, -ways[0], -ways[1])[lane]
+        here = outs[a].at[me.slot(me.ring(offset), order[i], core)]
+        src = shards[a] if (lane == 0 and i == 0 and core is me.core) else here
+        return send(src, here, psend.at[a, lane, i], precv.at[a, lane, i], pair)
+
+    def to_pair_half(a, i, way, core):
+        here = outs[a].at[me.slot(me.ring(2), order[i], core), :, half(a, way)]
+        return send(here, here, qsend.at[a, way, i], qrecv.at[a, way, i], pair)
+
+    every = range(kinds)
+    for a in every:
+        own(a).start()
+    greet(me, peers_of(me))
+    for a in every:
+        for way in range(2):
+            to_ring(a, 0, way).start()
+        for i in range(1, line_size):
+            to_line(a, i).start()
+    for a in every:
+        to_pair(a, 0, 0, me.core).start()
+
+    def line_stage(i):
+        for a in every:
+            from_line(a, i).wait_recv()
+            for way in range(2):
+                to_ring(a, i, way).start()
+            to_pair(a, i, 0, me.core).start()
+
+    def ring_stage(i):
+        for way in range(2):
+            for a in every:
+                from_ring(a, i, way).wait_recv()
+                if halved(a, way):
+                    onward(a, i, way).start()
+                to_pair(a, i, 1 + way, me.core).start()
+
+    def far_stage(i):
+        for way in range(2):
+            for a in every:
+                if halved(a, way):
+                    from_onward(a, i, way).wait_recv()
+                    to_pair_half(a, i, way, me.core).start()
+
+    for wave in range(line_size + 2):
+        if 1 <= wave < line_size:
+            line_stage(wave)
+        if 1 <= wave <= line_size:
+            ring_stage(wave - 1)
+        if 2 <= wave:
+            far_stage(wave - 2)
+    for a in every:
+        own(a).wait()
+        for i in range(line_size):
+            for lane in range(3):
+                to_pair(a, i, lane, 1 - me.core).wait_recv()
+                to_pair(a, i, lane, me.core).wait_send()
+            for way in range(2):
+                to_ring(a, i, way).wait_send()
+                if halved(a, way):
+                    to_pair_half(a, i, way, 1 - me.core).wait_recv()
+                    to_pair_half(a, i, way, me.core).wait_send()
+                    onward(a, i, way).wait_send()
+            if i:
+                to_line(a, i).wait_send()
+
+
+def gather(shards, ring_size, line_size, ident):
+    kinds = len(shards)
+    count = 2 * ring_size * line_size
+    sems = pltpu.SemaphoreType.DMA
+    return pl.pallas_call(
+        partial(gather_kernel, ring_size, line_size),
+        in_specs=[pl.BlockSpec(memory_space=pltpu.VMEM)] * kinds,
+        out_specs=[pl.BlockSpec(memory_space=pl.ANY)] * kinds,
+        out_shape=[jax.ShapeDtypeStruct((count,) + piece.shape, piece.dtype) for piece in shards],
+        scratch_shapes=[sems((kinds,))]
+        + [sems((kinds, line_size))] * 2
+        + [sems((kinds, 2, line_size))] * 4
+        + [sems((kinds, 3, line_size))] * 2
+        + [sems((kinds, 2, line_size))] * 2,
+        compiler_params=pltpu.CompilerParams(collective_id=ident, has_side_effects=True),
+        name="gather_shards",
+    )(*shards)
+
+
 def rms_factor(values, eps):
     return lax.rsqrt(jnp.mean(values * values, axis=-1, keepdims=True) + eps)
 
@@ -288,12 +635,20 @@
     return dvalues, jnp.sum(grad * scaled, axis=0)
 
 
-def gather(shards):
+def by_kernel(sizes, ring_size, fsdp_size):
+    return ring_size == 4 and fsdp_size % 2 == 0 and all(size % 8 == 0 for size in sizes)
+
+
+def gather_all(shards, sizes, ring_size, fsdp_size):
+    if by_kernel(sizes, ring_size, fsdp_size):
+        return gather(shards, ring_size, fsdp_size // 2, 0)
     return [lax.all_gather(piece, AXES, axis=0) for piece in shards]
 
 
-def scatter(grads):
-    return [lax.psum_scatter(piece, AXES, scatter_dimension=0) for piece in grads]
+def scatter_all(grads, ways, sizes, ring_size, fsdp_size):
+    if by_kernel(sizes, ring_size, fsdp_size):
+        return scatter(grads, ways, ring_size, fsdp_size // 2, 1)
+    return [lax.psum_scatter(piece.astype(F32), AXES, scatter_dimension=0) for piece in grads]
 
 
 def per_device(
@@ -313,11 +668,15 @@
     pad_mask,
     cotangent,
     *,
-    count,
+    ring_size,
+    fsdp_size,
 ):
+    count = ring_size * fsdp_size
     per_group = WIDTH // GROUPS
     latents = GROUPS * LATENT
     rows_d, rows_kv, rows_ff = D // count, latents // count, FF // count
+    rows_all = (rows_d, rows_kv, rows_ff)
+    vec_size = (2 * D + 2 * WIDTH) // count
 
     def rows_of(piece, rows):
         return piece.astype(BF).reshape(rows, -1)
@@ -329,16 +688,16 @@
     out_shard = rows_of(w_out, rows_d)
     ff_shard = jnp.concatenate([rows_of(w_gate, rows_d), rows_of(w_up, rows_d)], axis=1)
     down_shard = rows_of(w_down, rows_ff)
-    vec_shard = rows_of(vectors, 1)
-    w_in, w_kv, w_output, w_ff, w_dn, vecs = gather(
-        (in_shard, kv_shard, out_shard, ff_shard, down_shard, vec_shard)
+    vec_shard = jnp.broadcast_to(lax.reduce_precision(vectors, 8, 7).reshape(1, -1), (8, vec_size))
+    w_in, w_kv, w_output, w_ff, w_dn, vecs = gather_all(
+        (in_shard, kv_shard, out_shard, ff_shard, down_shard, vec_shard), rows_all, ring_size, fsdp_size
     )
     w_in = w_in.reshape(D, 3 * WIDTH + latents)
     w_kv = w_kv.reshape(GROUPS, LATENT, 2 * per_group)
     w_output = w_output.reshape(WIDTH, D)
     w_ff = w_ff.reshape(D, 2 * FF)
     w_dn = w_dn.reshape(FF, D)
-    vecs = vecs.reshape(-1).astype(F32)
+    vecs = vecs[:, 0].reshape(-1)
     gain_in, gain_mid = vecs[:D], vecs[D : 2 * D]
     decay_bias, out_gain = vecs[2 * D : 2 * D + WIDTH], vecs[2 * D + WIDTH :]
 
@@ -412,15 +771,20 @@
     grad_input = d_middle + d_inputs
     grad_vec = jnp.concatenate([d_gain_in, d_gain_mid, d_bias.reshape(-1), d_out_gain.reshape(-1)])
 
-    own_in, own_kv, own_out, own_ff, own_down, own_vec = scatter(
+    grad_vec = jnp.broadcast_to(grad_vec.reshape(count, 1, vec_size), (count, 8, vec_size))
+    own_in, own_kv, own_out, own_ff, own_down, own_vec = scatter_all(
         (
-            grad_in.reshape(count, rows_d, -1),
-            grad_kv.reshape(count, rows_kv, -1),
-            grad_out.reshape(count, rows_d, -1),
-            grad_ff.reshape(count, rows_d, -1),
-            grad_down.reshape(count, rows_ff, -1),
-            grad_vec.reshape(count, 1, -1),
-        )
+            grad_in.astype(BF).reshape(count, rows_d, -1),
+            grad_kv.astype(BF).reshape(count, rows_kv, -1),
+            grad_out.astype(BF).reshape(count, rows_d, -1),
+            grad_ff.astype(BF).reshape(count, rows_d, -1),
+            grad_down.astype(BF).reshape(count, rows_ff, -1),
+            grad_vec,
+        ),
+        (-1, -1, 1, 1, -1, 1),
+        rows_all,
+        ring_size,
+        fsdp_size,
     )
     return (
         block_out,
@@ -435,15 +799,15 @@
         own_ff[:, :FF].reshape(-1),
         own_ff[:, FF:].reshape(-1),
         own_down.reshape(-1),
-        own_vec.reshape(-1),
+        own_vec[0],
     )
 
 
 def solution(mesh):
-    count = mesh.shape["dp"] * mesh.shape["fsdp"]
+    sizes = {"ring_size": mesh.shape["dp"], "fsdp_size": mesh.shape["fsdp"]}
     rows, flat = P(AXES, None), P(AXES)
     in_specs = (rows,) + (flat,) * 13 + (rows,)
     out_specs = (rows, rows) + (flat,) * 11
     return jax.shard_map(
-        partial(per_device, count=count), mesh=mesh, in_specs=in_specs, out_specs=out_specs, check_vma=False
-    )
+        partial(per_device, **sizes), mesh=mesh, in_specs=in_specs, out_specs=out_specs, check_vma=False
+    )

time: 1360 us -> 610 us (0.45)
  waiting for transfers between devices: 926 us -> 0 us
  Pallas kernels: 77.3 us -> 363 us
  blocking collectives: 83 us -> 0 us
  matrix products: 181 us -> 167 us
  between operations: 15.1 us -> 1.37 us
    reduce_scatter x5 -> x0, waiting for transfers between devices: 723 us -> none  [scatter(): lax.psum_scatter(piece, AXES, scatter_dimension=0)]
    pallas_call x0 -> x2, Pallas kernels: none -> 286 us  [the longest x1 146 us: scatter(): pl.pallas_call(partial(scatter_kernel, ring_size, line_size, ways), in_sp...]
    all_gather x5 -> x0, waiting for transfers between devices: 202 us -> none  [gather(): return [lax.all_gather(piece, AXES, axis=0) for piece in shards]]
    all_gather x1 -> x0, blocking collectives: 43.6 us -> none  [gather(): return [lax.all_gather(piece, AXES, axis=0) for piece in shards]]
    unnamed x1 -> x0, blocking collectives: 39.4 us -> none
    unnamed x82 -> x78, local copies, waits for them, and re-layouts: 33.8 us -> 31.6 us
  transfers between devices with their start and end apart: 10 -> 0, of which waited for: 9 -> 0; matrix products, arithmetic and copies ran while one was open for 13% -> 0% of each run, Pallas kernels for 2% -> 0%
where the time goes in v2:
time: 610 us; the launch traced here: 605 us
  Pallas kernels  363 us (60%)
  matrix products  167 us (27%)
  local copies, waits for them, and re-layouts  46.3 us (8%)
  other arithmetic  27.6 us (5%)
    pallas_call x1, Pallas kernels, scatter(): pl.pallas_call(partial(scatter_kernel, ring_size, line_size, ways), in_sp...  146 us
    pallas_call x1, Pallas kernels, gather(): pl.pallas_call(partial(gather_kernel, ring_size, line_size), in_specs=[pl...  141 us
    dot_general x12, matrix products, mm(): lax.dot_general(left, right, (((1,), (0,)), ((), ())), preferred_element_...  74.5 us
    dot_general x6, matrix products, mm_tn(): lax.dot_general(left, right, (((0,), (0,)), ((), ())), preferred_element_...  46.2 us
    dot_general x6, matrix products, mm_nt(): lax.dot_general(left, right, (((1,), (1,)), ((), ())), preferred_element_...  46 us
    pallas_call x1, Pallas kernels, mixer_bwd(): pl.pallas_call(mixer_bwd_kernel, grid=(BANDS,), in_specs=[tokens] * 5 + [...  44.2 us
    pallas_call x1, Pallas kernels, mixer_fwd(): pl.pallas_call(mixer_fwd_kernel, grid=(BANDS,), in_specs=[tokens] * 5 + [...  32.9 us
    unnamed x78, local copies, waits for them, and re-layouts  31.6 us

profile of v2, /device:TPU:0, one launch (start us, length us, event | category | flops | bytes accessed | tf_op | source)
XLA Modules:
  0.0 605.4 jit_solution(232424641528940828)
XLA Ops:
  0.7 0.7 reduce_precision.3
  1.4 0.9 slice_reduce_fusion
  2.2 0.9 slice_reduce_fusion.1
  5.2 0.8 fusion.54
  5.9 0.8 convert_element_type.107
  6.7 0.8 convert_element_type.108
  8.1 0.8 convert_element_type.106
  9.0 0.9 convert_element_type.103
  9.9 0.9 convert_element_type.104
  10.9 0.9 convert_element_type.105
  11.8 0.7 pad_maximum_fusion.25.refs_0_
  12.6 0.9 convert_element_type.109
  14.1 1.0 convert_element_type.110
  15.4 1.0 convert_element_type.111
  16.6 0.8 pad_maximum_fusion.24.refs_3_
  17.4 0.8 reshape.210.refs_4_
  19.1 0.9 concatenate.58.cols_ref
  20.1 3.1 copy.62
  23.6 4.5 copy.72
  28.1 140.8 %gather_shards.1 = (bf16[32,32,3584]{2,1,0:T(8,128)(2,1)}, bf16[32,16,1024]{2,1,0:T(8,128)(2,1)}, bf16[32,32,1024]{2,1,0:T(8,128)(2,1)}, bf16[32,32,5632]{2,1,0:...) custom-call(bf16[32,3584]{1,0:T(8,128)(2,1)} %pad_maximum_fusion.25.refs_0_, ...), custom_call_target="tpu_custom_call" | custom-call | tf_op jit(solution)/shard_map/gather_shards/pallas_call | solution.py:612
  168.9 0.8 fusion.70
  169.7 2.7 convolution_convert_fusion.4
  172.5 1.1 fusion.68
  175.4 4.2 pad_maximum_fusion.3
  179.6 6.1 %broadcast_add_fusion.decay_ref = f32[1024,1024]{1,0:T(8,128)} fusion(f32[1024]{0:T(1024)S(1)} %bitcast.132, bf16[1024,3584]{1,0:T(8,128)(2,1)} %bitcast.138, bf16[1024,1024]{0,1:T(8,128)(2,1)S(1)} %copy.62, f32[1024]{0:T(1024)S(1)} %bitcast.123, f32[1024]{0:T(1024)S(1)} %add_rsqrt_fusion.1), kind=kOutput, calls=%fused_computation.46 | convolution fusion | flops 2152726528 | bytes 8400896 | tf_op jit(solution)/shard_map/dot_general | solution.py:31
  185.8 6.3 %fusion.18.gate_ref = f32[1024,1024]{1,0:T(8,128)} fusion(bf16[1024,3584]{1,0:T(8,128)(2,1)} %bitcast.139, bf16[1024,1024]{0,1:T(8,128)(2,1)S(1)} %copy.62, f32[1024]{0:T(1024)S(1)} %bitcast.124, f32[1024]{0:T(1024)S(1)} %add_rsqrt_fusion.1), kind=kOutput, calls=%fused_computation.38 | convolution fusion | flops 2151677952 | bytes 8396800 | tf_op jit(solution)/shard_map/dot_general | solution.py:31
  192.0 6.7 %fusion.22.q_ref = f32[1024,1024]{1,0:T(8,128)} fusion(bf16[1024,3584]{1,0:T(8,128)(2,1)} %bitcast.140, bf16[1024,1024]{0,1:T(8,128)(2,1)S(1)} %copy.62, f32[1024]{0:T(1024)S(1)} %bitcast.125, f32[1024]{0:T(1024)S(1)} %add_rsqrt_fusion.1), kind=kOutput, calls=%fused_computation.42 | convolution fusion | flops 2151677952 | bytes 8396800 | tf_op jit(solution)/shard_map/dot_general | solution.py:31
  198.8 32.9 %mixer_fwd.1 = (bf16[1024,1024]{1,0:T(8,128)(2,1)S(1)}, f32[1024,1024]{1,0:T(8,128)}, bf16[4,8,256,256]{3,2,1,0:T(8,128)(2,1)}) custom-call(f32[1024,1024]{1,0:T(8,128)} %fusion.22.q_ref, f32[1024,1024]{1,0:T(8,128)} %get-tuple-element.126.k_ref, f32[1024,1024]{1,0:T(8,128)} %get-tuple-element.127.v_ref, f32[1024,1024]{1,0:T(8,128)} %broadcast_add_fusion.decay_ref, ...), custom_call_target="tpu_custom_call" | custom-call | tf_op jit(solution)/shard_map/mixer_fwd/pallas_call | solution.py:249
  231.7 2.8 multiply_reduce_fusion.2
  235.0 1.3 copy-done.16
  236.3 13.4 %fusion.6 = f32[1024,2816]{1,0:T(8,128)} fusion(bf16[1024,1024]{0,1:T(8,128)(2,1)S(1)} %multiply_convert_fusion.3, bf16[1024,5632]{1,0:T(8,128)(2,1)} %bitcast.134), kind=kOutput, calls=%fused_computation.16 | convolution fusion | flops 5905580032 | bytes 19398656 | tf_op jit(solution)/shard_map/dot_general | solution.py:31
  249.7 9.1 %fusion.27 = f32[1024,2816]{1,0:T(8,128)} fusion(bf16[2816,1024]{1,0:T(8,128)(2,1)S(1)} %bitcast.145, bf16[1024,1024]{0,1:T(8,128)(2,1)S(1)} %copy-done.7, f32[1024]{0:T(1024)S(1)} %convert_element_type.120), kind=kOutput, calls=%fused_computation.48 | convolution fusion | flops 5908725760 | bytes 19402752 | tf_op jit(solution)/shard_map/dot_general | solution.py:35
  258.8 23.1 %multiply_convert_fusion.1 = (bf16[1024,2816]{1,0:T(8,128)(2,1)}, bf16[1024,2816]{1,0:T(8,128)(2,1)}, bf16[1024,2816]{1,0:T(8,128)(2,1)}) fusion(f32[1024,2816]{1,0:T(8,128)} %fusion.27, f32[1024,2816]{1,0:T(8,128)} %fusion.6, bf16[1024,1024]{0,1:T(8,128)(2,1)} %copy-done.16, bf16[1024,5632]{1,0:T(8,128)(2,1)} %bitcast.135), kind=kOutput, calls=%fused_computation.2 | convolution fusion | flops 5948833792 | bytes 48234496 | tf_op jit(solution)/shard_map/dot_general | solution.py:31
  281.9 11.6 %add_convert_fusion = bf16[1024,1024]{0,1:T(8,128)(2,1)} fusion(f32[1024,1024]{0,1:T(8,128)} %copy-done.6, bf16[1024,2816]{1,0:T(8,128)(2,1)} %get-tuple-element.102, bf16[2816,1024]{1,0:T(8,128)(2,1)} %bitcast.142), kind=kOutput, calls=%fused_computation.35 | convolution fusion | flops 5907677184 | bytes 17825792 | tf_op jit(solution)/shard_map/dot_general | solution.py:31
  293.5 20.6 %multiply_reduce_fusion = (f32[1024]{0:T(1024)S(1)}, f32[1024]{0:T(1024)S(1)}, f32[1024,1024]{0,1:T(8,128)}) fusion(f32[1024,1024]{0,1:T(8,128)} %copy-done.6, f32[1024]{0:T(1024)S(1)} %add_rsqrt_fusion, f32[1024]{0:T(1024)S(1)} %bitcast.116, bf16[1024,5632]{1,0:T(8,128)(2,1)} %bitcast.136, bf16[1024,2816]{1,0:T(8,128)(2,1)} %get-tuple-element.101, ...), kind=kOutput, calls=%fused_computation.30 | convolution fusion | flops 11840518144 | bytes 31473664 | tf_op jit(solution)/shard_map/dot_general | solution.py:35
  314.1 19.6 %convolution_convert_fusion = bf16[1024,5632]{1,0:T(8,128)(2,1)} fusion(bf16[1024,1024]{0,1:T(8,128)(2,1)} %copy-done.16, bf16[1024,2816]{1,0:T(8,128)(2,1)} %get-tuple-element.101, bf16[1024,2816]{1,0:T(8,128)(2,1)} %get-tuple-element.100), kind=kOutput, calls=%fused_computation.6 | convolution fusion | flops 11839995904 | bytes 25165824 | tf_op jit(solution)/shard_map/dot_general | solution.py:39
  333.7 3.9 copy.79
  337.7 5.3 multiply_add_fusion
  343.0 11.1 %convolution_convert_fusion.2 = bf16[2816,1024]{1,0:T(8,128)(2,1)} fusion(bf16[1024,2816]{1,0:T(8,128)(2,1)} %get-tuple-element.102, bf16[1024,1024]{0,1:T(8,128)(2,1)S(1)} %copy-done.8, f32[1024]{0:T(1024)S(1)} %convert_element_type.120), kind=kOutput, calls=%fused_computation.20 | convolution fusion | flops 5911609344 | bytes 13635584 | tf_op jit(solution)/shard_map/dot_general | solution.py:39
  354.2 3.8 convolution_convert_fusion.3
  358.0 4.4 fusion.41.dmix_ref
  362.3 44.2 %mixer_bwd.1 = (bf16[1024,1024]{1,0:T(8,128)(2,1)}, bf16[1024,1024]{1,0:T(8,128)(2,1)}, bf16[1024,1024]{1,0:T(8,128)(2,1)}, bf16[1024,1024]{1,0:T(8,128)(2,1)}, ...) custom-call(f32[1024,1024]{1,0:T(8,128)} %fusion.22.q_ref, ...), custom_call_target="tpu_custom_call" | custom-call | tf_op jit(solution)/shard_map/mixer_bwd/pallas_call | solution.py:269
  406.6 1.8 fusion.66
  409.0 0.7 fusion.36
  409.8 0.7 fusion.34
  410.5 1.1 pad_maximum_fusion.23
  411.8 0.8 copy-done.13
  413.8 0.7 fusion.38
  414.6 0.7 fusion.37
  415.4 0.8 copy-done.5
  416.2 10.4 %fusion.15 = (f32[1024]{0:T(1024)S(1)}, f32[1024]{0:T(1024)S(1)}, f32[1024,1024]{0,1:T(8,128)S(1)}) fusion(bf16[1024,1024]{0,1:T(8,128)(2,1)S(1)} %copy-done.5, f32[1024]{0:T(1024)S(1)} %copy-done.21, f32[1024]{0:T(1024)S(1)} %bitcast.126, bf16[1024,3584]{1,0:T(8,128)(2,1)S(1)} %fusion.37, bf16[1024,3584]{1,0:T(8,128)(2,1)} %bitcast.141), kind=kOutput, calls=%fused_computation.26 | convolution fusion | flops 7523530752 | bytes 20987904 | tf_op jit(solution)/shard_map/dot_general | solution.py:35
  426.6 10.2 %convolution_convert_fusion.1 = bf16[1024,3584]{1,0:T(8,128)(2,1)} fusion(bf16[1024,3584]{1,0:T(8,128)(2,1)S(1)} %fusion.37, bf16[1024,1024]{0,1:T(8,128)(2,1)S(1)} %copy-done.5, f32[1024]{0:T(1024)S(1)} %bitcast.127, f32[1024]{0:T(1024)S(1)} %copy-done.21), kind=kOutput, calls=%fused_computation.7 | convolution fusion | flops 7524057088 | bytes 16785408 | tf_op jit(solution)/shard_map/dot_general | solution.py:39
  436.8 3.0 fusion.14
  439.8 5.3 copy.80
  445.8 145.6 %scatter_sums.1 = (f32[32,3584]{1,0:T(8,128)}, f32[16,1024]{1,0:T(8,128)}, f32[32,1024]{1,0:T(8,128)}, f32[32,5632]{1,0:T(8,128)}, f32[88,1024]{1,0:T(8,128)}, /*index=5*/f32[8,128]{1,0:T(8,128)}) custom-call(bf16[32,32,3584]{2,1,0:T(8,128)(2,1)} %bitcast.94, bf16[32,16,1024]{2,1,0:T(8,128)(2,1)} %bitcast.100, bf16[32,32,1024]{2,1,0:T(8,128)(2,1)} %bitcast.101, ...), custom_call_target="tpu_custom_call" | custom-call | tf_op jit(solution)/shard_map/scatter_sums/pallas_call | solution.py:463
  591.4 1.6 copy.96
  593.0 0.8 slice_bitcast_fusion.12
  594.4 1.2 slice_bitcast_fusion.15
  596.2 0.8 slice_bitcast_fusion.11
  597.1 1.1 slice_bitcast_fusion.8
  600.8 1.8 copy.97
  602.6 1.1 fusion.69
  603.7 0.8 reshape.233
  604.5 0.8 reshape.232
  (100 shorter events, 14.2 us)
Async XLA Ops:
  0.6 16.7 %copy-start.19 = (f32[90112]{0:T(1024)S(1)}, f32[90112]{0:T(1024)}, u32[]{:S(2)}) copy-start(f32[90112]{0:T(1024)} %param.25) | copy-start | bytes 1081348
  5.2 193.6 %copy-start.1 = (f32[1024]{0:T(1024)}, f32[1024]{0:T(1024)S(1)}, u32[]{:S(2)}) copy-start(f32[1024]{0:T(1024)S(1)} %convert_element_type.115) | copy-start | bytes 12292
  20.1 178.7 %copy-start = (f32[1024,128]{1,0:T(8,128)}, f32[1024,128]{1,0:T(8,128)S(1)}, u32[]{:S(2)}) copy-start(f32[1024,128]{1,0:T(8,128)S(1)} %concatenate.58.cols_ref) | copy-start | bytes 1572868
  23.1 168.9 %copy-start.3 = (bf16[1024,1024]{0,1:T(8,128)(2,1)}, bf16[1024,1024]{0,1:T(8,128)(2,1)S(1)}, u32[]{:S(2)}) copy-start(bf16[1024,1024]{0,1:T(8,128)(2,1)S(1)} %copy.62) | copy-start | bytes 6291460
  23.6 168.4 %copy-start.20 = (f32[1024]{0:T(1024)}, f32[1024]{0:T(1024)S(1)}, u32[]{:S(2)}) copy-start(f32[1024]{0:T(1024)S(1)} %add_rsqrt_fusion.1) | copy-start | bytes 12292
  169.7 22.4 %copy-start.22 = (f32[8,1,128]{2,1,0:T(1,128)}, f32[8,1,128]{2,1,0:T(1,128)S(1)}, u32[]{:S(2)}) copy-start(f32[8,1,128]{2,1,0:T(1,128)S(1)} %get-tuple-element.117) | copy-start | bytes 12292
  169.7 29.1 %copy-start.2 = (f32[1,1024]{1,0:T(1,128)}, f32[1,1024]{1,0:T(1,128)S(1)}, u32[]{:S(2)}) copy-start(f32[1,1024]{1,0:T(1,128)S(1)} %get-tuple-element.115.gain_ref) | copy-start | bytes 12292
  169.7 2.8 copy-start.11
  172.5 2.4 copy-start.9
  198.8 32.9 %copy-start.4 = (bf16[1024,1024]{0,1:T(8,128)(2,1)S(1)}, bf16[1024,1024]{0,1:T(8,128)(2,1)}, u32[]{:S(2)}) copy-start(bf16[1024,1024]{0,1:T(8,128)(2,1)} %copy-done.3) | copy-start | bytes 6291460
  198.8 32.9 %copy-start.26 = (bf16[32,32,1024]{2,1,0:T(8,128)(2,1)S(1)}, bf16[32,32,1024]{2,1,0:T(8,128)(2,1)}, u32[]{:S(2)}) copy-start(bf16[32,32,1024]{2,1,0:T(8,128)(2,1)} %get-tuple-element.39) | copy-start | bytes 6291460
  234.5 15.1 %copy-start.6 = (f32[1024,1024]{0,1:T(8,128)}, f32[1024,1024]{0,1:T(8,128)S(1)}, u32[]{:S(2)}) copy-start(f32[1024,1024]{0,1:T(8,128)S(1)} %get-tuple-element.123) | copy-start | bytes 12582916
  234.6 15.1 %slice-start = ((s8[5767168]{0:T(1024)(128)(4,1)}), s8[4194304]{0:T(1024)(128)(4,1)S(1)}, s32[]{:S(2)}) async-start(s8[5767168]{0:T(1024)(128)(4,1)} %bitcast.143), calls=%async_computation | async-start | bytes 8388608
  235.0 1.3 copy-start.16
  236.3 13.4 %copy-start.7 = (bf16[1024,1024]{0,1:T(8,128)(2,1)S(1)}, bf16[1024,1024]{0,1:T(8,128)(2,1)}, u32[]{:S(2)}) copy-start(bf16[1024,1024]{0,1:T(8,128)(2,1)} %copy.72) | copy-start | bytes 6291460
  236.3 13.4 %slice-start.1 = ((s8[5767168]{0:T(1024)(128)(4,1)}), s8[1572864]{0:T(1024)(128)(4,1)S(1)}, s32[]{:S(2)}) async-start(s8[5767168]{0:T(1024)(128)(4,1)} %bitcast.143), calls=%async_computation.1 | async-start | bytes 3145728
  337.7 5.3 copy-start.8
  354.2 3.8 copy-start.27
  406.6 2.2 copy-start.15
  406.6 2.5 copy-start.10
  409.8 1.9 copy-start.14
  410.5 2.1 copy-start.13
  411.6 1.7 copy-start.12
  412.6 1.2 copy-start.18
  413.4 1.2 copy-start.17
  414.6 1.6 copy-start.5
  414.6 1.6 copy-start.21
  414.6 1.6 copy-start.23
  426.6 10.2 %copy-start.24 = (f32[1,1024]{1,0:T(1,128)S(1)}, f32[1,1024]{1,0:T(1,128)}, u32[]{:S(2)}) copy-start(f32[1,1024]{1,0:T(1,128)} %get-tuple-element.49) | copy-start | bytes 12292
  426.6 10.2 %copy-start.25 = (f32[1,1024]{1,0:T(1,128)S(1)}, f32[1,1024]{1,0:T(1,128)}, u32[]{:S(2)}) copy-start(f32[1,1024]{1,0:T(1,128)} %get-tuple-element.50) | copy-start | bytes 12292

commit v3 on v1

--- a/solution.py
+++ b/solution.py
@@ -24,6 +24,7 @@
 AXES = ("dp", "fsdp")
 BF = jnp.bfloat16
 F32 = jnp.float32
+MESH = pl.DeviceIdType.MESH
 
 
 def mm(left, right):
@@ -99,17 +100,32 @@
     return fresh, to_end, pad, allowed, fresh[SPAN - 1 : SPAN]
 
 
-def mixer_fwd_kernel(
-    q_ref, k_ref, v_ref, decay_ref, gate_ref, gain_ref, cols_ref, seg_ref, mixed_ref, heads_ref, states_ref, state
-):
+def mixer_fwd_kernel(comm, *refs):
+    kinds = comm[2] if comm else 0
+    normed_ref, latent_ref, wq_ref, wd_ref, wg_ref, wk_ref, wv_ref, bias_ref, gain_ref, cols_ref, seg_ref = refs[:11]
+    shards, refs = refs[11 : 11 + kinds], refs[11 + kinds :]
+    q_ref, k_ref, v_ref, decay_ref, gate_ref, mixed_ref, heads_ref, states_ref = refs[:8]
+    gathered, state, sems = refs[8 : 8 + kinds], refs[8 + kinds], refs[9 + kinds :]
+    band = pl.program_id(0)
+    job = Gather(comm[0], comm[1], shards, gathered, sems) if comm else None
+    stages = job.stages() if comm else []
+    ticks = BANDS * (CHUNKS + 1)
+    if comm:
+        pl.when(band == 0)(job.begin)
     masks = head_masks()
     diag = same_head()
     diag_ones = diag.astype(F32).astype(BF)
     lower_ones = triangle(True).astype(F32).astype(BF)
     state[...] = jnp.zeros_like(state)
     gain = gain_ref[...]
+    q_ref[...] = mm(normed_ref[...], wq_ref[...])
+    decay_ref[...] = mm(normed_ref[...], wd_ref[...]) + bias_ref[...]
+    gate_ref[...] = mm(normed_ref[...], wg_ref[...])
+    k_ref[...] = mm(latent_ref[...], wk_ref[0])
+    v_ref[...] = mm(latent_ref[...], wv_ref[0])
 
     def chunk(index, carry):
+        spread(stages, band * (CHUNKS + 1) + index, ticks)
         rows = pl.ds(pl.multiple_of(index * SPAN, SPAN), SPAN)
         fresh, to_end, pad, allowed, keep = flags(cols_ref, seg_ref, rows, index)
         up, down, half, _ = decays(decay_ref[rows, :], pad, lower_ones)
@@ -135,29 +151,25 @@
         return carry
 
     lax.fori_loop(0, CHUNKS, chunk, 0)
-
-
-def mixer_bwd_kernel(
-    q_ref,
-    k_ref,
-    v_ref,
-    decay_ref,
-    gate_ref,
-    gain_ref,
-    cols_ref,
-    seg_ref,
-    heads_ref,
-    states_ref,
-    dmix_ref,
-    dq_ref,
-    dk_ref,
-    dv_ref,
-    ddecay_ref,
-    dgate_ref,
-    dbias_ref,
-    dgain_ref,
-    state,
-):
+    spread(stages, band * (CHUNKS + 1) + CHUNKS, ticks)
+    if comm:
+        pl.when(band == BANDS - 1)(job.finish)
+
+
+def mixer_bwd_kernel(comm, *refs):
+    kinds = comm[2] if comm else 0
+    q_ref, k_ref, v_ref, decay_ref, gate_ref, gain_ref, cols_ref, seg_ref, heads_ref, states_ref = refs[:10]
+    dbranch_ref, wo_ref = refs[10:12]
+    grads, refs = refs[12 : 12 + kinds], refs[12 + kinds :]
+    dq_ref, dk_ref, dv_ref, ddecay_ref, dgate_ref, dbias_ref, dgain_ref = refs[:7]
+    sums, state, dmix_ref, scratch = refs[7 : 7 + kinds], refs[7 + kinds], refs[8 + kinds], refs[9 + kinds :]
+    band = pl.program_id(0)
+    job = scatter_of(comm[0], comm[1], grads, sums, scratch) if comm else None
+    stages = job.stages() if comm else []
+    ticks = BANDS * (CHUNKS + 1)
+    if comm:
+        pl.when(band == 0)(job.begin)
+    dmix_ref[...] = mm_nt(dbranch_ref[...], wo_ref[...])
     masks = head_masks()
     diag = same_head()
     diag_ones = diag.astype(F32).astype(BF)
@@ -169,6 +181,7 @@
     gain = gain_ref[...]
 
     def chunk(step, carry):
+        spread(stages, band * (CHUNKS + 1) + step, ticks)
         index = CHUNKS - 1 - step
         rows = pl.ds(pl.multiple_of(index * SPAN, SPAN), SPAN)
         fresh, to_end, pad, allowed, keep = flags(cols_ref, seg_ref, rows, index)
@@ -232,6 +245,9 @@
         return carry
 
     lax.fori_loop(0, CHUNKS, chunk, 0)
+    spread(stages, band * (CHUNKS + 1) + CHUNKS, ticks)
+    if comm:
+        pl.when(band == BANDS - 1)(job.finish)
 
 
 def band_specs():
@@ -243,38 +259,490 @@
     return tokens, vector, cols, segs, states
 
 
-def mixer_fwd(query, keys, values, decay_in, gate_in, out_gain, cols, segs):
+def fixed(shape):
+    return pl.BlockSpec(shape, lambda band: (0,) * len(shape), pipeline_mode=pl.Buffered(1))
+
+
+def mixer_fwd(normed, latent, w_in, w_kv, bias, gain, cols, segs, shards, comm):
     tokens, vector, cols_spec, segs_spec, states = band_specs()
+    kinds = len(shards)
+    half_bands = BANDS // GROUPS
+    in_specs = [fixed((LEN, D)), pl.BlockSpec((LEN, LATENT), lambda band: (0, band // half_bands))]
+    for part in range(3):
+        in_specs.append(pl.BlockSpec((D, LANES), lambda band, part=part: (0, part * BANDS + band)))
+    for part in range(2):
+        in_specs.append(
+            pl.BlockSpec(
+                (1, LATENT, LANES),
+                lambda band, part=part: (band // half_bands, 0, part * half_bands + band % half_bands),
+            )
+        )
+    in_specs += [vector, vector, cols_spec, segs_spec]
+    wide = jax.ShapeDtypeStruct((LEN, WIDTH), F32)
+    out_shape = [wide] * 5 + [
+        jax.ShapeDtypeStruct((LEN, WIDTH), BF),
+        wide,
+        jax.ShapeDtypeStruct((BANDS, CHUNKS, LANES, LANES), BF),
+    ]
+    scratch = [pltpu.VMEM((LANES, LANES), F32)]
+    params = {}
+    if comm:
+        count = 2 * comm[0] * comm[1]
+        in_specs += [fixed(shard.shape) for shard in shards]
+        out_shape += [jax.ShapeDtypeStruct((count,) + shard.shape, shard.dtype) for shard in shards]
+        scratch += gather_scratch(kinds, comm[1])
+        params = {"collective_id": comm[3], "has_side_effects": True}
+        comm = comm[:2] + (kinds,)
     return pl.pallas_call(
-        mixer_fwd_kernel,
+        partial(mixer_fwd_kernel, comm),
         grid=(BANDS,),
-        in_specs=[tokens] * 5 + [vector, cols_spec, segs_spec],
-        out_specs=[tokens, tokens, states],
-        out_shape=[
-            jax.ShapeDtypeStruct((LEN, WIDTH), BF),
-            jax.ShapeDtypeStruct((LEN, WIDTH), F32),
-            jax.ShapeDtypeStruct((BANDS, CHUNKS, LANES, LANES), BF),
-        ],
-        scratch_shapes=[pltpu.VMEM((LANES, LANES), F32)],
-        compiler_params=pltpu.CompilerParams(vmem_limit_bytes=48 << 20),
+        in_specs=in_specs,
+        out_specs=[tokens] * 7 + [states] + [pl.BlockSpec(memory_space=pl.ANY)] * kinds,
+        out_shape=out_shape,
+        scratch_shapes=scratch,
+        compiler_params=pltpu.CompilerParams(vmem_limit_bytes=52 << 20, **params),
         name="mixer_fwd",
-    )(query, keys, values, decay_in, gate_in, out_gain, cols, segs)
-
-
-def mixer_bwd(query, keys, values, decay_in, gate_in, out_gain, cols, segs, heads, states_in, dmix):
+    )(normed, latent, w_in, w_in, w_in, w_kv, w_kv, bias, gain, cols, segs, *shards)
+
+
+def mixer_bwd(saved, d_branch, w_output, grads, comm):
     tokens, vector, cols_spec, segs_spec, states = band_specs()
+    kinds = len(grads)
     low = jax.ShapeDtypeStruct((LEN, WIDTH), BF)
     sums = jax.ShapeDtypeStruct((1, WIDTH), F32)
+    in_specs = [tokens] * 5 + [vector, cols_spec, segs_spec, tokens, states]
+    in_specs += [fixed((LEN, D)), pl.BlockSpec((LANES, D), lambda band: (band, 0))]
+    out_specs, out_shape = [tokens] * 5 + [vector, vector], [low] * 5 + [sums, sums]
+    scratch = [pltpu.VMEM((LANES, LANES), F32), pltpu.VMEM((LEN, LANES), F32)]
+    params = {}
+    if comm:
+        in_specs += [pl.BlockSpec(memory_space=pl.ANY)] * kinds
+        out_specs += [fixed(grad.shape[1:]) for grad in grads]
+        out_shape += [jax.ShapeDtypeStruct(grad.shape[1:], F32) for grad in grads]
+        scratch += scatter_scratch(grads, comm[0], comm[1])
+        params = {"collective_id": comm[3], "has_side_effects": True}
+        comm = comm[:2] + (kinds,)
     return pl.pallas_call(
-        mixer_bwd_kernel,
+        partial(mixer_bwd_kernel, comm),
         grid=(BANDS,),
-        in_specs=[tokens] * 5 + [vector, cols_spec, segs_spec, tokens, states, tokens],
-        out_specs=[tokens] * 5 + [vector, vector],
-        out_shape=[low] * 5 + [sums, sums],
-        scratch_shapes=[pltpu.VMEM((LANES, LANES), F32)],
-        compiler_params=pltpu.CompilerParams(vmem_limit_bytes=56 << 20),
+        in_specs=in_specs,
+        out_specs=out_specs,
+        out_shape=out_shape,
+        scratch_shapes=scratch,
+        compiler_params=pltpu.CompilerParams(vmem_limit_bytes=63 << 20, **params),
         name="mixer_bwd",
-    )(query, keys, values, decay_in, gate_in, out_gain, cols, segs, heads, states_in, dmix)
+    )(*saved, d_branch, w_output, *grads)
+
+
+class Place:
+    def __init__(self, ring_size, line_size):
+        self.ring_size, self.line_size = ring_size, line_size
+        self.d, f = lax.axis_index("dp"), lax.axis_index("fsdp")
+        self.z, self.core = f // 2, f % 2
+        self.pos = self.at_ring(self.d)
+
+    def at_ring(self, index):
+        if self.ring_size != 4:
+            return index
+        return index + (index // 2) * (1 - 2 * (index % 2))
+
+    def ring(self, offset):
+        return self.at_ring((self.pos + offset + self.ring_size) % self.ring_size)
+
+    def far(self, i):
+        n = self.line_size
+        low = self.z < n // 2
+        near = jnp.where(low, self.z, n - 1 - self.z)
+        if i == n - 1:
+            return self.z
+        line = n - 1 - i - jnp.where(n - 1 - i <= near, 1, 0)
+        return jnp.where(low, line, n - 1 - line)
+
+    def device(self, d, z, core):
+        return (d, 2 * z + core)
+
+    def slot(self, d, z, core):
+        return d * (2 * self.line_size) + 2 * z + core
+
+
+def greet(place, peers):
+    barrier = pltpu.get_barrier_semaphore()
+    for peer in peers:
+        pl.semaphore_signal(barrier, inc=1, device_id=peer, device_id_type=MESH)
+    pl.semaphore_wait(barrier, len(peers))
+
+
+def peers_of(place):
+    me = place
+    peers = [me.device(me.d, me.z, 1 - me.core)]
+    peers += [me.device(me.ring(step), me.z, me.core) for step in (1, -1)]
+    peers += [me.device(me.d, me.far(i), me.core) for i in range(me.line_size - 1)]
+    return peers
+
+
+def send(src, dst, send_sem, recv_sem, device):
+    return pltpu.make_async_remote_copy(
+        src_ref=src, dst_ref=dst, send_sem=send_sem, recv_sem=recv_sem, device_id=device, device_id_type=MESH
+    )
+
+
+class Scatter:
+    def __init__(self, ring_size, line_size, grads, outs, accs, parts, hops, tails, sems):
+        self.ring_size, self.line_size = ring_size, line_size
+        self.grads, self.outs = grads, outs
+        self.accs, self.parts, self.hops, self.tails = accs, parts, hops, tails
+        self.load_sem, self.psend, self.precv, self.hsend, self.hrecv, self.tsend, self.trecv = sems
+        self.me = Place(ring_size, line_size)
+        self.order = [self.me.far(i) for i in range(line_size)]
+        self.every = range(len(grads))
+        self.waves = [
+            (step, wave - step)
+            for wave in range(1, ring_size + line_size)
+            for step in range(1, ring_size + 1)
+            if 0 <= wave - step < line_size
+        ]
+
+    def way(self, a, i):
+        return 1 if (a + i) % 2 == 0 else -1
+
+    def dest(self, a, step, i, core):
+        me = self.me
+        return self.grads[a].at[me.slot(me.ring(-step * self.way(a, i)), self.order[i], core)]
+
+    def load(self, a, step, i):
+        return pltpu.make_async_copy(
+            self.dest(a, step, i, self.me.core), self.accs[a].at[step - 1, i], self.load_sem.at[a, step - 1, i]
+        )
+
+    def to_pair(self, a, step, i):
+        me = self.me
+        return send(
+            self.dest(a, step, i, 1 - me.core),
+            self.parts[a].at[step - 1, i],
+            self.psend.at[a, step - 1, i],
+            self.precv.at[a, step - 1, i],
+            me.device(me.d, me.z, 1 - me.core),
+        )
+
+    def to_ring(self, a, step, i):
+        me = self.me
+        return send(
+            self.accs[a].at[step - 1, i],
+            self.hops[a].at[step - 1, i],
+            self.hsend.at[a, step - 1, i],
+            self.hrecv.at[a, step - 1, i],
+            me.device(me.ring(self.way(a, i)), me.z, me.core),
+        )
+
+    def to_line(self, a, i):
+        me = self.me
+        return send(
+            self.accs[a].at[self.ring_size - 1, i],
+            self.tails[a].at[me.z],
+            self.tsend.at[a, i],
+            self.trecv.at[a, me.z],
+            me.device(me.d, self.order[i], me.core),
+        )
+
+    def from_line(self, a, i):
+        me = self.me
+        here = self.tails[a].at[self.order[i]]
+        return send(
+            here, here, self.tsend.at[a, i], self.trecv.at[a, self.order[i]], me.device(me.d, self.order[i], me.core)
+        )
+
+    def blocks(self, a):
+        width = self.grads[a].shape[-1]
+        block = 512 if width % 512 == 0 else width
+        return width // block, block
+
+    def add_up(self, a, step, i):
+        number, block = self.blocks(a)
+        acc, final = self.accs[a], step == self.ring_size and i == self.line_size - 1
+
+        def body(j, carry):
+            cols = pl.ds(pl.multiple_of(j * block, block), block)
+            total = acc[step - 1, i, :, cols].astype(F32) + self.parts[a][step - 1, i, :, cols].astype(F32)
+            if step > 1:
+                total += self.hops[a][step - 2, i, :, cols].astype(F32)
+            if final:
+                self.outs[a][:, cols] = total
+            else:
+                acc[step - 1, i, :, cols] = total.astype(acc.dtype)
+            return carry
+
+        lax.fori_loop(0, number, body, 0)
+
+    def begin(self):
+        for step, i in self.waves:
+            for a in self.every:
+                self.load(a, step, i).start()
+        greet(self.me, peers_of(self.me))
+        for step, i in self.waves:
+            for a in self.every:
+                self.to_pair(a, step, i).start()
+
+    def entry(self, step, i):
+        for a in self.every:
+            self.load(a, step, i).wait()
+            self.to_pair(a, step, i).wait_recv()
+            if step > 1:
+                self.to_ring(a, step - 1, i).wait_recv()
+            self.add_up(a, step, i)
+            if step < self.ring_size:
+                self.to_ring(a, step, i).start()
+            elif i < self.line_size - 1:
+                self.to_line(a, i).start()
+
+    def stages(self):
+        return [partial(self.entry, step, i) for step, i in self.waves]
+
+    def finish(self):
+        last = self.line_size - 1
+        for a in self.every:
+            for i in range(last):
+                self.from_line(a, i).wait_recv()
+            number, block = self.blocks(a)
+
+            def body(j, carry, a=a, block=block):
+                cols = pl.ds(pl.multiple_of(j * block, block), block)
+                total = self.outs[a][:, cols]
+                for i in range(last):
+                    total += self.tails[a][self.order[i], :, cols].astype(F32)
+                self.outs[a][:, cols] = total
+                return carry
+
+            lax.fori_loop(0, number, body, 0)
+        for step, i in self.waves:
+            for a in self.every:
+                self.to_pair(a, step, i).wait_send()
+                if step < self.ring_size:
+                    self.to_ring(a, step, i).wait_send()
+                elif i < last:
+                    self.to_line(a, i).wait_send()
+
+
+def scatter_scratch(grads, ring_size, line_size):
+    kinds = len(grads)
+    sems = pltpu.SemaphoreType.DMA
+    scratch = []
+    for lead in ((ring_size, line_size), (ring_size, line_size), (ring_size - 1, line_size), (line_size,)):
+        scratch += [pltpu.VMEM(lead + grad.shape[1:], grad.dtype) for grad in grads]
+    return scratch + [sems((kinds, ring_size, line_size))] * 5 + [sems((kinds, line_size))] * 2
+
+
+def scatter_of(ring_size, line_size, grads, outs, scratch):
+    kinds = len(grads)
+    rooms = [scratch[k * kinds : (k + 1) * kinds] for k in range(4)]
+    return Scatter(ring_size, line_size, grads, outs, *rooms, scratch[4 * kinds :])
+
+
+def scatter_kernel(ring_size, line_size, kinds, *refs):
+    job = scatter_of(ring_size, line_size, refs[:kinds], refs[kinds : 2 * kinds], refs[2 * kinds :])
+    job.begin()
+    for stage in job.stages():
+        stage()
+    job.finish()
+
+
+def scatter(grads, ring_size, line_size, ident):
+    kinds = len(grads)
+    return pl.pallas_call(
+        partial(scatter_kernel, ring_size, line_size, kinds),
+        in_specs=[pl.BlockSpec(memory_space=pl.ANY)] * kinds,
+        out_specs=[pl.BlockSpec(memory_space=pltpu.VMEM)] * kinds,
+        out_shape=[jax.ShapeDtypeStruct(grad.shape[1:], F32) for grad in grads],
+        scratch_shapes=scatter_scratch(grads, ring_size, line_size),
+        compiler_params=pltpu.CompilerParams(
+            collective_id=ident, has_side_effects=True, vmem_limit_bytes=60 << 20
+        ),
+        name="scatter_sums",
+    )(*grads)
+
+
+class Gather:
+    def __init__(self, ring_size, line_size, shards, outs, sems):
+        self.line_size = line_size
+        self.shards, self.outs = shards, outs
+        (
+            self.own_sem,
+            self.zsend,
+            self.zrecv,
+            self.hsend,
+            self.hrecv,
+            self.osend,
+            self.orecv,
+            self.psend,
+            self.precv,
+            self.qsend,
+            self.qrecv,
+        ) = sems
+        self.me = Place(ring_size, line_size)
+        self.order = [self.me.far(line_size - 1 - i) for i in range(line_size)]
+        self.pair = self.me.device(self.me.d, self.me.z, 1 - self.me.core)
+        self.mine = self.me.slot(self.me.d, self.me.z, self.me.core)
+        self.every = range(len(shards))
+
+    def half(self, a, way):
+        width = self.shards[a].shape[-1]
+        if width % 256:
+            return pl.ds(0, width)
+        return pl.ds(0 if way == 0 else width // 2, width // 2)
+
+    def halved(self, a, way):
+        return self.shards[a].shape[-1] % 256 == 0 or way == 0
+
+    def beside(self, way):
+        return self.me.device(self.me.ring(1 - 2 * way), self.me.z, self.me.core)
+
+    def spot(self, a, offset, i, core):
+        return self.outs[a].at[self.me.slot(self.me.ring(offset), self.order[i], core)]
+
+    def own(self, a):
+        return pltpu.make_async_copy(self.shards[a], self.outs[a].at[self.mine], self.own_sem.at[a])
+
+    def to_line(self, a, i):
+        me = self.me
+        return send(
+            self.shards[a],
+            self.outs[a].at[self.mine],
+            self.zsend.at[a, i],
+            self.zrecv.at[a, me.z],
+            me.device(me.d, self.order[i], me.core),
+        )
+
+    def from_line(self, a, i):
+        me = self.me
+        here = self.spot(a, 0, i, me.core)
+        return send(
+            here, here, self.zsend.at[a, i], self.zrecv.at[a, self.order[i]], me.device(me.d, self.order[i], me.core)
+        )
+
+    def to_ring(self, a, i, way):
+        here = self.spot(a, 0, i, self.me.core)
+        src = self.shards[a] if i == 0 else here
+        return send(src, here, self.hsend.at[a, way, i], self.hrecv.at[a, way, i], self.beside(way))
+
+    def from_ring(self, a, i, way):
+        here = self.spot(a, 2 * way - 1, i, self.me.core)
+        return send(here, here, self.hsend.at[a, way, i], self.hrecv.at[a, way, i], self.beside(1 - way))
+
+    def onward(self, a, i, way):
+        here = self.spot(a, 2 * way - 1, i, self.me.core).at[:, self.half(a, way)]
+        return send(here, here, self.osend.at[a, way, i], self.orecv.at[a, way, i], self.beside(way))
+
+    def from_onward(self, a, i, way):
+        here = self.spot(a, 2, i, self.me.core).at[:, self.half(a, way)]
+        return send(here, here, self.osend.at[a, way, i], self.orecv.at[a, way, i], self.beside(1 - way))
+
+    def to_pair(self, a, i, lane, core):
+        here = self.spot(a, (0, -1, 1)[lane], i, core)
+        src = self.shards[a] if (lane == 0 and i == 0 and core is self.me.core) else here
+        return send(src, here, self.psend.at[a, lane, i], self.precv.at[a, lane, i], self.pair)
+
+    def to_pair_half(self, a, i, way, core):
+        here = self.spot(a, 2, i, core).at[:, self.half(a, way)]
+        return send(here, here, self.qsend.at[a, way, i], self.qrecv.at[a, way, i], self.pair)
+
+    def begin(self):
+        for a in self.every:
+            self.own(a).start()
+        greet(self.me, peers_of(self.me))
+        for a in self.every:
+            for way in range(2):
+                self.to_ring(a, 0, way).start()
+            for i in range(1, self.line_size):
+                self.to_line(a, i).start()
+        for a in self.every:
+            self.to_pair(a, 0, 0, self.me.core).start()
+
+    def line_stage(self, i):
+        for a in self.every:
+            self.from_line(a, i).wait_recv()
+            for way in range(2):
+                self.to_ring(a, i, way).start()
+            self.to_pair(a, i, 0, self.me.core).start()
+
+    def ring_stage(self, i):
+        for way in range(2):
+            for a in self.every:
+                self.from_ring(a, i, way).wait_recv()
+                if self.halved(a, way):
+                    self.onward(a, i, way).start()
+                self.to_pair(a, i, 1 + way, self.me.core).start()
+
+    def far_stage(self, i):
+        for way in range(2):
+            for a in self.every:
+                if self.halved(a, way):
+                    self.from_onward(a, i, way).wait_recv()
+                    self.to_pair_half(a, i, way, self.me.core).start()
+
+    def stages(self):
+        found = []
+        for wave in range(self.line_size + 2):
+            if 1 <= wave < self.line_size:
+                found.append(partial(self.line_stage, wave))
+            if 1 <= wave <= self.line_size:
+                found.append(partial(self.ring_stage, wave - 1))
+            if 2 <= wave:
+                found.append(partial(self.far_stage, wave - 2))
+        return found
+
+    def finish(self):
+        core = self.me.core
+        for a in self.every:
+            self.own(a).wait()
+            for i in range(self.line_size):
+                for lane in range(3):
+                    self.to_pair(a, i, lane, 1 - core).wait_recv()
+                    self.to_pair(a, i, lane, core).wait_send()
+                for way in range(2):
+                    self.to_ring(a, i, way).wait_send()
+                    if self.halved(a, way):
+                        self.to_pair_half(a, i, way, 1 - core).wait_recv()
+                        self.to_pair_half(a, i, way, core).wait_send()
+                        self.onward(a, i, way).wait_send()
+                if i:
+                    self.to_line(a, i).wait_send()
+
+
+def gather_scratch(kinds, line_size):
+    sems = pltpu.SemaphoreType.DMA
+    return (
+        [sems((kinds,))]
+        + [sems((kinds, line_size))] * 2
+        + [sems((kinds, 2, line_size))] * 4
+        + [sems((kinds, 3, line_size))] * 2
+        + [sems((kinds, 2, line_size))] * 2
+    )
+
+
+def gather_kernel(ring_size, line_size, kinds, *refs):
+    job = Gather(ring_size, line_size, refs[:kinds], refs[kinds : 2 * kinds], refs[2 * kinds :])
+    job.begin()
+    for stage in job.stages():
+        stage()
+    job.finish()
+
+
+def gather(shards, ring_size, line_size, ident):
+    kinds = len(shards)
+    count = 2 * ring_size * line_size
+    return pl.pallas_call(
+        partial(gather_kernel, ring_size, line_size, kinds),
+        in_specs=[pl.BlockSpec(memory_space=pltpu.VMEM)] * kinds,
+        out_specs=[pl.BlockSpec(memory_space=pl.ANY)] * kinds,
+        out_shape=[jax.ShapeDtypeStruct((count,) + piece.shape, piece.dtype) for piece in shards],
+        scratch_shapes=gather_scratch(kinds, line_size),
+        compiler_params=pltpu.CompilerParams(collective_id=ident, has_side_effects=True),
+        name="gather_shards",
+    )(*shards)
+
+
+def spread(stages, tick, ticks):
+    for number, stage in enumerate(stages):
+        pl.when(tick == number * ticks // len(stages))(stage)
 
 
 def rms_factor(values, eps):
@@ -288,12 +756,16 @@
     return dvalues, jnp.sum(grad * scaled, axis=0)
 
 
-def gather(shards):
+def by_kernel(sizes, ring_size, fsdp_size):
+    return ring_size == 4 and fsdp_size % 4 == 0 and all(size % 8 == 0 for size in sizes)
+
+
+def gather_plain(shards):
     return [lax.all_gather(piece, AXES, axis=0) for piece in shards]
 
 
-def scatter(grads):
-    return [lax.psum_scatter(piece, AXES, scatter_dimension=0) for piece in grads]
+def scatter_plain(grads):
+    return [lax.psum_scatter(piece.astype(F32), AXES, scatter_dimension=0) for piece in grads]
 
 
 def per_device(
@@ -313,11 +785,15 @@
     pad_mask,
     cotangent,
     *,
-    count,
+    ring_size,
+    fsdp_size,
 ):
+    count = ring_size * fsdp_size
     per_group = WIDTH // GROUPS
     latents = GROUPS * LATENT
     rows_d, rows_kv, rows_ff = D // count, latents // count, FF // count
+    rows_all = (rows_d, rows_kv, rows_ff)
+    vec_size = (2 * D + 2 * WIDTH) // count
 
     def rows_of(piece, rows):
         return piece.astype(BF).reshape(rows, -1)
@@ -329,16 +805,14 @@
     out_shard = rows_of(w_out, rows_d)
     ff_shard = jnp.concatenate([rows_of(w_gate, rows_d), rows_of(w_up, rows_d)], axis=1)
     down_shard = rows_of(w_down, rows_ff)
-    vec_shard = rows_of(vectors, 1)
-    w_in, w_kv, w_output, w_ff, w_dn, vecs = gather(
-        (in_shard, kv_shard, out_shard, ff_shard, down_shard, vec_shard)
-    )
+    vec_shard = jnp.broadcast_to(lax.reduce_precision(vectors, 8, 7).reshape(1, -1), (8, vec_size))
+    own = by_kernel(rows_all, ring_size, fsdp_size)
+    comm = (ring_size, fsdp_size // 2)
+    early, late = (in_shard, kv_shard, vec_shard), (out_shard, ff_shard, down_shard)
+    w_in, w_kv, vecs = gather(early, *comm, 0) if own else gather_plain(early)
     w_in = w_in.reshape(D, 3 * WIDTH + latents)
     w_kv = w_kv.reshape(GROUPS, LATENT, 2 * per_group)
-    w_output = w_output.reshape(WIDTH, D)
-    w_ff = w_ff.reshape(D, 2 * FF)
-    w_dn = w_dn.reshape(FF, D)
-    vecs = vecs.reshape(-1).astype(F32)
+    vecs = vecs[:, 0].reshape(-1)
     gain_in, gain_mid = vecs[:D], vecs[D : 2 * D]
     decay_bias, out_gain = vecs[2 * D : 2 * D + WIDTH], vecs[2 * D + WIDTH :]
 
@@ -356,18 +830,15 @@
     inputs = hidden_in.astype(F32)
     factor_in = rms_factor(inputs, 1e-5)
     normed = (inputs * factor_in * gain_in).astype(BF)
-    query = mm(normed, w_in[:, :WIDTH])
-    decay_in = mm(normed, w_in[:, WIDTH : 2 * WIDTH]) + decay_bias
-    gate_in = mm(normed, w_in[:, 2 * WIDTH : 3 * WIDTH])
     latent = mm(normed, w_in[:, 3 * WIDTH :]).astype(BF)
-    keys = jnp.concatenate(
-        [mm(latent[:, g * LATENT : (g + 1) * LATENT], w_kv[g, :, :per_group]) for g in range(GROUPS)], axis=1
+    bias_row, gain_row = decay_bias.reshape(1, WIDTH), out_gain.reshape(1, WIDTH)
+    query, keys, values, decay_in, gate_in, mixed, heads, states, *rest = mixer_fwd(
+        normed, latent, w_in, w_kv, bias_row, gain_row, cols, segs, late if own else (), comm + (0, 2) if own else None
     )
-    values = jnp.concatenate(
-        [mm(latent[:, g * LATENT : (g + 1) * LATENT], w_kv[g, :, per_group:]) for g in range(GROUPS)], axis=1
-    )
-    gain_row = out_gain.reshape(1, WIDTH)
-    mixed, heads, states = mixer_fwd(query, keys, values, decay_in, gate_in, gain_row, cols, segs)
+    w_output, w_ff, w_dn = rest if own else gather_plain(late)
+    w_output = w_output.reshape(WIDTH, D)
+    w_ff = w_ff.reshape(D, 2 * FF)
+    w_dn = w_dn.reshape(FF, D)
     middle = inputs + mm(mixed, w_output)
     factor_mid = rms_factor(middle, 1e-5)
     normed_mid = (middle * factor_mid * gain_mid).astype(BF)
@@ -391,11 +862,13 @@
     d_middle = d_middle + d_outf
     d_branch = d_middle.astype(BF)
     grad_out = mm_tn(mixed, d_branch)
-    d_mixed = mm_nt(d_branch, w_output)
-
-    d_query, d_keys, d_values, d_decay, d_gatein, d_bias, d_out_gain = mixer_bwd(
-        query, keys, values, decay_in, gate_in, gain_row, cols, segs, heads, states, d_mixed
+
+    sent = (grad_ff.astype(BF).reshape(count, rows_d, -1), grad_down.astype(BF).reshape(count, rows_ff, -1))
+    saved = (query, keys, values, decay_in, gate_in, gain_row, cols, segs, heads, states)
+    d_query, d_keys, d_values, d_decay, d_gatein, d_bias, d_out_gain, *rest = mixer_bwd(
+        saved, d_branch, w_output, sent if own else (), comm + (0, 3) if own else None
     )
+    own_ff, own_down = rest if own else scatter_plain(sent)
     grad_kv, d_latent = [], []
     for g in range(GROUPS):
         d_kv = jnp.concatenate(
@@ -412,16 +885,14 @@
     grad_input = d_middle + d_inputs
     grad_vec = jnp.concatenate([d_gain_in, d_gain_mid, d_bias.reshape(-1), d_out_gain.reshape(-1)])
 
-    own_in, own_kv, own_out, own_ff, own_down, own_vec = scatter(
-        (
-            grad_in.reshape(count, rows_d, -1),
-            grad_kv.reshape(count, rows_kv, -1),
-            grad_out.reshape(count, rows_d, -1),
-            grad_ff.reshape(count, rows_d, -1),
-            grad_down.reshape(count, rows_ff, -1),
-            grad_vec.reshape(count, 1, -1),
-        )
+    grad_vec = jnp.broadcast_to(grad_vec.reshape(count, 1, vec_size), (count, 8, vec_size))
+    sent = (
+        grad_in.astype(BF).reshape(count, rows_d, -1),
+        grad_kv.astype(BF).reshape(count, rows_kv, -1),
+        grad_out.astype(BF).reshape(count, rows_d, -1),
+        grad_vec,
     )
+    own_in, own_kv, own_out, own_vec = scatter(sent, *comm, 1) if own else scatter_plain(sent)
     return (
         block_out,
         grad_input,
@@ -435,15 +906,15 @@
         own_ff[:, :FF].reshape(-1),
         own_ff[:, FF:].reshape(-1),
         own_down.reshape(-1),
-        own_vec.reshape(-1),
+        own_vec[0],
     )
 
 
 def solution(mesh):
-    count = mesh.shape["dp"] * mesh.shape["fsdp"]
+    sizes = {"ring_size": mesh.shape["dp"], "fsdp_size": mesh.shape["fsdp"]}
     rows, flat = P(AXES, None), P(AXES)
     in_specs = (rows,) + (flat,) * 13 + (rows,)
     out_specs = (rows, rows) + (flat,) * 11
     return jax.shard_map(
-        partial(per_device, count=count), mesh=mesh, in_specs=in_specs, out_specs=out_specs, check_vma=False
+        partial(per_device, **sizes), mesh=mesh, in_specs=in_specs, out_specs=out_specs, check_vma=False
     )

time: 1360 us -> 536 us (0.39)
  waiting for transfers between devices: 926 us -> 0 us
  Pallas kernels: 77.3 us -> 327 us
  blocking collectives: 83 us -> 0 us
  matrix products: 181 us -> 135 us
    reduce_scatter x5 -> x0, waiting for transfers between devices: 723 us -> none  [scatter(): lax.psum_scatter(piece, AXES, scatter_dimension=0)]
    pallas_call x2 -> x4, Pallas kernels: 77.3 us -> 327 us  [the longest x1 106 us: mixer_fwd(): pl.pallas_call(partial(mixer_fwd_kernel, comm), grid=(BANDS,), in_specs=i...]
    all_gather x5 -> x0, waiting for transfers between devices: 202 us -> none  [gather(): return [lax.all_gather(piece, AXES, axis=0) for piece in shards]]
    all_gather x1 -> x0, blocking collectives: 43.6 us -> none  [gather(): return [lax.all_gather(piece, AXES, axis=0) for piece in shards]]
    unnamed x1 -> x0, blocking collectives: 39.4 us -> none
    dot_general x12 -> x5, matrix products: 76.6 us -> 51.4 us  [mm(): lax.dot_general(left, right, (((1,), (0,)), ((), ())), preferred_element_...]
    unnamed x82 -> x88, local copies, waits for them, and re-layouts: 33.8 us -> 18.8 us
    dot_general x6 -> x5, matrix products: 52.1 us -> 40.6 us  [mm_nt(): lax.dot_general(left, right, (((1,), (1,)), ((), ())), preferred_element_...]
  transfers between devices with their start and end apart: 10 -> 0, of which waited for: 9 -> 0; matrix products, arithmetic and copies ran while one was open for 13% -> 0% of each run, Pallas kernels for 2% -> 0%
where the time goes in v3:
time: 536 us; the launch traced here: 525 us
  Pallas kernels  327 us (61%)
  matrix products  135 us (25%)
  local copies, waits for them, and re-layouts  38.5 us (7%)
  other arithmetic  23.1 us (4%)
    pallas_call x1, Pallas kernels, mixer_fwd(): pl.pallas_call(partial(mixer_fwd_kernel, comm), grid=(BANDS,), in_specs=i...  106 us
    pallas_call x1, Pallas kernels, mixer_bwd(): pl.pallas_call(partial(mixer_bwd_kernel, comm), grid=(BANDS,), in_specs=i...  102 us
    pallas_call x1, Pallas kernels, scatter(): pl.pallas_call(partial(scatter_kernel, ring_size, line_size, kinds), in_s...  64.6 us
    pallas_call x1, Pallas kernels, gather(): pl.pallas_call(partial(gather_kernel, ring_size, line_size, kinds), in_sp...  54.7 us
    dot_general x5, matrix products, mm(): lax.dot_general(left, right, (((1,), (0,)), ((), ())), preferred_element_...  51.4 us
    dot_general x6, matrix products, mm_tn(): lax.dot_general(left, right, (((0,), (0,)), ((), ())), preferred_element_...  43.3 us
    dot_general x5, matrix products, mm_nt(): lax.dot_general(left, right, (((1,), (1,)), ((), ())), preferred_element_...  40.6 us
    unnamed x88, local copies, waits for them, and re-layouts  18.8 us

profile of v3, /device:TPU:0, one launch (start us, length us, event | category | flops | bytes accessed | tf_op | source)
XLA Modules:
  0.0 525.3 jit_solution(3069399107784404385)
XLA Ops:
  0.7 0.7 reduce_precision.3
  1.4 0.9 slice_reduce_fusion
  2.3 0.9 slice_reduce_fusion.1
  3.8 0.7 convert_element_type.116
  4.5 0.7 convert_element_type.111
  5.2 2.1 fusion.16
  7.3 0.8 fusion.35
  8.1 0.8 convert_element_type.107
  8.9 0.8 convert_element_type.108
  10.3 0.8 convert_element_type.106
  11.2 0.9 convert_element_type.103
  12.1 0.9 convert_element_type.104
  13.1 0.9 convert_element_type.105
  14.0 0.7 pad_maximum_fusion.23.refs_0_
  14.7 0.9 convert_element_type.117
  16.4 1.0 copy.39
  17.4 1.0 copy.40
  18.4 1.0 copy.38
  19.4 1.0 copy.41
  20.5 0.8 broadcast_in_dim.9
  21.3 2.0 concatenate.49.refs_9_.refs_6_
  23.4 54.7 %gather_shards.1 = (bf16[32,32,3584]{2,1,0:T(8,128)(2,1)}, bf16[32,16,1024]{2,1,0:T(8,128)(2,1)}, f32[32,8,128]{2,1,0:T(8,128)}) custom-call(bf16[32,3584]{1,0:T(8,128)(2,1)} %pad_maximum_fusion.23.refs_0_, bf16[16,1024]{1,0:T(8,128)(2,1)} %pad_maximum_fusion.24.refs_1_, f32[8,128]{1,0:T(8,128)} %broadcast_in_dim.8.refs_2_), custom_call_target="tpu_custom_call" | custom-call | tf_op jit(solution)/shard_map/gather_shards/pallas_call | solution.py:732
  78.1 0.8 fusion.47
  78.9 2.3 fusion.45
  81.8 4.2 convolution_convert_fusion.4.refs_1_
  86.0 106.0 %mixer_fwd.1 = (f32[1024,1024]{1,0:T(8,128)}, f32[1024,1024]{1,0:T(8,128)}, f32[1024,1024]{1,0:T(8,128)}, f32[1024,1024]{1,0:T(8,128)}, f32[1024,1024]{1,0:T(8,1...) custom-call(bf16[1024,1024]{1,0:T(8,128)(2,1)} %copy-done.7, ...), custom_call_target="tpu_custom_call" | custom-call | tf_op jit(solution)/shard_map/mixer_fwd/pallas_call | solution.py:296
  192.0 4.9 multiply_reduce_fusion.2
  196.9 2.0 copy-done.5
  199.3 1.3 copy-done.14
  200.7 9.0 %fusion.6 = f32[1024,2816]{1,0:T(8,128)} fusion(bf16[1024,1024]{1,0:T(8,128)(2,1)S(1)} %multiply_convert_fusion.3, bf16[1024,5632]{1,0:T(8,128)(2,1)S(1)} %bitcast.131), kind=kOutput, calls=%fused_computation.16 | convolution fusion | flops 5905580032 | bytes 19398656 | tf_op jit(solution)/shard_map/dot_general | solution.py:31
  209.7 9.1 %fusion.30 = f32[1024,2816]{1,0:T(8,128)} fusion(bf16[2816,1024]{1,0:T(8,128)(2,1)S(1)} %bitcast.135, bf16[1024,1024]{1,0:T(8,128)(2,1)S(1)} %copy-done.10, f32[1024]{0:T(1024)S(1)} %convert_element_type.116), kind=kOutput, calls=%fused_computation.52 | convolution fusion | flops 5908725760 | bytes 19402752 | tf_op jit(solution)/shard_map/dot_general | solution.py:35
  218.8 21.9 %multiply_convert_fusion.1 = (bf16[1024,2816]{1,0:T(8,128)(2,1)}, bf16[1024,2816]{1,0:T(8,128)(2,1)}, bf16[1024,2816]{1,0:T(8,128)(2,1)}) fusion(f32[1024,2816]{1,0:T(8,128)} %fusion.30, f32[1024,2816]{1,0:T(8,128)} %fusion.6, bf16[1024,1024]{1,0:T(8,128)(2,1)} %copy-done.14, bf16[1024,5632]{1,0:T(8,128)(2,1)} %bitcast.127), kind=kOutput, calls=%fused_computation.2 | convolution fusion | flops 5948833792 | bytes 48234496 | tf_op jit(solution)/shard_map/dot_general | solution.py:31
  240.7 11.4 %add_convert_fusion = bf16[1024,1024]{1,0:T(8,128)(2,1)} fusion(f32[1024,1024]{1,0:T(8,128)} %copy-done.5, bf16[1024,2816]{1,0:T(8,128)(2,1)} %get-tuple-element.75, bf16[2816,1024]{1,0:T(8,128)(2,1)} %bitcast.132), kind=kOutput, calls=%fused_computation.33 | convolution fusion | flops 5907677184 | bytes 17825792 | tf_op jit(solution)/shard_map/dot_general | solution.py:31
  252.1 22.0 %multiply_reduce_fusion = (f32[1024]{0:T(1024)S(1)}, f32[1024]{0:T(1024)S(1)}, f32[1024,1024]{1,0:T(8,128)}) fusion(f32[1024,1024]{1,0:T(8,128)} %copy-done.5, f32[1024]{0:T(1024)S(1)} %add_rsqrt_fusion, f32[1024]{0:T(1024)S(1)} %bitcast.114, bf16[1024,5632]{1,0:T(8,128)(2,1)} %bitcast.128, bf16[1024,2816]{1,0:T(8,128)(2,1)} %get-tuple-element.74, ...), kind=kOutput, calls=%fused_computation.28 | convolution fusion | flops 11840518144 | bytes 31473664 | tf_op jit(solution)/shard_map/dot_general | solution.py:35
  274.1 19.5 %convolution_convert_fusion = bf16[1024,5632]{1,0:T(8,128)(2,1)} fusion(bf16[1024,1024]{1,0:T(8,128)(2,1)} %copy-done.14, bf16[1024,2816]{1,0:T(8,128)(2,1)} %get-tuple-element.74, bf16[1024,2816]{1,0:T(8,128)(2,1)} %get-tuple-element.73), kind=kOutput, calls=%fused_computation.6 | convolution fusion | flops 11839995904 | bytes 25165824 | tf_op jit(solution)/shard_map/dot_general | solution.py:39
  293.6 5.6 %fusion.42 = (bf16[1024,1024]{1,0:T(8,128)(2,1)S(1)}, f32[1024,1024]{1,0:T(8,128)}) fusion(f32[1024]{0:T(1024)S(1)} %convert_element_type.116, bf16[1024,1024]{1,0:T(8,128)(2,1)S(1)} %copy-done.10, f32[1024]{0:T(1024)S(1)} %broadcast_multiply_fusion.1, f32[1024,1024]{1,0:T(8,128)} %copy-done.5, f32[1024,1024]{1,0:T(8,128)} %get-tuple-element.97, ...), kind=kLoop, calls=%fused_computation.88 | loop fusion | flops 9437184 | bytes 16793600 | tf_op jit(solution)/shard_map/convert_element_type | solution.py:863
  299.3 1.0 copy-done.29
  300.3 8.5 %convolution_convert_fusion.2 = bf16[2816,1024]{1,0:T(8,128)(2,1)} fusion(bf16[1024,2816]{1,0:T(8,128)(2,1)S(1)} %copy-done.29, bf16[1024,1024]{1,0:T(8,128)(2,1)S(1)} %copy-done.10, f32[1024]{0:T(1024)S(1)} %convert_element_type.116), kind=kOutput, calls=%fused_computation.20 | convolution fusion | flops 5911609344 | bytes 13635584 | tf_op jit(solution)/shard_map/dot_general | solution.py:39
  308.7 3.8 convolution_convert_fusion.3
  312.5 101.5 %mixer_bwd.1 = (bf16[1024,1024]{1,0:T(8,128)(2,1)}, bf16[1024,1024]{1,0:T(8,128)(2,1)}, bf16[1024,1024]{1,0:T(8,128)(2,1)}, bf16[1024,1024]{1,0:T(8,128)(2,1)}, ...) custom-call(f32[1024,1024]{1,0:T(8,128)} %get-tuple-element.47.refs_, ...), custom_call_target="tpu_custom_call" | custom-call | tf_op jit(solution)/shard_map/mixer_bwd/pallas_call | solution.py:325
  414.0 1.9 copy.55
  415.9 1.1 fusion.46
  417.1 0.8 reshape.236
  417.8 0.8 reshape.235
  418.6 2.0 fusion.43
  420.6 0.7 fusion.25
  421.3 0.7 fusion.23
  422.1 1.1 pad_maximum_fusion.21
  423.3 0.9 copy-done.12
  425.4 0.7 fusion.27
  426.2 0.7 fusion.26
  427.2 1.0 slice-done.1
  428.3 0.7 copy-done.4
  429.0 8.1 %fusion.15 = (f32[1024]{0:T(1024)S(1)}, f32[1024]{0:T(1024)S(1)}, f32[1024,1024]{1,0:T(8,128)S(1)}) fusion(bf16[1024,1024]{1,0:T(8,128)(2,1)S(1)} %copy-done.4, f32[1024]{0:T(1024)S(1)} %copy-done.23, f32[1024]{0:T(1024)S(1)} %bitcast.117, bf16[1024,3584]{1,0:T(8,128)(2,1)S(1)} %fusion.26, bf16[1024,3584]{1,0:T(8,128)(2,1)S(1)} %bitcast.90), kind=kOutput, calls=%fused_computation.26 | convolution fusion | flops 7523530752 | bytes 20987904 | tf_op jit(solution)/shard_map/dot_general | solution.py:35
  437.1 10.1 %convolution_convert_fusion.1 = bf16[1024,3584]{1,0:T(8,128)(2,1)} fusion(bf16[1024,1024]{1,0:T(8,128)(2,1)S(1)} %copy-done.8, bf16[1024,3584]{1,0:T(8,128)(2,1)S(1)} %fusion.26), kind=kOutput, calls=%fused_computation.7 | convolution fusion | flops 7519862784 | bytes 16777216 | tf_op jit(solution)/shard_map/dot_general | solution.py:39
  447.2 3.0 fusion.14
  450.9 64.6 %scatter_sums.1 = (f32[32,3584]{1,0:T(8,128)}, f32[16,1024]{1,0:T(8,128)}, f32[32,1024]{1,0:T(8,128)}, f32[8,128]{1,0:T(8,128)}) custom-call(bf16[32,32,3584]{2,1,0:T(8,128)(2,1)} %bitcast.94, bf16[32,16,1024]{2,1,0:T(8,128)(2,1)} %bitcast.96, bf16[32,32,1024]{2,1,0:T(8,128)(2,1)} %bitcast.97, f32[32,8,128]{2,1,0:T(8,128)} %broadcast_in_dim.11.refs_3_), custom_call_target="tpu_custom_call" | custom-call | tf_op jit(solution)/shard_map/scatter_sums/pallas_call | solution.py:550
  515.4 1.6 copy.54
  517.0 0.8 slice_bitcast_fusion.4
  518.4 1.2 slice_bitcast_fusion.8
  520.2 0.8 slice_bitcast_fusion.3
  521.1 1.1 slice_bitcast_fusion
  522.1 0.7 copy.53
  523.5 0.7 copy.52
  (103 shorter events, 8.2 us)
Async XLA Ops:
  0.6 15.6 %copy-start.21 = (f32[90112]{0:T(1024)S(1)}, f32[90112]{0:T(1024)}, u32[]{:S(2)}) copy-start(f32[90112]{0:T(1024)} %param.25) | copy-start | bytes 1081348
  0.7 15.3 %copy-start.20 = (f32[90112]{0:T(1024)S(1)}, f32[90112]{0:T(1024)}, u32[]{:S(2)}) copy-start(f32[90112]{0:T(1024)} %param.24) | copy-start | bytes 1081348
  0.7 15.0 %copy-start.19 = (f32[90112]{0:T(1024)S(1)}, f32[90112]{0:T(1024)}, u32[]{:S(2)}) copy-start(f32[90112]{0:T(1024)} %param.23) | copy-start | bytes 1081348
  5.2 80.7 %copy-start.1 = (f32[1024]{0:T(1024)}, f32[1024]{0:T(1024)S(1)}, u32[]{:S(2)}) copy-start(f32[1024]{0:T(1024)S(1)} %convert_element_type.111) | copy-start | bytes 12292
  7.3 73.9 %copy-start.22 = (f32[1024]{0:T(1024)}, f32[1024]{0:T(1024)S(1)}, u32[]{:S(2)}) copy-start(f32[1024]{0:T(1024)S(1)} %add_rsqrt_fusion.1) | copy-start | bytes 12292
  16.4 64.9 %copy-start.3 = (bf16[1024,1024]{1,0:T(8,128)(2,1)S(1)}, bf16[1024,1024]{1,0:T(8,128)(2,1)}, u32[]{:S(2)}) copy-start(bf16[1024,1024]{1,0:T(8,128)(2,1)} %param.15) | copy-start | bytes 6291460
  23.4 62.6 %copy-start = (f32[1024,128]{1,0:T(8,128)}, f32[1024,128]{1,0:T(8,128)S(1)}, u32[]{:S(2)}) copy-start(f32[1024,128]{1,0:T(8,128)S(1)} %concatenate.49.refs_9_.refs_6_) | copy-start | bytes 1572868
  78.9 7.1 %copy-start.2 = (f32[1,1024]{1,0:T(1,128)}, f32[1,1024]{1,0:T(1,128)S(1)}, u32[]{:S(2)}) copy-start(f32[1,1024]{1,0:T(1,128)S(1)} %get-tuple-element.88.refs_8_.refs_5_) | copy-start | bytes 12292
  78.9 7.1 %copy-start.24 = (f32[8,1,128]{2,1,0:T(1,128)}, f32[8,1,128]{2,1,0:T(1,128)S(1)}, u32[]{:S(2)}) copy-start(f32[8,1,128]{2,1,0:T(1,128)S(1)} %get-tuple-element.90) | copy-start | bytes 12292
  81.8 4.2 copy-start.7
  192.0 8.7 %slice-start.2 = ((s8[11534336]{0:T(1024)(128)(4,1)}), s8[4194304]{0:T(1024)(128)(4,1)S(1)}, s32[]{:S(2)}) async-start(s8[11534336]{0:T(1024)(128)(4,1)} %bitcast.129), calls=%async_computation.2 | async-start | bytes 8388608
  192.0 8.7 %slice-start.3 = ((s8[11534336]{0:T(1024)(128)(4,1)}), s8[4194304]{0:T(1024)(128)(4,1)S(1)}, s32[]{:S(2)}) async-start(s8[11534336]{0:T(1024)(128)(4,1)} %bitcast.129), calls=%async_computation.3 | async-start | bytes 8388608
  192.0 8.7 %slice-start.4 = ((s8[11534336]{0:T(1024)(128)(4,1)}), s8[3145728]{0:T(1024)(128)(4,1)S(1)}, s32[]{:S(2)}) async-start(s8[11534336]{0:T(1024)(128)(4,1)} %bitcast.129), calls=%async_computation.4 | async-start | bytes 6291456
  196.9 2.0 copy-start.5
  198.9 10.8 %slice-start.5 = ((s8[5767168]{0:T(1024)(128)(4,1)}), s8[4194304]{0:T(1024)(128)(4,1)S(1)}, s32[]{:S(2)}) async-start(s8[5767168]{0:T(1024)(128)(4,1)} %bitcast.133), calls=%async_computation.5 | async-start | bytes 8388608
  199.3 1.3 copy-start.14
  200.6 9.1 %copy-start.10 = (bf16[1024,1024]{1,0:T(8,128)(2,1)S(1)}, bf16[1024,1024]{1,0:T(8,128)(2,1)}, u32[]{:S(2)}) copy-start(bf16[1024,1024]{1,0:T(8,128)(2,1)} %param.29) | copy-start | bytes 6291460
  200.7 9.1 %slice-start.6 = ((s8[5767168]{0:T(1024)(128)(4,1)}), s8[1572864]{0:T(1024)(128)(4,1)S(1)}, s32[]{:S(2)}) async-start(s8[5767168]{0:T(1024)(128)(4,1)} %bitcast.133), calls=%async_computation.6 | async-start | bytes 3145728
  293.6 6.6 %copy-start.29 = (bf16[1024,2816]{1,0:T(8,128)(2,1)S(1)}, bf16[1024,2816]{1,0:T(8,128)(2,1)}, u32[]{:S(2)}) copy-start(bf16[1024,2816]{1,0:T(8,128)(2,1)} %get-tuple-element.75) | copy-start | bytes 17301508
  300.2 8.5 %copy-start.9 = (bf16[1024,1024]{1,0:T(8,128)(2,1)}, bf16[1024,1024]{1,0:T(8,128)(2,1)S(1)}, u32[]{:S(2)}) copy-start(bf16[1024,1024]{1,0:T(8,128)(2,1)S(1)} %get-tuple-element.71.refs_10_) | copy-start | bytes 6291460
  300.3 8.5 %copy-start.28 = (bf16[1024,1024]{1,0:T(8,128)(2,1)S(1)}, bf16[1024,1024]{1,0:T(8,128)(2,1)}, u32[]{:S(2)}) copy-start(bf16[1024,1024]{1,0:T(8,128)(2,1)} %get-tuple-element.43) | copy-start | bytes 6291460
  414.0 4.6 copy-start.15
  418.6 2.0 copy-start.16
  421.3 1.8 copy-start.13
  422.1 2.1 copy-start.12
  423.1 1.7 copy-start.11
  424.2 1.2 copy-start.18
  424.9 1.3 copy-start.17
  424.9 2.4 slice-start
  425.4 2.9 slice-start.1
  426.1 2.8 copy-start.4
  426.2 2.8 copy-start.23
  426.2 2.8 copy-start.25
  429.0 8.1 %copy-start.8 = (bf16[1024,1024]{1,0:T(8,128)(2,1)S(1)}, bf16[1024,1024]{1,0:T(8,128)(2,1)}, u32[]{:S(2)}) copy-start(bf16[1024,1024]{1,0:T(8,128)(2,1)} %copy-done.7) | copy-start | bytes 6291460
  437.1 10.1 %copy-start.26 = (f32[1,1024]{1,0:T(1,128)S(1)}, f32[1,1024]{1,0:T(1,128)}, u32[]{:S(2)}) copy-start(f32[1,1024]{1,0:T(1,128)} %get-tuple-element.59) | copy-start | bytes 12292
  437.1 10.1 %copy-start.27 = (f32[1,1024]{1,0:T(1,128)S(1)}, f32[1,1024]{1,0:T(1,128)}, u32[]{:S(2)}) copy-start(f32[1,1024]{1,0:T(1,128)} %get-tuple-element.60) | copy-start | bytes 12292
  437.1 10.1 %copy-start.6 = (f32[1024,1024]{1,0:T(8,128)S(1)}, f32[1024,1024]{1,0:T(8,128)}, u32[]{:S(2)}) copy-start(f32[1024,1024]{1,0:T(8,128)} %get-tuple-element.72) | copy-start | bytes 12582916

commit v4 on v3

--- a/solution.py
+++ b/solution.py
@@ -93,16 +93,22 @@
     return up, down, half, small
 
 
-def flags(cols_ref, seg_ref, rows, index):
-    cols = cols_ref[rows, :]
-    seg_col, fresh, to_end, pad = cols[:, 0:1], cols[:, 1:2], cols[:, 2:3], cols[:, 3:4]
-    allowed = (seg_col == seg_ref[index]) & triangle(True)
-    return fresh, to_end, pad, allowed, fresh[SPAN - 1 : SPAN]
+def flags(seg_ref, pad_ref, index):
+    seg_row = seg_ref[index]
+    seg_square = jnp.transpose(jnp.broadcast_to(seg_row, (SPAN, SPAN)))
+    pad = jnp.transpose(jnp.broadcast_to(pad_ref[index], (SPAN, SPAN)))[:, 0:1]
+    seg_col, ending = seg_square[:, 0:1], seg_row[:, SPAN - 1 :]
+    before = seg_ref[jnp.maximum(index - 1, 0)][:, SPAN - 1 :]
+    fresh = (seg_col == before).astype(F32)
+    to_end = (seg_col == ending).astype(F32)
+    keep = (ending == before).astype(F32)
+    allowed = (seg_square == seg_row) & triangle(True)
+    return fresh, to_end, pad, allowed, keep
 
 
 def mixer_fwd_kernel(comm, *refs):
     kinds = comm[2] if comm else 0
-    normed_ref, latent_ref, wq_ref, wd_ref, wg_ref, wk_ref, wv_ref, bias_ref, gain_ref, cols_ref, seg_ref = refs[:11]
+    normed_ref, latent_ref, wq_ref, wd_ref, wg_ref, wk_ref, wv_ref, bias_ref, gain_ref, seg_ref, pad_ref = refs[:11]
     shards, refs = refs[11 : 11 + kinds], refs[11 + kinds :]
     q_ref, k_ref, v_ref, decay_ref, gate_ref, mixed_ref, heads_ref, states_ref = refs[:8]
     gathered, state, sems = refs[8 : 8 + kinds], refs[8 + kinds], refs[9 + kinds :]
@@ -127,7 +133,7 @@
     def chunk(index, carry):
         spread(stages, band * (CHUNKS + 1) + index, ticks)
         rows = pl.ds(pl.multiple_of(index * SPAN, SPAN), SPAN)
-        fresh, to_end, pad, allowed, keep = flags(cols_ref, seg_ref, rows, index)
+        fresh, to_end, pad, allowed, keep = flags(seg_ref, pad_ref, index)
         up, down, half, _ = decays(decay_ref[rows, :], pad, lower_ones)
         query = q_ref[rows, :] * (HEAD_DIM**-0.5) * up
         key = k_ref[rows, :] * pad * down
@@ -158,7 +164,7 @@
 
 def mixer_bwd_kernel(comm, *refs):
     kinds = comm[2] if comm else 0
-    q_ref, k_ref, v_ref, decay_ref, gate_ref, gain_ref, cols_ref, seg_ref, heads_ref, states_ref = refs[:10]
+    q_ref, k_ref, v_ref, decay_ref, gate_ref, gain_ref, seg_ref, pad_ref, heads_ref, states_ref = refs[:10]
     dbranch_ref, wo_ref = refs[10:12]
     grads, refs = refs[12 : 12 + kinds], refs[12 + kinds :]
     dq_ref, dk_ref, dv_ref, ddecay_ref, dgate_ref, dbias_ref, dgain_ref = refs[:7]
@@ -184,7 +190,7 @@
         spread(stages, band * (CHUNKS + 1) + step, ticks)
         index = CHUNKS - 1 - step
         rows = pl.ds(pl.multiple_of(index * SPAN, SPAN), SPAN)
-        fresh, to_end, pad, allowed, keep = flags(cols_ref, seg_ref, rows, index)
+        fresh, to_end, pad, allowed, keep = flags(seg_ref, pad_ref, index)
         heads = heads_ref[rows, :]
         scale = lax.rsqrt(exact_right(heads * heads, diag_ones) * (1.0 / HEAD_DIM) + 1e-2)
         normed = heads * scale
@@ -253,18 +259,17 @@
 def band_specs():
     tokens = pl.BlockSpec((LEN, LANES), lambda band: (0, band))
     vector = pl.BlockSpec((1, LANES), lambda band: (0, band))
-    cols = pl.BlockSpec((LEN, 128), lambda band: (0, 0))
     segs = pl.BlockSpec((CHUNKS, 1, SPAN), lambda band: (0, 0, 0))
     states = pl.BlockSpec((1, CHUNKS, LANES, LANES), lambda band: (band, 0, 0, 0))
-    return tokens, vector, cols, segs, states
+    return tokens, vector, segs, states
 
 
 def fixed(shape):
     return pl.BlockSpec(shape, lambda band: (0,) * len(shape), pipeline_mode=pl.Buffered(1))
 
 
-def mixer_fwd(normed, latent, w_in, w_kv, bias, gain, cols, segs, shards, comm):
-    tokens, vector, cols_spec, segs_spec, states = band_specs()
+def mixer_fwd(normed, latent, w_in, w_kv, bias, gain, segs, pads, shards, comm):
+    tokens, vector, segs_spec, states = band_specs()
     kinds = len(shards)
     half_bands = BANDS // GROUPS
     in_specs = [fixed((LEN, D)), pl.BlockSpec((LEN, LATENT), lambda band: (0, band // half_bands))]
@@ -277,7 +282,7 @@
                 lambda band, part=part: (band // half_bands, 0, part * half_bands + band % half_bands),
             )
         )
-    in_specs += [vector, vector, cols_spec, segs_spec]
+    in_specs += [vector, vector, segs_spec, segs_spec]
     wide = jax.ShapeDtypeStruct((LEN, WIDTH), F32)
     out_shape = [wide] * 5 + [
         jax.ShapeDtypeStruct((LEN, WIDTH), BF),
@@ -302,15 +307,15 @@
         scratch_shapes=scratch,
         compiler_params=pltpu.CompilerParams(vmem_limit_bytes=52 << 20, **params),
         name="mixer_fwd",
-    )(normed, latent, w_in, w_in, w_in, w_kv, w_kv, bias, gain, cols, segs, *shards)
+    )(normed, latent, w_in, w_in, w_in, w_kv, w_kv, bias, gain, segs, pads, *shards)
 
 
 def mixer_bwd(saved, d_branch, w_output, grads, comm):
-    tokens, vector, cols_spec, segs_spec, states = band_specs()
+    tokens, vector, segs_spec, states = band_specs()
     kinds = len(grads)
     low = jax.ShapeDtypeStruct((LEN, WIDTH), BF)
     sums = jax.ShapeDtypeStruct((1, WIDTH), F32)
-    in_specs = [tokens] * 5 + [vector, cols_spec, segs_spec, tokens, states]
+    in_specs = [tokens] * 5 + [vector, segs_spec, segs_spec, tokens, states]
     in_specs += [fixed((LEN, D)), pl.BlockSpec((LANES, D), lambda band: (band, 0))]
     out_specs, out_shape = [tokens] * 5 + [vector, vector], [low] * 5 + [sums, sums]
     scratch = [pltpu.VMEM((LANES, LANES), F32), pltpu.VMEM((LEN, LANES), F32)]
@@ -601,22 +606,36 @@
     def own(self, a):
         return pltpu.make_async_copy(self.shards[a], self.outs[a].at[self.mine], self.own_sem.at[a])
 
-    def to_line(self, a, i):
+    def along(self, a, i, up):
         me = self.me
+        here = self.spot(a, 0, i, me.core)
         return send(
-            self.shards[a],
-            self.outs[a].at[self.mine],
-            self.zsend.at[a, i],
-            self.zrecv.at[a, me.z],
-            me.device(me.d, self.order[i], me.core),
+            self.shards[a] if i == 0 else here,
+            here,
+            self.zsend.at[a, up, i],
+            self.zrecv.at[a, self.order[i]],
+            me.device(me.d, me.z + 2 * up - 1, me.core),
         )
 
     def from_line(self, a, i):
         me = self.me
         here = self.spot(a, 0, i, me.core)
         return send(
-            here, here, self.zsend.at[a, i], self.zrecv.at[a, self.order[i]], me.device(me.d, self.order[i], me.core)
-        )
+            here, here, self.zsend.at[a, 0, i], self.zrecv.at[a, self.order[i]], me.device(me.d, self.order[i], me.core)
+        )
+
+    def pass_on(self, act, i):
+        me, last = self.me, self.line_size - 1
+        upward, downward = me.z < last, me.z > 0
+        if i:
+            upward &= self.order[i] < me.z
+            downward &= self.order[i] > me.z
+        for up, wanted in ((1, upward), (0, downward)):
+
+            @pl.when(wanted)
+            def _(up=up):
+                for a in self.every:
+                    act(self.along(a, i, up))
 
     def to_ring(self, a, i, way):
         here = self.spot(a, 0, i, self.me.core)
@@ -651,8 +670,7 @@
         for a in self.every:
             for way in range(2):
                 self.to_ring(a, 0, way).start()
-            for i in range(1, self.line_size):
-                self.to_line(a, i).start()
+        self.pass_on(lambda copy: copy.start(), 0)
         for a in self.every:
             self.to_pair(a, 0, 0, self.me.core).start()
 
@@ -661,6 +679,8 @@
             self.from_line(a, i).wait_recv()
             for way in range(2):
                 self.to_ring(a, i, way).start()
+        self.pass_on(lambda copy: copy.start(), i)
+        for a in self.every:
             self.to_pair(a, i, 0, self.me.core).start()
 
     def ring_stage(self, i):
@@ -703,15 +723,15 @@
                         self.to_pair_half(a, i, way, 1 - core).wait_recv()
                         self.to_pair_half(a, i, way, core).wait_send()
                         self.onward(a, i, way).wait_send()
-                if i:
-                    self.to_line(a, i).wait_send()
+        for i in range(self.line_size):
+            self.pass_on(lambda copy: copy.wait_send(), i)
 
 
 def gather_scratch(kinds, line_size):
     sems = pltpu.SemaphoreType.DMA
     return (
         [sems((kinds,))]
-        + [sems((kinds, line_size))] * 2
+        + [sems((kinds, 2, line_size)), sems((kinds, line_size))]
         + [sems((kinds, 2, line_size))] * 4
         + [sems((kinds, 3, line_size))] * 2
         + [sems((kinds, 2, line_size))] * 2
@@ -743,6 +763,50 @@
 def spread(stages, tick, ticks):
     for number, stage in enumerate(stages):
         pl.when(tick == number * ticks // len(stages))(stage)
+
+
+def pack_kernel(places, *refs):
+    flats, packed = refs[: len(places) + 1], refs[len(places) + 1 :]
+    for flat, (target, offset, tiles) in zip(flats, places):
+        out = packed[target]
+        rows = out.shape[0]
+        for j in range(tiles):
+            out[:, offset + j * 128 : offset + (j + 1) * 128] = flat[pl.ds(j, rows, stride=tiles), :].astype(BF)
+    packed[-1][...] = jnp.broadcast_to(flats[-1][...].astype(BF).astype(F32), packed[-1].shape)
+
+
+def pack(flats, vectors, places, shapes):
+    vmem = pl.BlockSpec(memory_space=pltpu.VMEM)
+    return pl.pallas_call(
+        partial(pack_kernel, places),
+        in_specs=[vmem] * (len(flats) + 1),
+        out_specs=[vmem] * (len(shapes) + 1),
+        out_shape=[jax.ShapeDtypeStruct(shape, BF) for shape in shapes] + [jax.ShapeDtypeStruct((8, 128), F32)],
+        name="pack_shards",
+    )(*[flat.reshape(-1, 128) for flat in flats], vectors.reshape(1, 128))
+
+
+def unpack_kernel(places, kinds, *refs):
+    packed, flats = refs[: kinds + 1], refs[kinds + 1 :]
+    for flat, (target, offset, tiles) in zip(flats, places):
+        source = packed[target]
+        rows = source.shape[0]
+        for j in range(tiles):
+            flat[pl.ds(j, rows, stride=tiles), :] = source[:, offset + j * 128 : offset + (j + 1) * 128]
+    flats[-1][...] = packed[-1][0:1]
+
+
+def unpack(packed, places):
+    vmem = pl.BlockSpec(memory_space=pltpu.VMEM)
+    sizes = [packed[target].shape[0] * tiles for target, _, tiles in places] + [1]
+    flats = pl.pallas_call(
+        partial(unpack_kernel, places, len(packed) - 1),
+        in_specs=[vmem] * len(packed),
+        out_specs=[vmem] * len(sizes),
+        out_shape=[jax.ShapeDtypeStruct((size, 128), F32) for size in sizes],
+        name="unpack_sums",
+    )(*packed)
+    return [flat.reshape(-1) for flat in flats]
 
 
 def rms_factor(values, eps):
@@ -795,18 +859,43 @@
     rows_all = (rows_d, rows_kv, rows_ff)
     vec_size = (2 * D + 2 * WIDTH) // count
 
-    def rows_of(piece, rows):
-        return piece.astype(BF).reshape(rows, -1)
-
-    in_shard = jnp.concatenate(
-        [rows_of(piece, rows_d) for piece in (w_query, w_decay, w_outgate, w_latent)], axis=1
+    own = by_kernel(rows_all, ring_size, fsdp_size) and vec_size == 128
+    flat_weights = (w_query, w_latent, w_key_up, w_value_up, w_decay, w_outgate, w_out, w_gate, w_up, w_down)
+    wide, half_kv, ff = WIDTH // 128, per_group // 128, FF // 128
+    places = (
+        (0, 0, wide),
+        (0, 3 * WIDTH, latents // 128),
+        (1, 0, half_kv),
+        (1, per_group, half_kv),
+        (0, WIDTH, wide),
+        (0, 2 * WIDTH, wide),
+        (2, 0, D // 128),
+        (3, 0, ff),
+        (3, FF, ff),
+        (4, 0, D // 128),
     )
-    kv_shard = jnp.concatenate([rows_of(w_key_up, rows_kv), rows_of(w_value_up, rows_kv)], axis=1)
-    out_shard = rows_of(w_out, rows_d)
-    ff_shard = jnp.concatenate([rows_of(w_gate, rows_d), rows_of(w_up, rows_d)], axis=1)
-    down_shard = rows_of(w_down, rows_ff)
-    vec_shard = jnp.broadcast_to(lax.reduce_precision(vectors, 8, 7).reshape(1, -1), (8, vec_size))
-    own = by_kernel(rows_all, ring_size, fsdp_size)
+    if own:
+        shapes = (
+            (rows_d, 3 * WIDTH + latents),
+            (rows_kv, 2 * per_group),
+            (rows_d, D),
+            (rows_d, 2 * FF),
+            (rows_ff, D),
+        )
+        in_shard, kv_shard, out_shard, ff_shard, down_shard, vec_shard = pack(flat_weights, vectors, places, shapes)
+    else:
+
+        def rows_of(piece, rows):
+            return piece.astype(BF).reshape(rows, -1)
+
+        in_shard = jnp.concatenate(
+            [rows_of(piece, rows_d) for piece in (w_query, w_decay, w_outgate, w_latent)], axis=1
+        )
+        kv_shard = jnp.concatenate([rows_of(w_key_up, rows_kv), rows_of(w_value_up, rows_kv)], axis=1)
+        out_shard = rows_of(w_out, rows_d)
+        ff_shard = jnp.concatenate([rows_of(w_gate, rows_d), rows_of(w_up, rows_d)], axis=1)
+        down_shard = rows_of(w_down, rows_ff)
+        vec_shard = jnp.broadcast_to(lax.reduce_precision(vectors, 8, 7).reshape(1, -1), (8, vec_size))
     comm = (ring_size, fsdp_size // 2)
     early, late = (in_shard, kv_shard, vec_shard), (out_shard, ff_shard, down_shard)
     w_in, w_kv, vecs = gather(early, *comm, 0) if own else gather_plain(early)
@@ -816,16 +905,9 @@
     gain_in, gain_mid = vecs[:D], vecs[D : 2 * D]
     decay_bias, out_gain = vecs[2 * D : 2 * D + WIDTH], vecs[2 * D + WIDTH :]
 
-    seg = seg_ids.reshape(CHUNKS, SPAN)
-    before = jnp.concatenate([jnp.full((1,), -1, seg.dtype), seg[:-1, -1]])
-    fresh = (seg == before[:, None]).astype(F32).reshape(LEN, 1)
-    to_end = (seg == seg[:, -1:]).astype(F32).reshape(LEN, 1)
+    segs = seg_ids.astype(F32).reshape(CHUNKS, 1, SPAN)
+    pads = pad_mask.astype(F32).reshape(CHUNKS, 1, SPAN)
     pad = pad_mask.astype(F32).reshape(LEN, 1)
-    seg_col = seg_ids.astype(F32).reshape(LEN, 1)
-    cols = jnp.concatenate(
-        [seg_col, fresh, to_end, pad, jnp.zeros((LEN, 124), F32)], axis=1
-    )
-    segs = seg_ids.astype(F32).reshape(CHUNKS, 1, SPAN)
 
     inputs = hidden_in.astype(F32)
     factor_in = rms_factor(inputs, 1e-5)
@@ -833,7 +915,7 @@
     latent = mm(normed, w_in[:, 3 * WIDTH :]).astype(BF)
     bias_row, gain_row = decay_bias.reshape(1, WIDTH), out_gain.reshape(1, WIDTH)
     query, keys, values, decay_in, gate_in, mixed, heads, states, *rest = mixer_fwd(
-        normed, latent, w_in, w_kv, bias_row, gain_row, cols, segs, late if own else (), comm + (0, 2) if own else None
+        normed, latent, w_in, w_kv, bias_row, gain_row, segs, pads, late if own else (), comm + (0, 2) if own else None
     )
     w_output, w_ff, w_dn = rest if own else gather_plain(late)
     w_output = w_output.reshape(WIDTH, D)
@@ -864,7 +946,7 @@
     grad_out = mm_tn(mixed, d_branch)
 
     sent = (grad_ff.astype(BF).reshape(count, rows_d, -1), grad_down.astype(BF).reshape(count, rows_ff, -1))
-    saved = (query, keys, values, decay_in, gate_in, gain_row, cols, segs, heads, states)
+    saved = (query, keys, values, decay_in, gate_in, gain_row, segs, pads, heads, states)
     d_query, d_keys, d_values, d_decay, d_gatein, d_bias, d_out_gain, *rest = mixer_bwd(
         saved, d_branch, w_output, sent if own else (), comm + (0, 3) if own else None
     )
@@ -893,6 +975,8 @@
         grad_vec,
     )
     own_in, own_kv, own_out, own_vec = scatter(sent, *comm, 1) if own else scatter_plain(sent)
+    if own:
+        return (block_out, grad_input, *unpack((own_in, own_kv, own_out, own_ff, own_down, own_vec), places))
     return (
         block_out,
         grad_input,

time: 536 us -> 482 us (0.90); the launches traced: 525 us -> 478 us
  local copies, waits for them, and re-layouts: 38.5 us -> 10.8 us
  Pallas kernels: 327 us -> 310 us
    unnamed x88 -> x73, local copies, waits for them, and re-layouts: 18.8 us -> 4.47 us
    pallas_call x1, Pallas kernels: 106 us -> 93 us  [mixer_fwd(): pl.pallas_call(partial(mixer_fwd_kernel, comm), grid=(BANDS,), in_specs=i...]
    pallas_call x1, Pallas kernels: 54.7 us -> 46.7 us  [gather(): pl.pallas_call(partial(gather_kernel, ring_size, line_size, kinds), in_sp...]
    convert_element_type x13 -> x2, other arithmetic: 8.22 us -> 1.53 us  [the longest x1 0.84 us: per_device(): pads = pad_mask.astype(F32).reshape(CHUNKS, 1, SPAN)]
where the time goes in v4:
time: 482 us; the launch traced here: 478 us
  Pallas kernels  310 us (64%)
  matrix products  137 us (28%)
  other arithmetic  18 us (4%)
  local copies, waits for them, and re-layouts  10.8 us (2%)
    pallas_call x1, Pallas kernels, mixer_bwd(): pl.pallas_call(partial(mixer_bwd_kernel, comm), grid=(BANDS,), in_specs=i...  101 us
    pallas_call x1, Pallas kernels, mixer_fwd(): pl.pallas_call(partial(mixer_fwd_kernel, comm), grid=(BANDS,), in_specs=i...  93 us
    pallas_call x1, Pallas kernels, scatter(): pl.pallas_call(partial(scatter_kernel, ring_size, line_size, kinds), in_s...  63.7 us
    dot_general x5, matrix products, mm(): lax.dot_general(left, right, (((1,), (0,)), ((), ())), preferred_element_...  53.6 us
    pallas_call x1, Pallas kernels, gather(): pl.pallas_call(partial(gather_kernel, ring_size, line_size, kinds), in_sp...  46.7 us
    dot_general x6, matrix products, mm_tn(): lax.dot_general(left, right, (((0,), (0,)), ((), ())), preferred_element_...  43.3 us
    dot_general x5, matrix products, mm_nt(): lax.dot_general(left, right, (((1,), (1,)), ((), ())), preferred_element_...  40.6 us

profile of v4, /device:TPU:0, one launch (start us, length us, event | category | flops | bytes accessed | tf_op | source)
XLA Modules:
  0.0 477.7 jit_solution(6726343610490892828)
XLA Ops:
  0.6 0.0 copy-start.8
  0.7 0.8 convert_element_type.62
  1.5 0.7 convert_element_type.61
  2.2 2.1 fusion.16
  4.3 0.0 copy-start.20
  4.3 2.6 pack_shards.1
  6.9 46.7 %gather_shards.1 = (bf16[32,32,3584]{2,1,0:T(8,128)(2,1)}, bf16[32,16,1024]{2,1,0:T(8,128)(2,1)}, f32[32,8,128]{2,1,0:T(8,128)}) custom-call(bf16[32,3584]{1,0:T(8,128)(2,1)} %get-tuple-element.57.refs_0_, bf16[16,1024]{1,0:T(8,128)(2,1)} %get-tuple-element.58.refs_1_, f32[8,128]{1,0:T(8,128)} %get-tuple-element.59.refs_2_), custom_call_target="tpu_custom_call" | custom-call | tf_op jit(solution)/shard_map/gather_shards/pallas_call | solution.py:752
  53.6 0.8 fusion.44
  54.4 0.0 copy-start.7
  54.4 0.0 copy-start.22
  54.4 2.3 fusion.43
  56.7 0.0 copy-done.8
  56.7 0.5 fusion.10.refs_0_
  57.3 0.0 copy-start.2
  57.3 0.0 copy-start.3
  57.3 0.0 copy-start.4
  57.3 3.2 convolution_convert_fusion.4.refs_1_
  60.6 0.0 copy-done.6
  60.6 0.0 copy-done.20
  60.6 0.0 copy-done.7
  60.6 0.0 copy-done.22
  60.7 93.0 %mixer_fwd.1 = (f32[1024,1024]{1,0:T(8,128)}, f32[1024,1024]{1,0:T(8,128)}, f32[1024,1024]{1,0:T(8,128)}, f32[1024,1024]{1,0:T(8,128)}, f32[1024,1024]{1,0:T(8,1...) custom-call(bf16[1024,1024]{1,0:T(8,128)(2,1)} %copy-done.12, ...), custom_call_target="tpu_custom_call" | custom-call | tf_op jit(solution)/shard_map/mixer_fwd/pallas_call | solution.py:301
  153.7 0.0 slice-start.2
  153.7 0.0 slice-start.3
  153.7 0.0 slice-start.4
  153.7 6.8 %multiply_reduce_fusion.2 = (f32[1024]{0:T(1024)S(1)}, f32[1024,1024]{1,0:T(8,128)}) fusion(bf16[1024,1024]{1,0:T(8,128)(2,1)} %get-tuple-element.66, bf16[1024,1024]{1,0:T(8,128)(2,1)} %bitcast.84, bf16[1024,1024]{1,0:T(8,128)(2,1)S(1)} %copy-done.8), kind=kOutput, calls=%fused_computation.35 | convolution fusion | flops 2151676928 | bytes 10489856 | tf_op jit(solution)/shard_map/dot_general | solution.py:31
  160.5 4.1 multiply_convert_fusion.3
  164.6 0.0 copy-start.14
  164.6 0.0 slice-start.6
  164.6 10.3 %fusion.6 = f32[1024,2816]{1,0:T(8,128)} fusion(bf16[1024,1024]{1,0:T(8,128)(2,1)} %multiply_convert_fusion.3, bf16[1024,5632]{1,0:T(8,128)(2,1)S(1)} %bitcast.114), kind=kOutput, calls=%fused_computation.16 | convolution fusion | flops 5905580032 | bytes 19398656 | tf_op jit(solution)/shard_map/dot_general | solution.py:31
  174.9 9.5 %fusion.30 = f32[1024,2816]{1,0:T(8,128)} fusion(bf16[2816,1024]{1,0:T(8,128)(2,1)S(1)} %bitcast.118, bf16[1024,1024]{1,0:T(8,128)(2,1)S(1)} %copy-done.14, f32[1024]{0:T(1024)S(1)} %convert_element_type.62), kind=kOutput, calls=%fused_computation.52 | convolution fusion | flops 5908725760 | bytes 19402752 | tf_op jit(solution)/shard_map/dot_general | solution.py:35
  184.4 21.9 %multiply_convert_fusion.1 = (bf16[1024,2816]{1,0:T(8,128)(2,1)}, bf16[1024,2816]{1,0:T(8,128)(2,1)}, bf16[1024,2816]{1,0:T(8,128)(2,1)}) fusion(f32[1024,2816]{1,0:T(8,128)} %fusion.30, f32[1024,2816]{1,0:T(8,128)} %fusion.6, bf16[1024,1024]{1,0:T(8,128)(2,1)} %multiply_convert_fusion.3, bf16[1024,5632]{1,0:T(8,128)(2,1)} %bitcast.110), kind=kOutput, calls=%fused_computation.2 | convolution fusion | flops 5948833792 | bytes 48234496 | tf_op jit(solution)/shard_map/dot_general | solution.py:31
  206.3 11.4 %add_convert_fusion = bf16[1024,1024]{1,0:T(8,128)(2,1)} fusion(f32[1024,1024]{1,0:T(8,128)} %get-tuple-element.121, bf16[1024,2816]{1,0:T(8,128)(2,1)} %get-tuple-element.109, bf16[2816,1024]{1,0:T(8,128)(2,1)} %bitcast.115), kind=kOutput, calls=%fused_computation.33 | convolution fusion | flops 5907677184 | bytes 17825792 | tf_op jit(solution)/shard_map/dot_general | solution.py:31
  217.7 21.6 %multiply_reduce_fusion = (f32[1024]{0:T(1024)S(1)}, f32[1024]{0:T(1024)S(1)}, f32[1024,1024]{1,0:T(8,128)}) fusion(f32[1024,1024]{1,0:T(8,128)} %get-tuple-element.121, f32[1024]{0:T(1024)S(1)} %add_rsqrt_fusion, f32[1024]{0:T(1024)S(1)} %bitcast.98, bf16[1024,5632]{1,0:T(8,128)(2,1)} %bitcast.111, bf16[1024,2816]{1,0:T(8,128)(2,1)} %get-tuple-element.108, ...), kind=kOutput, calls=%fused_computation.28 | convolution fusion | flops 11840518144 | bytes 31473664 | tf_op jit(solution)/shard_map/dot_general | solution.py:35
  239.3 19.7 %convolution_convert_fusion = bf16[1024,5632]{1,0:T(8,128)(2,1)} fusion(bf16[1024,1024]{1,0:T(8,128)(2,1)} %multiply_convert_fusion.3, bf16[1024,2816]{1,0:T(8,128)(2,1)} %get-tuple-element.108, bf16[1024,2816]{1,0:T(8,128)(2,1)} %get-tuple-element.107), kind=kOutput, calls=%fused_computation.6 | convolution fusion | flops 11839995904 | bytes 25165824 | tf_op jit(solution)/shard_map/dot_general | solution.py:39
  259.0 5.6 %fusion.40 = (bf16[1024,1024]{1,0:T(8,128)(2,1)S(1)}, f32[1024,1024]{1,0:T(8,128)}) fusion(f32[1024]{0:T(1024)S(1)} %convert_element_type.62, bf16[1024,1024]{1,0:T(8,128)(2,1)S(1)} %copy-done.14, f32[1024]{0:T(1024)S(1)} %broadcast_multiply_fusion.1, f32[1024,1024]{1,0:T(8,128)} %get-tuple-element.121, f32[1024,1024]{1,0:T(8,128)} %get-tuple-element.122, ...), kind=kLoop, calls=%fused_computation.71 | loop fusion | flops 9437184 | bytes 16793600 | tf_op jit(solution)/shard_map/convert_element_type | solution.py:945
  264.6 3.8 convolution_convert_fusion.3
  268.4 8.3 %convolution_convert_fusion.2 = bf16[2816,1024]{1,0:T(8,128)(2,1)} fusion(bf16[1024,2816]{1,0:T(8,128)(2,1)S(1)} %copy-done.27, bf16[1024,1024]{1,0:T(8,128)(2,1)S(1)} %copy-done.14, f32[1024]{0:T(1024)S(1)} %convert_element_type.62), kind=kOutput, calls=%fused_computation.20 | convolution fusion | flops 5911609344 | bytes 13635584 | tf_op jit(solution)/shard_map/dot_general | solution.py:39
  276.7 101.3 %mixer_bwd.1 = (bf16[1024,1024]{1,0:T(8,128)(2,1)}, bf16[1024,1024]{1,0:T(8,128)(2,1)}, bf16[1024,1024]{1,0:T(8,128)(2,1)}, bf16[1024,1024]{1,0:T(8,128)(2,1)}, ...) custom-call(f32[1024,1024]{1,0:T(8,128)} %get-tuple-element.70.refs_, ...), custom_call_target="tpu_custom_call" | custom-call | tf_op jit(solution)/shard_map/mixer_bwd/pallas_call | solution.py:330
  378.0 2.5 fusion.41
  380.5 0.7 fusion.25
  381.3 0.7 fusion.23
  382.0 1.1 pad_maximum_fusion.21
  383.2 0.2 constant_dynamic-update-slice_fusion.2
  383.3 0.8 copy-done.16
  384.1 0.2 constant_dynamic-update-slice_fusion.1
  384.3 0.6 copy-done.15
  384.9 0.2 constant_dynamic-update-slice_fusion
  385.1 0.3 copy-done.19
  385.3 0.7 fusion.27
  386.1 0.0 copy-start.9
  386.1 0.0 copy-start.21
  386.1 0.0 copy-start.23
  386.1 0.7 fusion.26
  386.9 0.4 slice-done
  387.3 1.0 slice-done.1
  388.3 0.7 copy-done.9
  389.1 8.1 %fusion.15 = (f32[1024]{0:T(1024)S(1)}, f32[1024]{0:T(1024)S(1)}, f32[1024,1024]{1,0:T(8,128)S(1)}) fusion(bf16[1024,1024]{1,0:T(8,128)(2,1)S(1)} %copy-done.9, f32[1024]{0:T(1024)S(1)} %copy-done.21, f32[1024]{0:T(1024)S(1)} %bitcast.101, bf16[1024,3584]{1,0:T(8,128)(2,1)S(1)} %fusion.26, bf16[1024,3584]{1,0:T(8,128)(2,1)S(1)} %bitcast.77), kind=kOutput, calls=%fused_computation.26 | convolution fusion | flops 7523530752 | bytes 20987904 | tf_op jit(solution)/shard_map/dot_general | solution.py:35
  397.1 0.0 copy-start.10
  397.2 10.0 %convolution_convert_fusion.1 = bf16[1024,3584]{1,0:T(8,128)(2,1)} fusion(bf16[1024,1024]{1,0:T(8,128)(2,1)S(1)} %copy-done.13, bf16[1024,3584]{1,0:T(8,128)(2,1)S(1)} %fusion.26), kind=kOutput, calls=%fused_computation.7 | convolution fusion | flops 7519862784 | bytes 16777216 | tf_op jit(solution)/shard_map/dot_general | solution.py:39
  407.2 3.0 fusion.14
  410.3 0.7 broadcast_in_dim.5.refs_3_
  410.9 63.7 %scatter_sums.1 = (f32[32,3584]{1,0:T(8,128)}, f32[16,1024]{1,0:T(8,128)}, f32[32,1024]{1,0:T(8,128)}, f32[8,128]{1,0:T(8,128)}) custom-call(bf16[32,32,3584]{2,1,0:T(8,128)(2,1)} %bitcast.81, bf16[32,16,1024]{2,1,0:T(8,128)(2,1)} %bitcast.83, bf16[32,32,1024]{2,1,0:T(8,128)(2,1)} %bitcast.86, f32[32,8,128]{2,1,0:T(8,128)} %broadcast_in_dim.5.refs_3_), custom_call_target="tpu_custom_call" | custom-call | tf_op jit(solution)/shard_map/scatter_sums/pallas_call | solution.py:555
  474.6 2.6 unpack_sums.1
  (51 shorter events, 0.1 us)
Async XLA Ops:
  0.6 56.1 %copy-start.8 = (bf16[1024,1024]{1,0:T(8,128)(2,1)S(1)}, bf16[1024,1024]{1,0:T(8,128)(2,1)}, u32[]{:S(2)}) copy-start(bf16[1024,1024]{1,0:T(8,128)(2,1)} %param.15) | copy-start | bytes 6291460
  1.5 266.9 %copy-start.5 = (f32[1024]{0:T(1024)}, f32[1024]{0:T(1024)S(1)}, u32[]{:S(2)}) copy-start(f32[1024]{0:T(1024)S(1)} %convert_element_type.62) | copy-start | bytes 12292
  2.2 58.4 %copy-start.6 = (f32[1024]{0:T(1024)}, f32[1024]{0:T(1024)S(1)}, u32[]{:S(2)}) copy-start(f32[1024]{0:T(1024)S(1)} %convert_element_type.61) | copy-start | bytes 12292
  4.3 56.3 %copy-start.20 = (f32[1024]{0:T(1024)}, f32[1024]{0:T(1024)S(1)}, u32[]{:S(2)}) copy-start(f32[1024]{0:T(1024)S(1)} %add_rsqrt_fusion.1) | copy-start | bytes 12292
  54.4 6.2 %copy-start.7 = (f32[1,1024]{1,0:T(1,128)}, f32[1,1024]{1,0:T(1,128)S(1)}, u32[]{:S(2)}) copy-start(f32[1,1024]{1,0:T(1,128)S(1)} %get-tuple-element.117.refs_8_.refs_5_) | copy-start | bytes 12292
  54.4 6.2 %copy-start.22 = (f32[8,1,128]{2,1,0:T(1,128)}, f32[8,1,128]{2,1,0:T(1,128)S(1)}, u32[]{:S(2)}) copy-start(f32[8,1,128]{2,1,0:T(1,128)S(1)} %get-tuple-element.119) | copy-start | bytes 12292
  57.3 3.3 copy-start.12
  57.3 3.3 copy-start.2
  57.3 3.3 copy-start.3
  57.3 3.3 copy-start.4
  60.7 93.0 %copy-start = (bf16[1024,512]{1,0:T(8,128)(2,1)}, bf16[1024,512]{1,0:T(8,128)(2,1)S(1)}, u32[]{:S(2)}) copy-start(bf16[1024,512]{1,0:T(8,128)(2,1)S(1)} %convolution_convert_fusion.4.refs_1_) | copy-start | bytes 3145732
  153.7 10.9 %slice-start.2 = ((s8[11534336]{0:T(1024)(128)(4,1)}), s8[4194304]{0:T(1024)(128)(4,1)S(1)}, s32[]{:S(2)}) async-start(s8[11534336]{0:T(1024)(128)(4,1)} %bitcast.112), calls=%async_computation.2 | async-start | bytes 8388608
  153.7 10.9 %slice-start.3 = ((s8[11534336]{0:T(1024)(128)(4,1)}), s8[4194304]{0:T(1024)(128)(4,1)S(1)}, s32[]{:S(2)}) async-start(s8[11534336]{0:T(1024)(128)(4,1)} %bitcast.112), calls=%async_computation.3 | async-start | bytes 8388608
  153.7 10.9 %slice-start.4 = ((s8[11534336]{0:T(1024)(128)(4,1)}), s8[3145728]{0:T(1024)(128)(4,1)S(1)}, s32[]{:S(2)}) async-start(s8[11534336]{0:T(1024)(128)(4,1)} %bitcast.112), calls=%async_computation.4 | async-start | bytes 6291456
  160.5 14.4 %slice-start.5 = ((s8[5767168]{0:T(1024)(128)(4,1)}), s8[4194304]{0:T(1024)(128)(4,1)S(1)}, s32[]{:S(2)}) async-start(s8[5767168]{0:T(1024)(128)(4,1)} %bitcast.116), calls=%async_computation.5 | async-start | bytes 8388608
  164.6 10.3 %copy-start.14 = (bf16[1024,1024]{1,0:T(8,128)(2,1)S(1)}, bf16[1024,1024]{1,0:T(8,128)(2,1)}, u32[]{:S(2)}) copy-start(bf16[1024,1024]{1,0:T(8,128)(2,1)} %param.29) | copy-start | bytes 6291460
  164.6 10.3 %slice-start.6 = ((s8[5767168]{0:T(1024)(128)(4,1)}), s8[1572864]{0:T(1024)(128)(4,1)S(1)}, s32[]{:S(2)}) async-start(s8[5767168]{0:T(1024)(128)(4,1)} %bitcast.116), calls=%async_computation.6 | async-start | bytes 3145728
  259.0 5.6 %copy-start.26 = (bf16[1024,1024]{1,0:T(8,128)(2,1)S(1)}, bf16[1024,1024]{1,0:T(8,128)(2,1)}, u32[]{:S(2)}) copy-start(bf16[1024,1024]{1,0:T(8,128)(2,1)} %get-tuple-element.66) | copy-start | bytes 6291460
  264.6 3.8 copy-start.11
  264.6 3.8 copy-start.27
  378.0 2.5 copy-start.1
  381.3 1.9 copy-start.17
  382.0 2.1 copy-start.16
  383.2 1.7 copy-start.15
  384.1 1.2 copy-start.19
  384.9 1.2 copy-start.18
  384.9 2.4 slice-start
  385.3 3.0 slice-start.1
  386.1 2.9 copy-start.9
  386.1 2.9 copy-start.21
  386.1 2.9 copy-start.23
  389.0 8.1 %copy-start.13 = (bf16[1024,1024]{1,0:T(8,128)(2,1)S(1)}, bf16[1024,1024]{1,0:T(8,128)(2,1)}, u32[]{:S(2)}) copy-start(bf16[1024,1024]{1,0:T(8,128)(2,1)} %copy-done.12) | copy-start | bytes 6291460
  397.1 10.1 %copy-start.24 = (f32[1,1024]{1,0:T(1,128)S(1)}, f32[1,1024]{1,0:T(1,128)}, u32[]{:S(2)}) copy-start(f32[1,1024]{1,0:T(1,128)} %get-tuple-element.82) | copy-start | bytes 12292
  397.1 10.1 %copy-start.25 = (f32[1,1024]{1,0:T(1,128)S(1)}, f32[1,1024]{1,0:T(1,128)}, u32[]{:S(2)}) copy-start(f32[1,1024]{1,0:T(1,128)} %get-tuple-element.83) | copy-start | bytes 12292
  397.1 10.1 %copy-start.10 = (f32[1024,1024]{1,0:T(8,128)S(1)}, f32[1024,1024]{1,0:T(8,128)}, u32[]{:S(2)}) copy-start(f32[1024,1024]{1,0:T(8,128)} %get-tuple-element.106) | copy-start | bytes 12582916

commit v5 on v4

--- a/solution.py
+++ b/solution.py
@@ -765,6 +765,140 @@
         pl.when(tick == number * ticks // len(stages))(stage)
 
 
+BLOCK = 256
+PART = 256
+
+
+def ffn_kernel(
+    x_ref,
+    mixed_ref,
+    wo_ref,
+    cot_ref,
+    pad_ref,
+    gain_ref,
+    wg_ref,
+    wu_ref,
+    wd_ref,
+    out_ref,
+    dmid_ref,
+    dbranch_ref,
+    ggate_ref,
+    gup_ref,
+    gdown_ref,
+    dgain_ref,
+    middle,
+    normed,
+    normed_t,
+    dffn,
+    out_acc,
+    dn_acc,
+    hidden,
+    dgate,
+    dup,
+):
+    step = pl.program_id(0)
+    gain = gain_ref[...]
+
+    @pl.when(step == 0)
+    def _():
+        middle[...] = mm(mixed_ref[...], wo_ref[...])
+        out_acc[...] = jnp.zeros_like(out_acc)
+        dn_acc[...] = jnp.zeros_like(dn_acc)
+
+        def start(index, carry):
+            rows = pl.ds(pl.multiple_of(index * SPAN, SPAN), SPAN)
+            value = middle[rows, :] + x_ref[rows, :].astype(F32)
+            middle[rows, :] = value
+            low = (value * rms_factor(value, 1e-5) * gain).astype(BF)
+            normed[rows, :] = low
+            normed_t[:, rows] = jnp.transpose(low)
+            pad = jnp.transpose(jnp.broadcast_to(pad_ref[index], (SPAN, SPAN)))[:, 0:1]
+            dffn[rows, :] = (cot_ref[rows, :].astype(F32) * pad).astype(BF)
+            return carry
+
+        lax.fori_loop(0, CHUNKS, start, 0)
+
+    wg, wu, wd = wg_ref[...], wu_ref[...], wd_ref[...]
+    for part in range(LEN // PART):
+        rows = pl.ds(part * PART, PART)
+        gate, up = mm(normed[rows, :], wg), mm(normed[rows, :], wu)
+        dhidden = mm_nt(dffn[rows, :], wd)
+        sig = 1.0 / (1.0 + jnp.exp(-gate))
+        silu = gate * sig
+        hidden[rows, :] = (silu * up).astype(BF)
+        dgate[rows, :] = (dhidden * up * (sig * (1.0 + gate * (1.0 - sig)))).astype(BF)
+        dup[rows, :] = (dhidden * silu).astype(BF)
+    gdown_ref[...] = mm_tn(hidden[...], dffn[...]).astype(BF)
+    ggate_ref[...] = mm(normed_t[...], dgate[...]).astype(BF)
+    gup_ref[...] = mm(normed_t[...], dup[...]).astype(BF)
+    out_acc[...] += mm(hidden[...], wd)
+    dn_acc[...] += mm_nt(dgate[...], wg) + mm_nt(dup[...], wu)
+
+    @pl.when(step == pl.num_programs(0) - 1)
+    def _():
+        dgain_ref[...] = jnp.zeros_like(dgain_ref)
+
+        def end(index, carry):
+            rows = pl.ds(pl.multiple_of(index * SPAN, SPAN), SPAN)
+            value = middle[rows, :]
+            out_ref[rows, :] = (value + out_acc[rows, :]).astype(BF)
+            factor = rms_factor(value, 1e-5)
+            scaled = value * factor
+            grad = dn_acc[rows, :]
+            dscaled = grad * gain
+            dmid = factor * (dscaled - scaled * jnp.mean(dscaled * scaled, axis=-1, keepdims=True))
+            dmid += dffn[rows, :].astype(F32)
+            dmid_ref[rows, :] = dmid
+            dbranch_ref[rows, :] = dmid.astype(BF)
+            dgain_ref[...] += jnp.sum(grad * scaled, axis=0, keepdims=True)
+            return carry
+
+        lax.fori_loop(0, CHUNKS, end, 0)
+
+
+def feed_forward(hidden_in, mixed, w_output, cotangent, pads, gain_mid, w_ff, w_dn):
+    blocks = FF // BLOCK
+    square = fixed((LEN, D))
+    column = pl.BlockSpec((D, BLOCK), lambda step: (0, step))
+    band = pl.BlockSpec((BLOCK, D), lambda step: (step, 0))
+    return pl.pallas_call(
+        ffn_kernel,
+        grid=(blocks,),
+        in_specs=[
+            square,
+            square,
+            fixed((WIDTH, D)),
+            square,
+            fixed((CHUNKS, 1, SPAN)),
+            fixed((1, D)),
+            column,
+            pl.BlockSpec((D, BLOCK), lambda step: (0, blocks + step)),
+            band,
+        ],
+        out_specs=[square, square, square, column, column, band, fixed((1, D))],
+        out_shape=[
+            jax.ShapeDtypeStruct((LEN, D), BF),
+            jax.ShapeDtypeStruct((LEN, D), F32),
+            jax.ShapeDtypeStruct((LEN, D), BF),
+            jax.ShapeDtypeStruct((D, FF), BF),
+            jax.ShapeDtypeStruct((D, FF), BF),
+            jax.ShapeDtypeStruct((FF, D), BF),
+            jax.ShapeDtypeStruct((1, D), F32),
+        ],
+        scratch_shapes=[
+            pltpu.VMEM((LEN, D), F32),
+            pltpu.VMEM((LEN, D), BF),
+            pltpu.VMEM((D, LEN), BF),
+            pltpu.VMEM((LEN, D), BF),
+            pltpu.VMEM((LEN, D), F32),
+            pltpu.VMEM((LEN, D), F32),
+        ]
+        + [pltpu.VMEM((LEN, BLOCK), BF)] * 3,
+        compiler_params=pltpu.CompilerParams(vmem_limit_bytes=62 << 20),
+        name="feed_forward",
+    )(hidden_in, mixed, w_output, cotangent, pads, gain_mid, w_ff, w_ff, w_dn)
+
+
 def pack_kernel(places, *refs):
     flats, packed = refs[: len(places) + 1], refs[len(places) + 1 :]
     for flat, (target, offset, tiles) in zip(flats, places):
@@ -874,6 +1008,7 @@
         (3, FF, ff),
         (4, 0, D // 128),
     )
+    sums_at = places[:7] + ((3, 0, ff), (4, 0, ff), (5, 0, D // 128))
     if own:
         shapes = (
             (rows_d, 3 * WIDTH + latents),
@@ -907,7 +1042,6 @@
 
     segs = seg_ids.astype(F32).reshape(CHUNKS, 1, SPAN)
     pads = pad_mask.astype(F32).reshape(CHUNKS, 1, SPAN)
-    pad = pad_mask.astype(F32).reshape(LEN, 1)
 
     inputs = hidden_in.astype(F32)
     factor_in = rms_factor(inputs, 1e-5)
@@ -921,36 +1055,21 @@
     w_output = w_output.reshape(WIDTH, D)
     w_ff = w_ff.reshape(D, 2 * FF)
     w_dn = w_dn.reshape(FF, D)
-    middle = inputs + mm(mixed, w_output)
-    factor_mid = rms_factor(middle, 1e-5)
-    normed_mid = (middle * factor_mid * gain_mid).astype(BF)
-    gate_val = mm(normed_mid, w_ff[:, :FF])
-    up_val = mm(normed_mid, w_ff[:, FF:])
-    sig = jax.nn.sigmoid(gate_val)
-    silu = gate_val * sig
-    hidden = (silu * up_val).astype(BF)
-    block_out = (middle + mm(hidden, w_dn)).astype(BF)
-
-    d_outf = cotangent.astype(F32) * pad
-    d_ffn = d_outf.astype(BF)
-    grad_down = mm_tn(hidden, d_ffn)
-    d_hidden = mm_nt(d_ffn, w_dn)
-    d_gate = (d_hidden * up_val * (sig * (1.0 + gate_val * (1.0 - sig)))).astype(BF)
-    d_up = (d_hidden * silu).astype(BF)
-    d_both = jnp.concatenate([d_gate, d_up], axis=1)
-    grad_ff = mm_tn(normed_mid, d_both)
-    d_normed_mid = mm_nt(d_both, w_ff)
-    d_middle, d_gain_mid = rms_back(d_normed_mid, middle, factor_mid, gain_mid)
-    d_middle = d_middle + d_outf
-    d_branch = d_middle.astype(BF)
+    block_out, d_middle, d_branch, grad_gate, grad_up, grad_down, d_gain_mid = feed_forward(
+        hidden_in, mixed, w_output, cotangent, pads, gain_mid.reshape(1, D), w_ff, w_dn
+    )
     grad_out = mm_tn(mixed, d_branch)
 
-    sent = (grad_ff.astype(BF).reshape(count, rows_d, -1), grad_down.astype(BF).reshape(count, rows_ff, -1))
+    sent = (
+        grad_gate.reshape(count, rows_d, -1),
+        grad_up.reshape(count, rows_d, -1),
+        grad_down.reshape(count, rows_ff, -1),
+    )
     saved = (query, keys, values, decay_in, gate_in, gain_row, segs, pads, heads, states)
     d_query, d_keys, d_values, d_decay, d_gatein, d_bias, d_out_gain, *rest = mixer_bwd(
         saved, d_branch, w_output, sent if own else (), comm + (0, 3) if own else None
     )
-    own_ff, own_down = rest if own else scatter_plain(sent)
+    own_gate, own_up, own_down = rest if own else scatter_plain(sent)
     grad_kv, d_latent = [], []
     for g in range(GROUPS):
         d_kv = jnp.concatenate(
@@ -965,7 +1084,7 @@
     d_normed = mm_nt(d_in, w_in)
     d_inputs, d_gain_in = rms_back(d_normed, inputs, factor_in, gain_in)
     grad_input = d_middle + d_inputs
-    grad_vec = jnp.concatenate([d_gain_in, d_gain_mid, d_bias.reshape(-1), d_out_gain.reshape(-1)])
+    grad_vec = jnp.concatenate([d_gain_in, d_gain_mid.reshape(-1), d_bias.reshape(-1), d_out_gain.reshape(-1)])
 
     grad_vec = jnp.broadcast_to(grad_vec.reshape(count, 1, vec_size), (count, 8, vec_size))
     sent = (
@@ -976,7 +1095,7 @@
     )
     own_in, own_kv, own_out, own_vec = scatter(sent, *comm, 1) if own else scatter_plain(sent)
     if own:
-        return (block_out, grad_input, *unpack((own_in, own_kv, own_out, own_ff, own_down, own_vec), places))
+        return (block_out, grad_input, *unpack((own_in, own_kv, own_out, own_gate, own_up, own_down, own_vec), sums_at))
     return (
         block_out,
         grad_input,
@@ -987,8 +1106,8 @@
         own_in[:, WIDTH : 2 * WIDTH].reshape(-1),
         own_in[:, 2 * WIDTH : 3 * WIDTH].reshape(-1),
         own_out.reshape(-1),
-        own_ff[:, :FF].reshape(-1),
-        own_ff[:, FF:].reshape(-1),
+        own_gate.reshape(-1),
+        own_up.reshape(-1),
         own_down.reshape(-1),
         own_vec[0],
     )

time: 482 us -> 440 us (0.913)
  matrix products: 137 us -> 30.3 us
  Pallas kernels: 310 us -> 381 us
  other arithmetic: 18 us -> 8.28 us
    pallas_call x0 -> x1, Pallas kernels: none -> 74.1 us  [feed_forward(): pl.pallas_call(ffn_kernel, grid=(blocks,), in_specs=[square, square, fixe...]
    dot_general x5 -> x1, matrix products: 53.6 us -> 3.25 us  [mm(): lax.dot_general(left, right, (((1,), (0,)), ((), ())), preferred_element_...]
    dot_general x5 -> x3, matrix products: 40.6 us -> 9.54 us  [mm_nt(): lax.dot_general(left, right, (((1,), (1,)), ((), ())), preferred_element_...]
    dot_general x6 -> x4, matrix products: 43.3 us -> 17.5 us  [mm_tn(): lax.dot_general(left, right, (((0,), (0,)), ((), ())), preferred_element_...]
    convert_element_type x2 -> x0, other arithmetic: 9.67 us -> none  [the longest x1 5.61 us: per_device(): d_branch = d_middle.astype(BF)]
    pallas_call x1, Pallas kernels: 101 us -> 94.5 us  [mixer_bwd(): pl.pallas_call(partial(mixer_bwd_kernel, comm), grid=(BANDS,), in_specs=i...]
where the time goes in v5:
time: 440 us; the launch traced here: 432 us
  Pallas kernels  381 us (87%)
  matrix products  30.3 us (7%)
  local copies, waits for them, and re-layouts  11 us (2%)
  other arithmetic  8.28 us (2%)
    pallas_call x1, Pallas kernels, mixer_bwd(): pl.pallas_call(partial(mixer_bwd_kernel, comm), grid=(BANDS,), in_specs=i...  94.5 us
    pallas_call x1, Pallas kernels, mixer_fwd(): pl.pallas_call(partial(mixer_fwd_kernel, comm), grid=(BANDS,), in_specs=i...  92.9 us
    pallas_call x1, Pallas kernels, feed_forward(): pl.pallas_call(ffn_kernel, grid=(blocks,), in_specs=[square, square, fixe...  74.1 us
    pallas_call x1, Pallas kernels, scatter(): pl.pallas_call(partial(scatter_kernel, ring_size, line_size, kinds), in_s...  68 us
    pallas_call x1, Pallas kernels, gather(): pl.pallas_call(partial(gather_kernel, ring_size, line_size, kinds), in_sp...  46.7 us
    dot_general x4, matrix products, mm_tn(): lax.dot_general(left, right, (((0,), (0,)), ((), ())), preferred_element_...  17.5 us
    dot_general x3, matrix products, mm_nt(): lax.dot_general(left, right, (((1,), (1,)), ((), ())), preferred_element_...  9.54 us

profile of v5, /device:TPU:0, one launch (start us, length us, event | category | flops | bytes accessed | tf_op | source)
XLA Modules:
  0.0 432.4 jit_solution(2435811141168807074)
XLA Ops:
  0.6 0.0 copy-start.8
  0.7 0.8 convert_element_type.30
  1.5 0.7 convert_element_type.31
  2.2 2.1 fusion.10
  4.3 2.6 pack_shards.1
  6.9 46.7 %gather_shards.1 = (bf16[32,32,3584]{2,1,0:T(8,128)(2,1)}, bf16[32,16,1024]{2,1,0:T(8,128)(2,1)}, f32[32,8,128]{2,1,0:T(8,128)}) custom-call(bf16[32,3584]{1,0:T(8,128)(2,1)} %get-tuple-element.65.refs_0_, bf16[16,1024]{1,0:T(8,128)(2,1)} %get-tuple-element.66.refs_1_, f32[8,128]{1,0:T(8,128)} %get-tuple-element.67.refs_2_), custom_call_target="tpu_custom_call" | custom-call | tf_op jit(solution)/shard_map/gather_shards/pallas_call | solution.py:752
  53.6 1.4 slice_bitcast_fusion
  55.0 2.1 fusion.30
  57.1 0.0 copy-done.8
  57.1 0.5 fusion.4.refs_0_
  57.6 0.0 copy-start.10
  57.7 0.0 copy-start.2
  57.7 0.0 copy-start.3
  57.7 0.0 copy-start.4
  57.7 3.2 convolution_convert_fusion.2.refs_1_
  60.9 0.0 copy-done.6
  61.0 0.0 copy-done.5
  61.0 0.0 copy-done.7
  61.0 0.0 copy-done.10
  61.0 0.0 copy-done.2
  61.0 0.0 copy-done.3
  61.0 0.0 copy-done.4
  61.0 0.0 copy-start
  61.0 92.9 %mixer_fwd.1 = (f32[1024,1024]{1,0:T(8,128)}, f32[1024,1024]{1,0:T(8,128)}, f32[1024,1024]{1,0:T(8,128)}, f32[1024,1024]{1,0:T(8,128)}, f32[1024,1024]{1,0:T(8,1...) custom-call(bf16[1024,1024]{1,0:T(8,128)(2,1)} %copy-done.10, ...), custom_call_target="tpu_custom_call" | custom-call | tf_op jit(solution)/shard_map/mixer_fwd/pallas_call | solution.py:301
  153.9 0.0 copy-done
  153.9 74.1 %feed_forward.1 = (bf16[1024,1024]{1,0:T(8,128)(2,1)}, f32[1024,1024]{1,0:T(8,128)}, bf16[1024,1024]{1,0:T(8,128)(2,1)}, bf16[1024,2816]{1,0:T(8,128)(2,1)}, bf1...) custom-call(bf16[1024,1024]{1,0:T(8,128)(2,1)} %x_ref.1, ...), custom_call_target="tpu_custom_call" | custom-call | tf_op jit(solution)/shard_map/feed_forward/pallas_call | solution.py:864
  228.1 6.0 %convolution_convert_fusion.1 = bf16[1024,1024]{1,0:T(8,128)(2,1)} fusion(bf16[1024,1024]{1,0:T(8,128)(2,1)} %get-tuple-element.74.mixed_ref, bf16[1024,1024]{1,0:T(8,128)(2,1)} %get-tuple-element.87.refs_10_), kind=kOutput, calls=%fused_computation.16 | convolution fusion | flops 2148532224 | bytes 6291456 | tf_op jit(solution)/shard_map/dot_general | solution.py:39
  234.1 94.5 %mixer_bwd.1 = (bf16[1024,1024]{1,0:T(8,128)(2,1)}, bf16[1024,1024]{1,0:T(8,128)(2,1)}, bf16[1024,1024]{1,0:T(8,128)(2,1)}, bf16[1024,1024]{1,0:T(8,128)(2,1)}, ...) custom-call(f32[1024,1024]{1,0:T(8,128)} %get-tuple-element.80.refs_, ...), custom_call_target="tpu_custom_call" | custom-call | tf_op jit(solution)/shard_map/mixer_bwd/pallas_call | solution.py:330
  328.6 0.0 copy-start.1
  328.6 2.5 fusion.28
  331.1 0.0 copy-done.1
  331.1 0.7 fusion.18
  331.9 0.0 copy-start.15
  331.9 0.7 fusion.16
  332.6 0.0 copy-start.14
  332.6 1.1 pad_maximum_fusion.18
  333.7 0.0 copy-done.15
  333.7 0.2 constant_dynamic-update-slice_fusion.2
  333.9 0.9 copy-done.14
  334.7 0.2 constant_dynamic-update-slice_fusion.1
  334.9 0.5 copy-done.13
  335.4 0.2 constant_dynamic-update-slice_fusion
  335.6 0.4 copy-done.16
  335.9 0.7 fusion.20
  336.7 0.0 copy-start.9
  336.7 0.7 fusion.19
  337.4 0.2 slice-done
  337.6 1.1 slice-done.1
  338.7 0.7 copy-done.9
  339.4 8.1 %fusion.9 = (f32[1024]{0:T(1024)S(1)}, f32[1024]{0:T(1024)S(1)}, f32[1024,1024]{1,0:T(8,128)S(1)}) fusion(bf16[1024,1024]{1,0:T(8,128)(2,1)S(1)} %copy-done.9, f32[1024]{0:T(1024)S(1)} %add_rsqrt_fusion, f32[1024]{0:T(1024)S(1)} %bitcast.95, bf16[1024,3584]{1,0:T(8,128)(2,1)S(1)} %fusion.19, bf16[1024,3584]{1,0:T(8,128)(2,1)S(1)} %bitcast.70), kind=kOutput, calls=%fused_computation.12 | convolution fusion | flops 7523530752 | bytes 20987904 | tf_op jit(solution)/shard_map/dot_general | solution.py:35
  347.4 0.0 copy-done.11
  347.5 0.0 copy-start.17
  347.5 0.0 copy-start.18
  347.5 0.0 copy-start.19
  347.5 0.0 copy-start.12
  347.5 10.0 %convolution_convert_fusion = bf16[1024,3584]{1,0:T(8,128)(2,1)} fusion(bf16[1024,1024]{1,0:T(8,128)(2,1)S(1)} %copy-done.11, bf16[1024,3584]{1,0:T(8,128)(2,1)S(1)} %fusion.19), kind=kOutput, calls=%fused_computation | convolution fusion | flops 7519862784 | bytes 16777216 | tf_op jit(solution)/shard_map/dot_general | solution.py:39
  357.5 0.0 copy-done.17
  357.5 0.0 copy-done.18
  357.5 0.0 copy-done.19
  357.5 0.0 copy-done.12
  357.5 3.1 fusion.8
  360.6 0.7 broadcast_in_dim.5.refs_3_
  361.3 68.0 %scatter_sums.1 = (f32[32,3584]{1,0:T(8,128)}, f32[16,1024]{1,0:T(8,128)}, f32[32,1024]{1,0:T(8,128)}, f32[8,128]{1,0:T(8,128)}) custom-call(bf16[32,32,3584]{2,1,0:T(8,128)(2,1)} %bitcast.77, bf16[32,16,1024]{2,1,0:T(8,128)(2,1)} %bitcast.82, bf16[32,32,1024]{2,1,0:T(8,128)(2,1)} %bitcast.83, f32[32,8,128]{2,1,0:T(8,128)} %broadcast_in_dim.5.refs_3_), custom_call_target="tpu_custom_call" | custom-call | tf_op jit(solution)/shard_map/scatter_sums/pallas_call | solution.py:555
  429.3 2.6 unpack_sums.1
  (12 shorter events, 0.0 us)
Async XLA Ops:
  0.6 56.5 %copy-start.8 = (bf16[1024,1024]{1,0:T(8,128)(2,1)S(1)}, bf16[1024,1024]{1,0:T(8,128)(2,1)}, u32[]{:S(2)}) copy-start(bf16[1024,1024]{1,0:T(8,128)(2,1)} %x_ref.1) | copy-start | bytes 6291460
  1.5 59.5 %copy-start.6 = (f32[1024]{0:T(1024)}, f32[1024]{0:T(1024)S(1)}, u32[]{:S(2)}) copy-start(f32[1024]{0:T(1024)S(1)} %convert_element_type.30) | copy-start | bytes 12292
  2.2 58.8 %copy-start.5 = (f32[1024]{0:T(1024)}, f32[1024]{0:T(1024)S(1)}, u32[]{:S(2)}) copy-start(f32[1024]{0:T(1024)S(1)} %convert_element_type.31) | copy-start | bytes 12292
  55.0 6.0 %copy-start.7 = (f32[1,1024]{1,0:T(1,128)}, f32[1,1024]{1,0:T(1,128)S(1)}, u32[]{:S(2)}) copy-start(f32[1,1024]{1,0:T(1,128)S(1)} %get-tuple-element.126.refs_8_.refs_5_) | copy-start | bytes 12292
  57.6 3.3 copy-start.10
  57.7 3.3 copy-start.2
  57.7 3.3 copy-start.3
  57.7 3.3 copy-start.4
  61.0 92.9 %copy-start = (bf16[1024,512]{1,0:T(8,128)(2,1)}, bf16[1024,512]{1,0:T(8,128)(2,1)S(1)}, u32[]{:S(2)}) copy-start(bf16[1024,512]{1,0:T(8,128)(2,1)S(1)} %convolution_convert_fusion.2.refs_1_) | copy-start | bytes 3145732
  328.6 2.5 copy-start.1
  331.9 1.8 copy-start.15
  332.6 2.1 copy-start.14
  333.7 1.7 copy-start.13
  334.7 1.2 copy-start.16
  335.4 2.2 slice-start
  335.9 2.8 slice-start.1
  336.7 2.7 copy-start.9
  339.4 8.1 %copy-start.11 = (bf16[1024,1024]{1,0:T(8,128)(2,1)S(1)}, bf16[1024,1024]{1,0:T(8,128)(2,1)}, u32[]{:S(2)}) copy-start(bf16[1024,1024]{1,0:T(8,128)(2,1)} %copy-done.10) | copy-start | bytes 6291460
  347.5 10.1 %copy-start.17 = (f32[1,1024]{1,0:T(1,128)S(1)}, f32[1,1024]{1,0:T(1,128)}, u32[]{:S(2)}) copy-start(f32[1,1024]{1,0:T(1,128)} %get-tuple-element.96) | copy-start | bytes 12292
  347.5 10.0 %copy-start.18 = (f32[1,1024]{1,0:T(1,128)S(1)}, f32[1,1024]{1,0:T(1,128)}, u32[]{:S(2)}) copy-start(f32[1,1024]{1,0:T(1,128)} %get-tuple-element.97) | copy-start | bytes 12292
  347.5 10.0 %copy-start.19 = (f32[1,1024]{1,0:T(1,128)S(1)}, f32[1,1024]{1,0:T(1,128)}, u32[]{:S(2)}) copy-start(f32[1,1024]{1,0:T(1,128)} %get-tuple-element.98) | copy-start | bytes 12292
  347.5 10.1 %copy-start.12 = (f32[1024,1024]{1,0:T(8,128)S(1)}, f32[1024,1024]{1,0:T(8,128)}, u32[]{:S(2)}) copy-start(f32[1024,1024]{1,0:T(8,128)} %get-tuple-element.79) | copy-start | bytes 12582916

commit v6 on v5

--- a/solution.py
+++ b/solution.py
@@ -21,6 +21,7 @@
 BANDS = WIDTH // LANES
 CHUNKS = LEN // SPAN
 LIMIT = 85.0
+TICKS = CHUNKS + 7
 AXES = ("dp", "fsdp")
 BF = jnp.bfloat16
 F32 = jnp.float32
@@ -108,10 +109,10 @@
 
 def mixer_fwd_kernel(comm, *refs):
     kinds = comm[2] if comm else 0
-    normed_ref, latent_ref, wq_ref, wd_ref, wg_ref, wk_ref, wv_ref, bias_ref, gain_ref, seg_ref, pad_ref = refs[:11]
-    shards, refs = refs[11 : 11 + kinds], refs[11 + kinds :]
-    q_ref, k_ref, v_ref, decay_ref, gate_ref, mixed_ref, heads_ref, states_ref = refs[:8]
-    gathered, state, sems = refs[8 : 8 + kinds], refs[8 + kinds], refs[9 + kinds :]
+    normed_ref, latent_ref, wp_ref, wkv_ref, bias_ref, gain_ref, seg_ref, pad_ref = refs[:8]
+    shards, refs = refs[8 : 8 + kinds], refs[8 + kinds :]
+    q_ref, k_ref, v_ref, decay_ref, gate_ref, mixed_ref, heads_ref, states_ref, normed_t_ref, latent_t_ref = refs[:10]
+    gathered, state, sems = refs[10 : 10 + kinds], refs[10 + kinds], refs[11 + kinds :]
     band = pl.program_id(0)
     job = Gather(comm[0], comm[1], shards, gathered, sems) if comm else None
     stages = job.stages() if comm else []
@@ -124,14 +125,15 @@
     lower_ones = triangle(True).astype(F32).astype(BF)
     state[...] = jnp.zeros_like(state)
     gain = gain_ref[...]
-    q_ref[...] = mm(normed_ref[...], wq_ref[...])
-    decay_ref[...] = mm(normed_ref[...], wd_ref[...]) + bias_ref[...]
-    gate_ref[...] = mm(normed_ref[...], wg_ref[...])
-    k_ref[...] = mm(latent_ref[...], wk_ref[0])
-    v_ref[...] = mm(latent_ref[...], wv_ref[0])
-
-    def chunk(index, carry):
-        spread(stages, band * (CHUNKS + 1) + index, ticks)
+    q_ref[...] = mm(normed_ref[...], wp_ref[:, :LANES])
+    decay_ref[...] = mm(normed_ref[...], wp_ref[:, LANES : 2 * LANES]) + bias_ref[...]
+    gate_ref[...] = mm(normed_ref[...], wp_ref[:, 2 * LANES :])
+    k_ref[...] = mm(latent_ref[...], wkv_ref[0, :, :LANES])
+    v_ref[...] = mm(latent_ref[...], wkv_ref[0, :, LANES:])
+    normed_t_ref[...] = jnp.transpose(normed_ref[:, pl.ds(pl.multiple_of(band * LANES, LANES), LANES)])
+    latent_t_ref[...] = jnp.transpose(latent_ref[...])
+
+    def chunk(index):
         rows = pl.ds(pl.multiple_of(index * SPAN, SPAN), SPAN)
         fresh, to_end, pad, allowed, keep = flags(seg_ref, pad_ref, index)
         up, down, half, _ = decays(decay_ref[rows, :], pad, lower_ones)
@@ -154,10 +156,13 @@
         gate = gate_ref[rows, :]
         silu = gate / (1.0 + jnp.exp(-gate))
         mixed_ref[rows, :] = (heads * scale * gain * silu).astype(BF)
+
+    def tick(index, carry):
+        spread(stages, band * (CHUNKS + 1) + index, ticks)
+        pl.when(index < CHUNKS)(lambda: chunk(index))
         return carry
 
-    lax.fori_loop(0, CHUNKS, chunk, 0)
-    spread(stages, band * (CHUNKS + 1) + CHUNKS, ticks)
+    lax.fori_loop(0, CHUNKS + 1, tick, 0)
     if comm:
         pl.when(band == BANDS - 1)(job.finish)
 
@@ -165,17 +170,27 @@
 def mixer_bwd_kernel(comm, *refs):
     kinds = comm[2] if comm else 0
     q_ref, k_ref, v_ref, decay_ref, gate_ref, gain_ref, seg_ref, pad_ref, heads_ref, states_ref = refs[:10]
-    dbranch_ref, wo_ref = refs[10:12]
-    grads, refs = refs[12 : 12 + kinds], refs[12 + kinds :]
-    dq_ref, dk_ref, dv_ref, ddecay_ref, dgate_ref, dbias_ref, dgain_ref = refs[:7]
-    sums, state, dmix_ref, scratch = refs[7 : 7 + kinds], refs[7 + kinds], refs[8 + kinds], refs[9 + kinds :]
+    dbranch_ref, wo_ref, mixed_ref, normed_t_ref, latent_t_ref = refs[10:15]
+    wp_ref, wl_ref, wkv_ref = refs[15:18]
+    grads, refs = refs[18 : 18 + kinds], refs[18 + kinds :]
+    gproj_ref, glat_ref, gkv_ref, gout_ref, dnormed_ref, dbias_ref, dgain_ref = refs[:7]
+    sums, refs = refs[7 : 7 + kinds], refs[7 + kinds :]
+    state, dmix_ref, dlatent, dproj, dkv = refs[:5]
+    scratch = refs[5:]
+    dq_ref, ddecay_ref, dgate_ref = (dproj.at[:, part * LANES : (part + 1) * LANES] for part in range(3))
+    dk_ref, dv_ref = (dkv.at[:, part * LANES : (part + 1) * LANES] for part in range(2))
     band = pl.program_id(0)
     job = scatter_of(comm[0], comm[1], grads, sums, scratch) if comm else None
     stages = job.stages() if comm else []
-    ticks = BANDS * (CHUNKS + 1)
+    ticks = BANDS * TICKS
     if comm:
         pl.when(band == 0)(job.begin)
     dmix_ref[...] = mm_nt(dbranch_ref[...], wo_ref[...])
+
+    @pl.when(band == 0)
+    def _():
+        dnormed_ref[...] = jnp.zeros_like(dnormed_ref)
+
     masks = head_masks()
     diag = same_head()
     diag_ones = diag.astype(F32).astype(BF)
@@ -186,8 +201,7 @@
     dgain_ref[...] = jnp.zeros_like(dgain_ref)
     gain = gain_ref[...]
 
-    def chunk(step, carry):
-        spread(stages, band * (CHUNKS + 1) + step, ticks)
+    def chunk(step):
         index = CHUNKS - 1 - step
         rows = pl.ds(pl.multiple_of(index * SPAN, SPAN), SPAN)
         fresh, to_end, pad, allowed, keep = flags(seg_ref, pad_ref, index)
@@ -248,10 +262,49 @@
         ddecay = dlog * (pad * (1.0 / 16.0)) * other
         dbias_ref[...] += jnp.sum(ddecay, axis=0, keepdims=True)
         ddecay_ref[rows, :] = ddecay.astype(BF)
+
+    first, last = band % (BANDS // GROUPS) == 0, band % (BANDS // GROUPS) == BANDS // GROUPS - 1
+
+    def proj_piece(part):
+        cols = slice(part * 3 * LANES // 2, (part + 1) * 3 * LANES // 2)
+        gproj_ref[:, cols] = mm(normed_t_ref[...], dproj[:, cols]).astype(BF)
+
+    def out_piece():
+        gout_ref[...] = mm_tn(mixed_ref[...], dbranch_ref[...]).astype(BF)
+
+    def kv_piece():
+        gkv_ref[...] = mm(latent_t_ref[...], dkv[...]).astype(BF)
+        added = mm_nt(dkv[...], wkv_ref[0])
+
+        @pl.when(first)
+        def _():
+            dlatent[...] = added
+
+        @pl.when(jnp.logical_not(first))
+        def _():
+            dlatent[...] += added
+
+    def normed_piece(part):
+        rows = slice(part * LEN // 2, (part + 1) * LEN // 2)
+        dnormed_ref[rows, :] += mm_nt(dproj[rows, :], wp_ref[...])
+
+    def latent_piece():
+        low = dlatent[...].astype(BF)
+        glat_ref[...] = mm(normed_t_ref[...], low).astype(BF)
+        dnormed_ref[...] += mm_nt(low, wl_ref[...])
+
+    pieces = [partial(proj_piece, 0), partial(proj_piece, 1), out_piece, kv_piece]
+    pieces += [partial(normed_piece, 0), partial(normed_piece, 1)]
+
+    def tick(index, carry):
+        spread(stages, band * TICKS + index, ticks, 7)
+        pl.when(index < CHUNKS)(lambda: chunk(index))
+        for number, piece in enumerate(pieces):
+            pl.when(index == CHUNKS + number)(piece)
+        pl.when((index == CHUNKS + len(pieces)) & last)(latent_piece)
         return carry
 
-    lax.fori_loop(0, CHUNKS, chunk, 0)
-    spread(stages, band * (CHUNKS + 1) + CHUNKS, ticks)
+    lax.fori_loop(0, TICKS, tick, 0)
     if comm:
         pl.when(band == BANDS - 1)(job.finish)
 
@@ -273,21 +326,18 @@
     kinds = len(shards)
     half_bands = BANDS // GROUPS
     in_specs = [fixed((LEN, D)), pl.BlockSpec((LEN, LATENT), lambda band: (0, band // half_bands))]
-    for part in range(3):
-        in_specs.append(pl.BlockSpec((D, LANES), lambda band, part=part: (0, part * BANDS + band)))
-    for part in range(2):
-        in_specs.append(
-            pl.BlockSpec(
-                (1, LATENT, LANES),
-                lambda band, part=part: (band // half_bands, 0, part * half_bands + band % half_bands),
-            )
-        )
+    in_specs.append(pl.BlockSpec((D, 3 * LANES), lambda band: (0, band)))
+    in_specs.append(
+        pl.BlockSpec((1, LATENT, 2 * LANES), lambda band: (band // half_bands, 0, band % half_bands))
+    )
     in_specs += [vector, vector, segs_spec, segs_spec]
     wide = jax.ShapeDtypeStruct((LEN, WIDTH), F32)
     out_shape = [wide] * 5 + [
         jax.ShapeDtypeStruct((LEN, WIDTH), BF),
         wide,
         jax.ShapeDtypeStruct((BANDS, CHUNKS, LANES, LANES), BF),
+        jax.ShapeDtypeStruct((D, LEN), BF),
+        jax.ShapeDtypeStruct((GROUPS * LATENT, LEN), BF),
     ]
     scratch = [pltpu.VMEM((LANES, LANES), F32)]
     params = {}
@@ -302,23 +352,54 @@
         partial(mixer_fwd_kernel, comm),
         grid=(BANDS,),
         in_specs=in_specs,
-        out_specs=[tokens] * 7 + [states] + [pl.BlockSpec(memory_space=pl.ANY)] * kinds,
+        out_specs=[tokens] * 7
+        + [states, pl.BlockSpec((LANES, LEN), lambda band: (band, 0))]
+        + [pl.BlockSpec((LATENT, LEN), lambda band: (band // half_bands, 0))]
+        + [pl.BlockSpec(memory_space=pl.ANY)] * kinds,
         out_shape=out_shape,
         scratch_shapes=scratch,
         compiler_params=pltpu.CompilerParams(vmem_limit_bytes=52 << 20, **params),
         name="mixer_fwd",
-    )(normed, latent, w_in, w_in, w_in, w_kv, w_kv, bias, gain, segs, pads, *shards)
-
-
-def mixer_bwd(saved, d_branch, w_output, grads, comm):
-    tokens, vector, segs_spec, states = band_specs()
-    kinds = len(grads)
-    low = jax.ShapeDtypeStruct((LEN, WIDTH), BF)
+    )(normed, latent, w_in, w_kv, bias, gain, segs, pads, *shards)
+
+
+def mixer_bwd(saved, d_branch, w_output, mixed, normed_t, latent_t, w_in, w_kv, grads, comm):
+    _, vector, segs_spec, states = band_specs()
+    kinds, half_bands = len(grads), BANDS // GROUPS
+    once = pl.Buffered(1)
+    tokens = pl.BlockSpec((LEN, LANES), lambda band: (0, band))
+    rows = pl.BlockSpec((LANES, D), lambda band: (band, 0))
     sums = jax.ShapeDtypeStruct((1, WIDTH), F32)
     in_specs = [tokens] * 5 + [vector, segs_spec, segs_spec, tokens, states]
-    in_specs += [fixed((LEN, D)), pl.BlockSpec((LANES, D), lambda band: (band, 0))]
-    out_specs, out_shape = [tokens] * 5 + [vector, vector], [low] * 5 + [sums, sums]
-    scratch = [pltpu.VMEM((LANES, LANES), F32), pltpu.VMEM((LEN, LANES), F32)]
+    in_specs += [fixed((LEN, D)), rows, tokens, fixed((D, LEN))]
+    in_specs.append(pl.BlockSpec((LATENT, LEN), lambda band: (band // half_bands, 0), pipeline_mode=once))
+    in_specs.append(pl.BlockSpec((D, 3 * LANES), lambda band: (0, band)))
+    in_specs.append(
+        pl.BlockSpec((D, LATENT), lambda band: (0, 3 * BANDS + band // half_bands), pipeline_mode=once)
+    )
+    in_specs.append(
+        pl.BlockSpec((1, LATENT, 2 * LANES), lambda band: (band // half_bands, 0, band % half_bands))
+    )
+    out_specs = [
+        pl.BlockSpec((D, 3 * LANES), lambda band: (0, band)),
+        pl.BlockSpec((D, LATENT), lambda band: (0, band // half_bands)),
+        pl.BlockSpec((LATENT, 2 * LANES), lambda band: (band // half_bands, band % half_bands)),
+        rows,
+        fixed((LEN, D)),
+        vector,
+        vector,
+    ]
+    out_shape = [
+        jax.ShapeDtypeStruct((D, 3 * WIDTH), BF),
+        jax.ShapeDtypeStruct((D, GROUPS * LATENT), BF),
+        jax.ShapeDtypeStruct((GROUPS * LATENT, 2 * WIDTH // GROUPS), BF),
+        jax.ShapeDtypeStruct((WIDTH, D), BF),
+        jax.ShapeDtypeStruct((LEN, D), F32),
+        sums,
+        sums,
+    ]
+    scratch = [pltpu.VMEM((LANES, LANES), F32), pltpu.VMEM((LEN, LANES), F32), pltpu.VMEM((LEN, LATENT), F32)]
+    scratch += [pltpu.VMEM((LEN, 3 * LANES), BF), pltpu.VMEM((LEN, 2 * LANES), BF)]
     params = {}
     if comm:
         in_specs += [pl.BlockSpec(memory_space=pl.ANY)] * kinds
@@ -336,7 +417,7 @@
         scratch_shapes=scratch,
         compiler_params=pltpu.CompilerParams(vmem_limit_bytes=63 << 20, **params),
         name="mixer_bwd",
-    )(*saved, d_branch, w_output, *grads)
+    )(*saved, d_branch, w_output, mixed, normed_t, latent_t, w_in, w_in, w_kv, *grads)
 
 
 class Place:
@@ -389,6 +470,9 @@
     return pltpu.make_async_remote_copy(
         src_ref=src, dst_ref=dst, send_sem=send_sem, recv_sem=recv_sem, device_id=device, device_id_type=MESH
     )
+
+
+AHEAD = 4
 
 
 class Scatter:
@@ -414,9 +498,11 @@
         me = self.me
         return self.grads[a].at[me.slot(me.ring(-step * self.way(a, i)), self.order[i], core)]
 
-    def load(self, a, step, i):
+    def load(self, a, number):
+        step, i = self.waves[number]
+        slot = number % AHEAD
         return pltpu.make_async_copy(
-            self.dest(a, step, i, self.me.core), self.accs[a].at[step - 1, i], self.load_sem.at[a, step - 1, i]
+            self.dest(a, step, i, self.me.core), self.accs[a].at[slot], self.load_sem.at[a, slot]
         )
 
     def to_pair(self, a, step, i):
@@ -432,7 +518,7 @@
     def to_ring(self, a, step, i):
         me = self.me
         return send(
-            self.accs[a].at[step - 1, i],
+            self.parts[a].at[step - 1, i],
             self.hops[a].at[step - 1, i],
             self.hsend.at[a, step - 1, i],
             self.hrecv.at[a, step - 1, i],
@@ -442,7 +528,7 @@
     def to_line(self, a, i):
         me = self.me
         return send(
-            self.accs[a].at[self.ring_size - 1, i],
+            self.parts[a].at[self.ring_size - 1, i],
             self.tails[a].at[me.z],
             self.tsend.at[a, i],
             self.trecv.at[a, me.z],
@@ -461,46 +547,51 @@
         block = 512 if width % 512 == 0 else width
         return width // block, block
 
-    def add_up(self, a, step, i):
-        number, block = self.blocks(a)
-        acc, final = self.accs[a], step == self.ring_size and i == self.line_size - 1
+    def add_up(self, a, number):
+        step, i = self.waves[number]
+        count, block = self.blocks(a)
+        here, own = self.parts[a], self.accs[a]
+        final = step == self.ring_size and i == self.line_size - 1
 
         def body(j, carry):
             cols = pl.ds(pl.multiple_of(j * block, block), block)
-            total = acc[step - 1, i, :, cols].astype(F32) + self.parts[a][step - 1, i, :, cols].astype(F32)
+            total = own[number % AHEAD, :, cols].astype(F32) + here[step - 1, i, :, cols].astype(F32)
             if step > 1:
                 total += self.hops[a][step - 2, i, :, cols].astype(F32)
             if final:
                 self.outs[a][:, cols] = total
             else:
-                acc[step - 1, i, :, cols] = total.astype(acc.dtype)
+                here[step - 1, i, :, cols] = total.astype(here.dtype)
             return carry
 
-        lax.fori_loop(0, number, body, 0)
+        lax.fori_loop(0, count, body, 0)
 
     def begin(self):
-        for step, i in self.waves:
+        for number in range(min(AHEAD, len(self.waves))):
             for a in self.every:
-                self.load(a, step, i).start()
+                self.load(a, number).start()
         greet(self.me, peers_of(self.me))
         for step, i in self.waves:
             for a in self.every:
                 self.to_pair(a, step, i).start()
 
-    def entry(self, step, i):
+    def entry(self, number):
+        step, i = self.waves[number]
         for a in self.every:
-            self.load(a, step, i).wait()
+            self.load(a, number).wait()
             self.to_pair(a, step, i).wait_recv()
             if step > 1:
                 self.to_ring(a, step - 1, i).wait_recv()
-            self.add_up(a, step, i)
+            self.add_up(a, number)
             if step < self.ring_size:
                 self.to_ring(a, step, i).start()
             elif i < self.line_size - 1:
                 self.to_line(a, i).start()
+            if number + AHEAD < len(self.waves):
+                self.load(a, number + AHEAD).start()
 
     def stages(self):
-        return [partial(self.entry, step, i) for step, i in self.waves]
+        return [partial(self.entry, number) for number in range(len(self.waves))]
 
     def finish(self):
         last = self.line_size - 1
@@ -531,9 +622,14 @@
     kinds = len(grads)
     sems = pltpu.SemaphoreType.DMA
     scratch = []
-    for lead in ((ring_size, line_size), (ring_size, line_size), (ring_size - 1, line_size), (line_size,)):
+    for lead in ((AHEAD,), (ring_size, line_size), (ring_size - 1, line_size), (line_size,)):
         scratch += [pltpu.VMEM(lead + grad.shape[1:], grad.dtype) for grad in grads]
-    return scratch + [sems((kinds, ring_size, line_size))] * 5 + [sems((kinds, line_size))] * 2
+    return (
+        scratch
+        + [sems((kinds, AHEAD))]
+        + [sems((kinds, ring_size, line_size))] * 4
+        + [sems((kinds, line_size))] * 2
+    )
 
 
 def scatter_of(ring_size, line_size, grads, outs, scratch):
@@ -760,9 +856,9 @@
     )(*shards)
 
 
-def spread(stages, tick, ticks):
+def spread(stages, tick, ticks, reach=8):
     for number, stage in enumerate(stages):
-        pl.when(tick == number * ticks // len(stages))(stage)
+        pl.when(tick == number * (ticks * reach // 8) // len(stages))(stage)
 
 
 BLOCK = 256
@@ -901,11 +997,11 @@
 
 def pack_kernel(places, *refs):
     flats, packed = refs[: len(places) + 1], refs[len(places) + 1 :]
-    for flat, (target, offset, tiles) in zip(flats, places):
+    for flat, (target, offsets) in zip(flats, places):
         out = packed[target]
         rows = out.shape[0]
-        for j in range(tiles):
-            out[:, offset + j * 128 : offset + (j + 1) * 128] = flat[pl.ds(j, rows, stride=tiles), :].astype(BF)
+        for j, offset in enumerate(offsets):
+            out[:, offset : offset + 128] = flat[pl.ds(j, rows, stride=len(offsets)), :].astype(BF)
     packed[-1][...] = jnp.broadcast_to(flats[-1][...].astype(BF).astype(F32), packed[-1].shape)
 
 
@@ -921,20 +1017,20 @@
 
 
 def unpack_kernel(places, kinds, *refs):
-    packed, flats = refs[: kinds + 1], refs[kinds + 1 :]
-    for flat, (target, offset, tiles) in zip(flats, places):
+    packed, flats = refs[:kinds], refs[kinds:]
+    for flat, (target, offsets) in zip(flats, places):
         source = packed[target]
         rows = source.shape[0]
-        for j in range(tiles):
-            flat[pl.ds(j, rows, stride=tiles), :] = source[:, offset + j * 128 : offset + (j + 1) * 128]
+        for j, offset in enumerate(offsets):
+            flat[pl.ds(j, rows, stride=len(offsets)), :] = source[:, offset : offset + 128]
     flats[-1][...] = packed[-1][0:1]
 
 
 def unpack(packed, places):
     vmem = pl.BlockSpec(memory_space=pltpu.VMEM)
-    sizes = [packed[target].shape[0] * tiles for target, _, tiles in places] + [1]
+    sizes = [packed[target].shape[0] * len(offsets) for target, offsets in places] + [1]
     flats = pl.pallas_call(
-        partial(unpack_kernel, places, len(packed) - 1),
+        partial(unpack_kernel, places, len(packed)),
         in_specs=[vmem] * len(packed),
         out_specs=[vmem] * len(sizes),
         out_shape=[jax.ShapeDtypeStruct((size, 128), F32) for size in sizes],
@@ -995,20 +1091,40 @@
 
     own = by_kernel(rows_all, ring_size, fsdp_size) and vec_size == 128
     flat_weights = (w_query, w_latent, w_key_up, w_value_up, w_decay, w_outgate, w_out, w_gate, w_up, w_down)
-    wide, half_kv, ff = WIDTH // 128, per_group // 128, FF // 128
+    def proj(part):
+        return [tile // 2 * 3 * LANES + part * LANES + tile % 2 * 128 for tile in range(WIDTH // 128)]
+
+    def kv(part):
+        return [tile // 2 * 2 * LANES + part * LANES + tile % 2 * 128 for tile in range(per_group // 128)]
+
+    def straight(width, start=0):
+        return list(range(start, start + width, 128))
+
     places = (
-        (0, 0, wide),
-        (0, 3 * WIDTH, latents // 128),
-        (1, 0, half_kv),
-        (1, per_group, half_kv),
-        (0, WIDTH, wide),
-        (0, 2 * WIDTH, wide),
-        (2, 0, D // 128),
-        (3, 0, ff),
-        (3, FF, ff),
-        (4, 0, D // 128),
-    )
-    sums_at = places[:7] + ((3, 0, ff), (4, 0, ff), (5, 0, D // 128))
+        (0, proj(0)),
+        (0, straight(latents, 3 * WIDTH)),
+        (1, kv(0)),
+        (1, kv(1)),
+        (0, proj(1)),
+        (0, proj(2)),
+        (2, straight(D)),
+        (3, straight(FF)),
+        (3, straight(FF, FF)),
+        (4, straight(D)),
+    )
+
+    sums_at = (
+        (0, proj(0)),
+        (1, straight(latents)),
+        (2, kv(0)),
+        (2, kv(1)),
+        (0, proj(1)),
+        (0, proj(2)),
+        (3, straight(D)),
+        (4, straight(FF)),
+        (5, straight(FF)),
+        (6, straight(D)),
+    )
     if own:
         shapes = (
             (rows_d, 3 * WIDTH + latents),
@@ -1023,10 +1139,14 @@
         def rows_of(piece, rows):
             return piece.astype(BF).reshape(rows, -1)
 
+        def by_band(pieces, rows):
+            bands = [rows_of(piece, rows).reshape(rows, -1, 1, LANES) for piece in pieces]
+            return jnp.concatenate(bands, axis=2).reshape(rows, -1)
+
         in_shard = jnp.concatenate(
-            [rows_of(piece, rows_d) for piece in (w_query, w_decay, w_outgate, w_latent)], axis=1
+            [by_band((w_query, w_decay, w_outgate), rows_d), rows_of(w_latent, rows_d)], axis=1
         )
-        kv_shard = jnp.concatenate([rows_of(w_key_up, rows_kv), rows_of(w_value_up, rows_kv)], axis=1)
+        kv_shard = by_band((w_key_up, w_value_up), rows_kv)
         out_shard = rows_of(w_out, rows_d)
         ff_shard = jnp.concatenate([rows_of(w_gate, rows_d), rows_of(w_up, rows_d)], axis=1)
         down_shard = rows_of(w_down, rows_ff)
@@ -1048,7 +1168,7 @@
     normed = (inputs * factor_in * gain_in).astype(BF)
     latent = mm(normed, w_in[:, 3 * WIDTH :]).astype(BF)
     bias_row, gain_row = decay_bias.reshape(1, WIDTH), out_gain.reshape(1, WIDTH)
-    query, keys, values, decay_in, gate_in, mixed, heads, states, *rest = mixer_fwd(
+    query, keys, values, decay_in, gate_in, mixed, heads, states, normed_t, latent_t, *rest = mixer_fwd(
         normed, latent, w_in, w_kv, bias_row, gain_row, segs, pads, late if own else (), comm + (0, 2) if own else None
     )
     w_output, w_ff, w_dn = rest if own else gather_plain(late)
@@ -1058,7 +1178,6 @@
     block_out, d_middle, d_branch, grad_gate, grad_up, grad_down, d_gain_mid = feed_forward(
         hidden_in, mixed, w_output, cotangent, pads, gain_mid.reshape(1, D), w_ff, w_dn
     )
-    grad_out = mm_tn(mixed, d_branch)
 
     sent = (
         grad_gate.reshape(count, rows_d, -1),
@@ -1066,51 +1185,40 @@
         grad_down.reshape(count, rows_ff, -1),
     )
     saved = (query, keys, values, decay_in, gate_in, gain_row, segs, pads, heads, states)
-    d_query, d_keys, d_values, d_decay, d_gatein, d_bias, d_out_gain, *rest = mixer_bwd(
-        saved, d_branch, w_output, sent if own else (), comm + (0, 3) if own else None
+    grad_proj, grad_lat, grad_kv, grad_out, d_normed, d_bias, d_out_gain, *rest = mixer_bwd(
+        saved,
+        d_branch,
+        w_output,
+        mixed,
+        normed_t,
+        latent_t,
+        w_in,
+        w_kv,
+        sent if own else (),
+        comm + (0, 3) if own else None,
     )
     own_gate, own_up, own_down = rest if own else scatter_plain(sent)
-    grad_kv, d_latent = [], []
-    for g in range(GROUPS):
-        d_kv = jnp.concatenate(
-            [part[:, g * per_group : (g + 1) * per_group] for part in (d_keys, d_values)], axis=1
-        )
-        grad_kv.append(mm_tn(latent[:, g * LATENT : (g + 1) * LATENT], d_kv))
-        d_latent.append(mm_nt(d_kv, w_kv[g]))
-    grad_kv = jnp.concatenate(grad_kv, axis=0)
-    d_latent = jnp.concatenate(d_latent, axis=1).astype(BF)
-    d_in = jnp.concatenate([d_query, d_decay, d_gatein, d_latent], axis=1)
-    grad_in = mm_tn(normed, d_in)
-    d_normed = mm_nt(d_in, w_in)
     d_inputs, d_gain_in = rms_back(d_normed, inputs, factor_in, gain_in)
     grad_input = d_middle + d_inputs
     grad_vec = jnp.concatenate([d_gain_in, d_gain_mid.reshape(-1), d_bias.reshape(-1), d_out_gain.reshape(-1)])
 
     grad_vec = jnp.broadcast_to(grad_vec.reshape(count, 1, vec_size), (count, 8, vec_size))
     sent = (
-        grad_in.astype(BF).reshape(count, rows_d, -1),
-        grad_kv.astype(BF).reshape(count, rows_kv, -1),
-        grad_out.astype(BF).reshape(count, rows_d, -1),
+        grad_proj.reshape(count, rows_d, -1),
+        grad_lat.reshape(count, rows_d, -1),
+        grad_kv.reshape(count, rows_kv, -1),
+        grad_out.reshape(count, rows_d, -1),
         grad_vec,
     )
-    own_in, own_kv, own_out, own_vec = scatter(sent, *comm, 1) if own else scatter_plain(sent)
+    own_proj, own_lat, own_kv, own_out, own_vec = scatter(sent, *comm, 1) if own else scatter_plain(sent)
+    sums = (own_proj, own_lat, own_kv, own_out, own_gate, own_up, own_down, own_vec)
     if own:
-        return (block_out, grad_input, *unpack((own_in, own_kv, own_out, own_gate, own_up, own_down, own_vec), sums_at))
-    return (
-        block_out,
-        grad_input,
-        own_in[:, :WIDTH].reshape(-1),
-        own_in[:, 3 * WIDTH :].reshape(-1),
-        own_kv[:, :per_group].reshape(-1),
-        own_kv[:, per_group:].reshape(-1),
-        own_in[:, WIDTH : 2 * WIDTH].reshape(-1),
-        own_in[:, 2 * WIDTH : 3 * WIDTH].reshape(-1),
-        own_out.reshape(-1),
-        own_gate.reshape(-1),
-        own_up.reshape(-1),
-        own_down.reshape(-1),
-        own_vec[0],
-    )
+        return (block_out, grad_input, *unpack(sums, sums_at))
+    flats = []
+    for target, offsets in sums_at:
+        tiles = [sums[target][:, offset : offset + 128] for offset in offsets]
+        flats.append(jnp.concatenate(tiles, axis=1).reshape(-1))
+    return (block_out, grad_input, *flats, own_vec[0])
 
 
 def solution(mesh):

time: 440 us -> 408 us (0.927); the launches traced: 432 us -> 407 us
  matrix products: 30.3 us -> 4.21 us
  local copies, waits for them, and re-layouts: 11 us -> 3.54 us
  Pallas kernels: 381 us -> 386 us
    dot_general x7 -> x0, matrix products: 27 us -> none  [the longest x4 17.5 us: mm_tn(): lax.dot_general(left, right, (((0,), (0,)), ((), ())), preferred_element_...]
    pallas_call x1, Pallas kernels: 94.5 us -> 104 us  [mixer_bwd(): pl.pallas_call(partial(mixer_bwd_kernel, comm), grid=(BANDS,), in_specs=i...]
    pallas_call x1, Pallas kernels: 68 us -> 63.3 us  [scatter(): pl.pallas_call(partial(scatter_kernel, ring_size, line_size, kinds), in_s...]
    slice x2 -> x0, local copies, waits for them, and re-layouts: 4.64 us -> none  [the longest x1 2.53 us: per_device(): part[:, g * per_group:(g + 1) * per_group]]
where the time goes in v6:
time: 408 us; the launch traced here: 407 us
  Pallas kernels  386 us (95%)
  other arithmetic  12.5 us (3%)
  matrix products  4.21 us (1%)
    pallas_call x1, Pallas kernels, mixer_bwd(): pl.pallas_call(partial(mixer_bwd_kernel, comm), grid=(BANDS,), in_specs=i...  104 us
    pallas_call x1, Pallas kernels, mixer_fwd(): pl.pallas_call(partial(mixer_fwd_kernel, comm), grid=(BANDS,), in_specs=i...  93 us
    pallas_call x1, Pallas kernels, feed_forward(): pl.pallas_call(ffn_kernel, grid=(blocks,), in_specs=[square, square, fixe...  74.2 us
    pallas_call x1, Pallas kernels, scatter(): pl.pallas_call(partial(scatter_kernel, ring_size, line_size, kinds), in_s...  63.3 us
    pallas_call x1, Pallas kernels, gather(): pl.pallas_call(partial(gather_kernel, ring_size, line_size, kinds), in_sp...  46.7 us

profile of v6, /device:TPU:0, one launch (start us, length us, event | category | flops | bytes accessed | tf_op | source)
XLA Modules:
  0.0 407.3 jit_solution(11374355452135268698)
XLA Ops:
  0.6 0.0 copy-start.7
  0.7 0.8 convert_element_type.18
  1.5 0.0 copy-start.5
  1.5 0.7 convert_element_type.19
  2.2 0.0 copy-start.4
  2.2 2.1 fusion.10
  4.3 2.6 pack_shards.1
  6.9 46.7 %gather_shards.1 = (bf16[32,32,3584]{2,1,0:T(8,128)(2,1)}, bf16[32,16,1024]{2,1,0:T(8,128)(2,1)}, f32[32,8,128]{2,1,0:T(8,128)}) custom-call(bf16[32,3584]{1,0:T(8,128)(2,1)} %get-tuple-element.68.refs_0_, bf16[16,1024]{1,0:T(8,128)(2,1)} %get-tuple-element.69.refs_1_, f32[8,128]{1,0:T(8,128)} %get-tuple-element.70.refs_2_), custom_call_target="tpu_custom_call" | custom-call | tf_op jit(solution)/shard_map/gather_shards/pallas_call | solution.py:848
  53.6 1.4 slice_bitcast_fusion
  55.0 0.0 copy-start.6
  55.0 0.0 copy-done.7
  55.0 0.5 fusion.4.refs_0_
  55.5 0.0 copy-start.10
  55.6 0.0 copy-start.1
  55.6 0.0 copy-start.2
  55.6 0.0 copy-start.3
  55.6 4.2 %convolution_convert_fusion.refs_1_ = bf16[1024,512]{1,0:T(8,128)(2,1)} fusion(bf16[1024,1024]{1,0:T(8,128)(2,1)S(1)} %fusion.4.refs_0_, bf16[1024,3584]{1,0:T(8,128)(2,1)} %bitcast.55), kind=kOutput, calls=%fused_computation.13 | convolution fusion | flops 1074266112 | bytes 4194304 | tf_op jit(solution)/shard_map/dot_general | solution.py:32
  59.8 0.0 copy-done.5
  59.8 0.0 copy-done.4
  59.8 0.0 copy-done.6
  59.8 0.0 copy-done.10
  59.8 0.0 copy-done.1
  59.8 0.0 copy-done.2
  59.8 0.0 copy-done.3
  59.9 93.0 %mixer_fwd.1 = (f32[1024,1024]{1,0:T(8,128)}, f32[1024,1024]{1,0:T(8,128)}, f32[1024,1024]{1,0:T(8,128)}, f32[1024,1024]{1,0:T(8,128)}, f32[1024,1024]{1,0:T(8,1...) custom-call(bf16[1024,1024]{1,0:T(8,128)(2,1)} %copy-done.10, ...), custom_call_target="tpu_custom_call" | custom-call | tf_op jit(solution)/shard_map/mixer_fwd/pallas_call | solution.py:351
  152.9 0.0 copy-start
  152.9 1.0 copy-done
  153.9 74.2 %feed_forward.1 = (bf16[1024,1024]{1,0:T(8,128)(2,1)}, f32[1024,1024]{1,0:T(8,128)}, bf16[1024,1024]{1,0:T(8,128)(2,1)}, bf16[1024,2816]{1,0:T(8,128)(2,1)}, bf1...) custom-call(bf16[1024,1024]{1,0:T(8,128)(2,1)} %x_ref.1, ...), custom_call_target="tpu_custom_call" | custom-call | tf_op jit(solution)/shard_map/feed_forward/pallas_call | solution.py:960
  228.1 103.6 %mixer_bwd.1 = (bf16[1024,3072]{1,0:T(8,128)(2,1)}, bf16[1024,512]{1,0:T(8,128)(2,1)}, bf16[512,1024]{1,0:T(8,128)(2,1)}, bf16[1024,1024]{1,0:T(8,128)(2,1)}, f3...) custom-call(f32[1024,1024]{1,0:T(8,128)} %get-tuple-element.83.refs_, ...), custom_call_target="tpu_custom_call" | custom-call | tf_op jit(solution)/shard_map/mixer_bwd/pallas_call | solution.py:411
  331.7 0.0 copy-start.11
  331.7 0.0 copy-start.12
  331.7 0.0 copy-start.13
  331.7 0.0 copy-start.8
  331.7 0.0 copy-start.9
  331.7 4.2 %fusion.9 = (f32[1024]{0:T(1024)S(1)}, f32[1024]{0:T(1024)S(1)}) fusion(f32[1024,1024]{1,0:T(8,128)} %get-tuple-element.96, bf16[1024,1024]{1,0:T(8,128)(2,1)} %x_ref.1, f32[1024]{0:T(1024)S(1)} %add_rsqrt_fusion, f32[1024]{0:T(1024)S(1)} %bitcast.82), kind=kLoop, calls=%fused_computation.11 | loop fusion | flops 7337984 | bytes 6307840 | tf_op jit(solution)/shard_map/reduce_sum | solution.py:1050
  335.9 0.0 copy-done.11
  335.9 0.0 copy-done.12
  335.9 0.0 copy-done.13
  336.0 0.0 copy-done.8
  336.0 0.4 copy-done.9
  336.4 4.2 %fusion.8 = f32[1024,1024]{1,0:T(8,128)} fusion(f32[1024,1024]{1,0:T(8,128)} %get-tuple-element.82, bf16[1024,1024]{1,0:T(8,128)(2,1)S(1)} %copy-done.8, f32[1024,1024]{1,0:T(8,128)S(1)} %copy-done.9, f32[1024]{0:T(1024)S(1)} %broadcast_multiply_fusion, f32[1024]{0:T(1024)S(1)} %bitcast.83, f32[1024]{0:T(1024)S(1)} %add_rsqrt_fusion), kind=kLoop, calls=%fused_computation.10 | loop fusion | flops 7340032 | bytes 14692352 | tf_op jit(solution)/shard_map/add | solution.py:1202
  340.6 0.7 broadcast_in_dim.5.refs_4_
  341.3 63.3 %scatter_sums.1 = (f32[32,3072]{1,0:T(8,128)}, f32[32,512]{1,0:T(8,128)}, f32[16,1024]{1,0:T(8,128)}, f32[32,1024]{1,0:T(8,128)}, f32[8,128]{1,0:T(8,128)}) custom-call(bf16[32,32,3072]{2,1,0:T(8,128)(2,1)} %bitcast.63, bf16[32,32,512]{2,1,0:T(8,128)(2,1)} %bitcast.71, bf16[32,16,1024]{2,1,0:T(8,128)(2,1)} %bitcast.72, bf16[32,32,1024]{2,1,0:T(8,128)(2,1)} %bitcast.70, ...), custom_call_target="tpu_custom_call" | custom-call | tf_op jit(solution)/shard_map/scatter_sums/pallas_call | solution.py:651
  404.6 2.7 unpack_sums.1
  (3 shorter events, 0.0 us)
Async XLA Ops:
  0.6 54.3 %copy-start.7 = (bf16[1024,1024]{1,0:T(8,128)(2,1)S(1)}, bf16[1024,1024]{1,0:T(8,128)(2,1)}, u32[]{:S(2)}) copy-start(bf16[1024,1024]{1,0:T(8,128)(2,1)} %x_ref.1) | copy-start | bytes 6291460
  1.5 58.3 %copy-start.5 = (f32[1024]{0:T(1024)}, f32[1024]{0:T(1024)S(1)}, u32[]{:S(2)}) copy-start(f32[1024]{0:T(1024)S(1)} %convert_element_type.18) | copy-start | bytes 12292
  2.2 57.6 %copy-start.4 = (f32[1024]{0:T(1024)}, f32[1024]{0:T(1024)S(1)}, u32[]{:S(2)}) copy-start(f32[1024]{0:T(1024)S(1)} %convert_element_type.19) | copy-start | bytes 12292
  55.0 4.8 %copy-start.6 = (f32[1,1024]{1,0:T(1,128)}, f32[1,1024]{1,0:T(1,128)S(1)}, u32[]{:S(2)}) copy-start(f32[1,1024]{1,0:T(1,128)S(1)} %get-tuple-element.126.refs_5_) | copy-start | bytes 12292
  55.5 4.3 %copy-start.10 = (bf16[1024,1024]{1,0:T(8,128)(2,1)}, bf16[1024,1024]{1,0:T(8,128)(2,1)S(1)}, u32[]{:S(2)}) copy-start(bf16[1024,1024]{1,0:T(8,128)(2,1)S(1)} %fusion.4.refs_0_) | copy-start | bytes 6291460
  55.6 4.3 %copy-start.1 = (bf16[32,5632]{1,0:T(8,128)(2,1)S(1)}, bf16[32,5632]{1,0:T(8,128)(2,1)}, u32[]{:S(2)}) copy-start(bf16[32,5632]{1,0:T(8,128)(2,1)} %get-tuple-element.75.refs_9_) | copy-start | bytes 1081348
  55.6 4.3 %copy-start.2 = (bf16[88,1024]{1,0:T(8,128)(2,1)S(1)}, bf16[88,1024]{1,0:T(8,128)(2,1)}, u32[]{:S(2)}) copy-start(bf16[88,1024]{1,0:T(8,128)(2,1)} %get-tuple-element.76.refs_10_) | copy-start | bytes 540676
  55.6 4.3 %copy-start.3 = (bf16[32,1024]{1,0:T(8,128)(2,1)S(1)}, bf16[32,1024]{1,0:T(8,128)(2,1)}, u32[]{:S(2)}) copy-start(bf16[32,1024]{1,0:T(8,128)(2,1)} %get-tuple-element.74.refs_8_) | copy-start | bytes 196612
  152.9 1.0 copy-start
  331.7 4.2 %copy-start.11 = (f32[1,1024]{1,0:T(1,128)S(1)}, f32[1,1024]{1,0:T(1,128)}, u32[]{:S(2)}) copy-start(f32[1,1024]{1,0:T(1,128)} %get-tuple-element.101) | copy-start | bytes 12292
  331.7 4.2 %copy-start.12 = (f32[1,1024]{1,0:T(1,128)S(1)}, f32[1,1024]{1,0:T(1,128)}, u32[]{:S(2)}) copy-start(f32[1,1024]{1,0:T(1,128)} %get-tuple-element.102) | copy-start | bytes 12292
  331.7 4.2 %copy-start.13 = (f32[1,1024]{1,0:T(1,128)S(1)}, f32[1,1024]{1,0:T(1,128)}, u32[]{:S(2)}) copy-start(f32[1,1024]{1,0:T(1,128)} %get-tuple-element.103) | copy-start | bytes 12292
  331.7 4.2 %copy-start.8 = (bf16[1024,1024]{1,0:T(8,128)(2,1)S(1)}, bf16[1024,1024]{1,0:T(8,128)(2,1)}, u32[]{:S(2)}) copy-start(bf16[1024,1024]{1,0:T(8,128)(2,1)} %x_ref.1) | copy-start | bytes 6291460
  331.7 4.7 %copy-start.9 = (f32[1024,1024]{1,0:T(8,128)S(1)}, f32[1024,1024]{1,0:T(8,128)}, u32[]{:S(2)}) copy-start(f32[1024,1024]{1,0:T(8,128)} %get-tuple-element.96) | copy-start | bytes 12582916
